TPU v7x, 32 devices: a whole 2x2x4 slice. The times are simulated.
32 devices in a mesh: blk: 8 (over z, x), span: 4 (over y, core).
Axes of the slice: x: 2, y: 2, z: 4, core: 2. Of those that a mesh axis runs over, the one named last changes fastest.
Arguments:
- fields: float32 [5, 125, 16384], P(None, None, ('blk', 'span')), may hold values from -6 to 6
- section_store: float32 [5, 125, 16384], P(None, None, ('blk', 'span')), may hold values from -6 to 6
- mean_velocity: float32 [3, 125, 16384], P(None, None, ('blk', 'span')), may hold values from -0.6 to 0.6
- sound_speed: float32 [125, 16384], P(None, ('blk', 'span')), may hold values from 0.7 to 1.5
- element_slot: int32 [16384], P(('blk', 'span')), may hold values from 0 to 511, as said below
- face_turn: int32 [8, 16], P('blk', 'span'), may hold values from 0 to 7
- rotor_offset: int32 [16], P('span'), may hold values from 0 to 7
Outputs:
- fields_next: float32 [5, 125, 16384], P(None, None, ('blk', 'span'))
- store_next: float32 [5, 125, 16384], P(None, None, ('blk', 'span'))
Inputs may be any that keep to these rules, and one draw needn't show every extreme that they name: `element_slot`: in each aligned block of 512 entries (the elements of one device) every number 0 to 511 appears once.
All inputs are finite; a program needn't handle non-finite values.
Results may differ from a plain program's by a relative error of at most 0.0003.
Values sent between devices are 32-bit elements; how exact they have to be, the bound alone decides.
No kernel may reach another device: no remote copies, remote signals or barrier semaphores. Data moves between devices by JAX's collectives and lax.ppermute only.
A program may use at most 128 MiB of HBM per device.

v0:
```python
import functools

import jax
import jax.numpy as jnp
import numpy as np
from jax import lax
from jax.experimental import pallas as pl
from jax.experimental.pallas import tpu as pltpu
from jax.sharding import PartitionSpec as P

ORDER = 4
NODE = ORDER + 1
FACE = NODE * NODE
VOL = NODE**3
LANES = 128
PAD = 32
VALS = 7

section_decay = -567301805773.0 / 1357537059087.0
section_gain = 5161836677717.0 / 13612068292357.0
time_step = 0.05
metric_scale = (1.0, 1.5, 0.75)
end_weight = 0.1

BF = jnp.bfloat16
F32 = jnp.float32
VMEM_LIMIT = 24 * 1024 * 1024


def lobatto_slopes():
    inner_root = np.sqrt(3.0 / 7.0)
    points = np.array([-1.0, -inner_root, 0.0, inner_root, 1.0])
    count = points.shape[0]
    slopes = np.zeros((count, count))
    for r in range(count):
        for c in range(count):
            if r == c:
                slopes[r, c] = sum(1.0 / (points[r] - points[o]) for o in range(count) if o != r)
            else:
                top = np.prod([points[r] - points[o] for o in range(count) if o != r])
                low = np.prod([points[c] - points[o] for o in range(count) if o != c])
                slopes[r, c] = top / (low * (points[r] - points[c]))
    return slopes


def split_np(table):
    high = np.asarray(table, np.float32).astype(BF)
    low = (np.asarray(table, np.float64) - high.astype(np.float64)).astype(BF)
    return high, low


def volume_matrix():
    slopes = lobatto_slopes()
    eye = np.eye(NODE)
    parts = (
        np.kron(np.kron(slopes, eye), eye),
        np.kron(np.kron(eye, slopes), eye),
        np.kron(np.kron(eye, eye), slopes),
    )
    full = np.zeros((LANES, 3 * LANES))
    for d in range(3):
        full[:VOL, d * LANES : d * LANES + VOL] = -time_step * metric_scale[d] * parts[d]
    high, low = split_np(full)
    return np.concatenate([high, low], 0)


def turn_matrix(inverse):
    table = np.zeros((PAD, 8 * PAD), np.float32)
    for code in range(8):
        index = np.arange(FACE).reshape(NODE, NODE)
        if inverse:
            if code & 2:
                index = index[:, ::-1]
            if code & 1:
                index = index[::-1, :]
            if code & 4:
                index = index.T
        else:
            if code & 4:
                index = index.T
            if code & 1:
                index = index[::-1, :]
            if code & 2:
                index = index[:, ::-1]
        for n, o in enumerate(index.reshape(-1)):
            table[n, code * PAD + o] = 1.0
    return table.astype(BF)


def dot(a, b):
    return jnp.dot(a, b, preferred_element_type=F32)


def dot_t(a, b):
    return lax.dot_general(a, b, (((1,), (1,)), ((), ())), preferred_element_type=F32)


def halves(x):
    high = x.astype(BF)
    return high, (x - high.astype(F32)).astype(BF)


def lane_iota(shape):
    return lax.broadcasted_iota(jnp.int32, shape, len(shape) - 1)


def row_iota(shape):
    return lax.broadcasted_iota(jnp.int32, shape, 0)


def face_rows(ref, v, tile, d, end):
    if d == 0:
        return ref[v, tile, pl.ds(end * FACE, FACE), :]
    if d == 1:
        starts = [i * FACE + end * NODE for i in range(NODE)]
        return jnp.concatenate([ref[v, tile, pl.ds(s, NODE), :] for s in starts], axis=0)
    return ref[v, tile, pl.ds(end, FACE, NODE), :]


def add_face_rows(ref, v, tile, d, end, value):
    if d == 0:
        ref[v, tile, pl.ds(end * FACE, FACE), :] += value
    elif d == 1:
        for i in range(NODE):
            ref[v, tile, pl.ds(i * FACE + end * NODE, NODE), :] += value[i * NODE : (i + 1) * NODE]
    else:
        ref[v, tile, pl.ds(end, FACE, NODE), :] += value


def value_index(f, d):
    return f if f < 5 else (5 + d if f == 5 else 8)


def stage_values(fields, velocity, sound, staged, tiles):
    for t in range(tiles):
        cols = slice(t * LANES, (t + 1) * LANES)
        for f in range(5):
            staged[f, t, 0:VOL, :] = fields[f, :, cols]
        for d in range(3):
            staged[5 + d, t, 0:VOL, :] = velocity[d, :, cols]
        staged[8, t, 0:VOL, :] = sound[:, cols]


def surface(own, other, d, side):
    qo, mo, co = own[:5], own[5], own[6]
    qn, mn, cn = other[:5], other[5], other[6]
    reach = jnp.maximum(jnp.abs(mo) + co, jnp.abs(mn) + cn)
    weight = side * 0.5 * time_step * metric_scale[d] / end_weight
    if side > 0:
        ao, an = mo - reach, mn - reach
    else:
        ao, an = mo + reach, mn + reach
    velocity_part = co * qo[1 + d] - cn * qn[1 + d]
    pressure_part = co * qo[4] - cn * qn[4]
    out = []
    for f in range(5):
        x = ao * qo[f] - an * qn[f]
        if f in (0, 4):
            x = x + velocity_part
        elif f == 1 + d:
            x = x + pressure_part
        out.append(weight * x)
    return out


def axis_parity(axis):
    return lax.rem(lax.axis_index(axis), 2)


def pack_kernel(
    per_span, axial, slot_s, turn_s, slot_v, fields, velocity, sound, turn_t,
    th_a, th_b, sp_a, sp_b, iface, staged, rows_hi, rows_lo, stack_hi, stack_lo,
):
    elems = slot_v.shape[1]
    tiles = elems // LANES
    half = axial // 2
    stage_values(fields, velocity, sound, staged, tiles)

    def theta_rows(out, end):
        for f in range(VALS):
            v = value_index(f, 0)
            for t in range(tiles):
                out[f * FACE : (f + 1) * FACE, t * LANES : (t + 1) * LANES] = face_rows(staged, v, t, 0, end * ORDER)
        out[VALS * FACE : VALS * FACE + 1, :] = slot_v[...].astype(F32)

    odd = axis_parity("blk")

    @pl.when(odd == 0)
    def _():
        theta_rows(th_a, 1)
        theta_rows(th_b, 0)

    @pl.when(odd == 1)
    def _():
        theta_rows(th_a, 0)
        theta_rows(th_b, 1)

    def gather_faces(d, end, target):
        for f in range(VALS):
            v = value_index(f, d)
            for t in range(tiles):
                x = face_rows(staged, v, t, d, end * ORDER)
                hi, lo = halves(jnp.concatenate([x, jnp.zeros((PAD - FACE, LANES), F32)], 0))
                rows_hi[f * PAD : (f + 1) * PAD, t * LANES : (t + 1) * LANES] = hi
                rows_lo[f * PAD : (f + 1) * PAD, t * LANES : (t + 1) * LANES] = lo
        one = (row_iota((elems, LANES)) == target).astype(BF)
        return dot(rows_hi[...], one) + dot(rows_lo[...], one)

    low = gather_faces(1, 0, slot_v[:, 0:axial])
    high = gather_faces(1, 1, slot_v[:, elems - axial : elems])
    span_odd = axis_parity("span")

    @pl.when(span_odd == 0)
    def _():
        sp_a[...] = high
        sp_b[...] = low

    @pl.when(span_odd == 1)
    def _():
        sp_a[...] = low
        sp_b[...] = high

    lane = lane_iota((1, LANES))
    column = lane % (2 * per_span)
    target = jnp.full((1, LANES), -1, jnp.int32)
    code = jnp.zeros((1, LANES), jnp.int32)
    for s in range(per_span):
        target = jnp.where(lane == s, slot_s[s * axial + half - 1], target)
        target = jnp.where(lane == per_span + s, slot_s[s * axial + half], target)
        code = jnp.where(column == per_span + s, turn_s[0, s], code)
    stator = gather_faces(2, 1, jnp.where(lane < per_span, target, -1))
    rotor = gather_faces(2, 0, jnp.where(lane < per_span, -1, target))
    both = stator + rotor
    packed = both[0:PAD]
    for f in range(1, VALS):
        packed = packed + pltpu.roll(both[f * PAD : (f + 1) * PAD], f * 2 * per_span, 1)
    iface[...] = turned(packed, code, turn_t, stack_hi, stack_lo)


def turned(packed, code, turn_t, stack_hi, stack_lo):
    hi, lo = packed.astype(BF).astype(F32), None
    lo = packed - hi
    for c in range(8):
        stack_hi[c * PAD : (c + 1) * PAD, :] = jnp.where(code == c, hi, 0.0).astype(BF)
        stack_lo[c * PAD : (c + 1) * PAD, :] = jnp.where(code == c, lo, 0.0).astype(BF)
    return dot(turn_t[...], stack_hi[...]) + dot(turn_t[...], stack_lo[...])


def volume_kernel(fields, velocity, sound, store, matrix, out, flux_hi, flux_lo):
    width = sound.shape[1]
    step = 16
    for r in range(0, VOL, step):
        n = min(step, VOL - r)
        rows = slice(r, r + n)
        q = [fields[f, rows, :] for f in range(5)]
        c = sound[rows, :]
        cp = c * q[4]
        for d in range(3):
            m = velocity[d, rows, :]
            cu = c * q[1 + d]
            for f in range(5):
                x = m * q[f]
                if f in (0, 4):
                    x = x + cu
                elif f == 1 + d:
                    x = x + cp
                if n < step:
                    x = jnp.concatenate([x, jnp.zeros((step - n, width), F32)], 0)
                hi, lo = halves(x)
                flux_hi[f, d * LANES + r : d * LANES + r + step, :] = hi
                flux_lo[f, d * LANES + r : d * LANES + r + step, :] = lo
    for f in range(5):
        a = dot(matrix[...], flux_hi[f])
        b = dot(matrix[0:LANES, :], flux_lo[f])
        total = a[0:LANES] + a[LANES : 2 * LANES] + b
        out[f] = section_decay * store[f] + total[0:VOL]


def neighbour_index(rows, slot_v):
    elems = slot_v.shape[1]
    own = (row_iota((elems, elems)) == slot_v[...]).astype(BF)
    base = 256.0
    table = jnp.concatenate(rows + [jnp.zeros((8 - len(rows), elems), F32)], 0)
    upper = jnp.floor(table * (1.0 / base))
    lower = table - upper * base
    both = jnp.concatenate([upper, lower], 0).astype(BF)
    moved = dot_t(both, own)
    return (moved[0:8] * base + moved[8:16]).astype(jnp.int32)


def pick_matrix(index_row, count):
    return (row_iota((count, index_row.shape[1])) == index_row).astype(BF)


def theta_ghost(recv, slot_v):
    elems = slot_v.shape[1]
    index = neighbour_index([recv[VALS * FACE : VALS * FACE + 1, :]], slot_v)
    one = pick_matrix(index[0:1], elems)
    hi, lo = halves(recv[...])
    return dot(hi, one) + dot(lo, one)


def face_kernel(
    per_span, axial, sectors, slabs, pieces,
    offset_s, turn_s, slot_v, fields, velocity, sound, part, th_a, sp_a, sp_b, turn_t, *rest,
):
    iface = rest[:pieces]
    fields_out, store_out = rest[pieces : pieces + 2]
    staged, acc, rows_hi, rows_lo, stack_hi, stack_lo, ghost = rest[pieces + 2 :]
    elems = slot_v.shape[1]
    tiles = elems // LANES
    half = axial // 2
    stage_values(fields, velocity, sound, staged, tiles)
    for t in range(tiles):
        for f in range(5):
            acc[f, t, 0:VOL, :] = part[f, :, t * LANES : (t + 1) * LANES]

    slots = slot_v[...].astype(F32)
    lane = lane_iota((1, elems))
    position = lane % axial
    row = lane // axial
    lanes_f = lane.astype(F32)
    span_low = jnp.where(lane < axial, elems + lanes_f, pltpu.roll(slots, axial, 1))
    span_high = jnp.where(lane >= elems - axial, axial + lanes_f, pltpu.roll(slots, elems - axial, 1))
    ax_low = jnp.where(position == half, elems + row.astype(F32), pltpu.roll(slots, 1, 1))
    ax_low = jnp.where(position == 0, elems + LANES - 1.0, ax_low)
    ax_high = jnp.where(position == half - 1, elems + per_span + row.astype(F32), pltpu.roll(slots, elems - 1, 1))
    ax_high = jnp.where(position == axial - 1, elems + LANES - 1.0, ax_high)
    index = neighbour_index([span_low, span_high, ax_low, ax_high], slot_v)

    def fill_rows(d, end):
        for f in range(VALS):
            v = value_index(f, d)
            for t in range(tiles):
                x = face_rows(staged, v, t, d, end * ORDER)
                hi, lo = halves(jnp.concatenate([x, jnp.zeros((PAD - FACE, LANES), F32)], 0))
                rows_hi[f * PAD : (f + 1) * PAD, t * LANES : (t + 1) * LANES] = hi
                rows_lo[f * PAD : (f + 1) * PAD, t * LANES : (t + 1) * LANES] = lo

    def one_side(d, side, index_row, extra, wall):
        end = ORDER if side > 0 else 0
        fill_rows(d, 0 if side > 0 else 1)
        hi, lo = halves(extra)
        rows_hi[:, elems : elems + LANES] = hi
        rows_lo[:, elems : elems + LANES] = lo
        one = pick_matrix(index_row, elems + LANES)
        ghost[...] = dot(rows_hi[...], one) + dot(rows_lo[...], one)
        for t in range(tiles):
            cols = slice(t * LANES, (t + 1) * LANES)
            own = [face_rows(staged, value_index(f, d), t, d, end) for f in range(VALS)]
            other = [ghost[f * PAD : f * PAD + FACE, cols] for f in range(VALS)]
            if wall is not None:
                at_wall = jnp.logical_and(index_row[:, cols] >= elems, wall)
                for f in range(VALS):
                    other[f] = jnp.where(at_wall, -own[f] if f == 1 + d else own[f], other[f])
            for f, x in enumerate(surface(own, other, d, side)):
                add_face_rows(acc, f, t, d, end, x)

    slab = lax.axis_index("span")
    slab_odd = lax.rem(slab, 2) == 1
    one_side(1, -1, index[0:1], jnp.where(slab_odd, sp_a[...], sp_b[...]), slab == 0)
    one_side(1, 1, index[1:2], jnp.where(slab_odd, sp_b[...], sp_a[...]), slab == slabs - 1)

    sector = lax.axis_index("blk")
    small = lane_iota((1, LANES))
    column = small % (2 * per_span)
    want = jnp.zeros((1, LANES), jnp.int32)
    code = jnp.zeros((1, LANES), jnp.int32)
    for s in range(per_span):
        shift = lax.rem(offset_s[s], sectors)
        want = jnp.where(column == s, lax.rem(sector - shift + sectors, sectors), want)
        want = jnp.where(column == per_span + s, lax.rem(sector + shift, sectors), want)
        code = jnp.where(column == s, turn_s[0, s], code)
    near = jnp.zeros((PAD, LANES), F32)
    k = 0
    for piece in iface:
        for b in range(piece.shape[0] // PAD):
            near = jnp.where(want == (sector ^ k), piece[b * PAD : (b + 1) * PAD, :], near)
            k += 1
    near = turned(near, code, turn_t, stack_hi, stack_lo)
    used = small < 2 * per_span
    extra = jnp.concatenate(
        [
            jnp.where(used, near if f == 0 else pltpu.roll(near, LANES - f * 2 * per_span, 1), 0.0)
            for f in range(VALS)
        ],
        0,
    )
    one_side(2, -1, index[2:3], extra, None)
    one_side(2, 1, index[3:4], extra, None)

    ghost[0 : VALS * FACE + 1, :] = theta_ghost(th_a, slot_v)

    def theta_side(side):
        for t in range(tiles):
            cols = slice(t * LANES, (t + 1) * LANES)
            end = ORDER if side > 0 else 0
            own = [face_rows(staged, value_index(f, 0), t, 0, end) for f in range(VALS)]
            other = [ghost[f * FACE : (f + 1) * FACE, cols] for f in range(VALS)]
            for f, x in enumerate(surface(own, other, 0, side)):
                add_face_rows(acc, f, t, 0, end, x)

    odd = lax.rem(sector, 2)

    @pl.when(odd == 0)
    def _():
        theta_side(1)

    @pl.when(odd == 1)
    def _():
        theta_side(-1)

    for t in range(tiles):
        cols = slice(t * LANES, (t + 1) * LANES)
        for f in range(5):
            total = acc[f, t, 0:VOL, :]
            store_out[f, :, cols] = total
            fields_out[f, :, cols] = fields[f, :, cols] + section_gain * total


def last_kernel(odd_s, slot_v, fields, velocity, sound, store_in, fields_alias, th_b, fields_out, store_out, ghost):
    del fields_alias
    elems = slot_v.shape[1]
    tiles = elems // LANES
    ghost[...] = theta_ghost(th_b, slot_v)
    store_out[...] = store_in[...]

    def theta_side(side):
        start = (ORDER * FACE) % PAD if side > 0 else 0
        rows = slice(start, start + FACE)
        for t in range(tiles):
            cols = slice(t * LANES, (t + 1) * LANES)
            own = [fields[f, rows, cols] for f in range(5)] + [velocity[0, rows, cols], sound[rows, cols]]
            other = [ghost[f * FACE : (f + 1) * FACE, cols] for f in range(VALS)]
            for f, x in enumerate(surface(own, other, 0, side)):
                store_out[f, rows, cols] += x

    @pl.when(odd_s[0] == 0)
    def _():
        theta_side(-1)

    @pl.when(odd_s[0] == 1)
    def _():
        theta_side(1)

    for f in range(5):
        fields_out[f] = fields[f] + section_gain * store_out[f]


def params(**extra):
    return pltpu.CompilerParams(vmem_limit_bytes=VMEM_LIMIT, **extra)


def vmem_spec():
    return pl.BlockSpec(memory_space=pltpu.VMEM)


def smem_spec():
    return pl.BlockSpec(memory_space=pltpu.SMEM)


def on_device(fields, section_store, mean_velocity, sound_speed, element_slot, face_turn, rotor_offset):
    per_theta, per_span = face_turn.shape
    elems = element_slot.shape[0]
    axial = elems // (per_theta * per_span)
    sectors, slabs = lax.axis_size("blk"), lax.axis_size("span")
    tiles = elems // LANES
    assert per_theta == 1 and axial == LANES and sectors % 2 == 0 and sectors & (sectors - 1) == 0
    assert 2 * per_span * VALS < LANES
    slot_row = element_slot.reshape(1, elems)
    sds = jax.ShapeDtypeStruct
    theta_shape = sds((VALS * FACE + 1, elems), F32)
    span_shape = sds((VALS * PAD, LANES), F32)
    th_a, th_b, sp_a, sp_b, iface = pl.pallas_call(
        functools.partial(pack_kernel, per_span, axial),
        out_shape=(theta_shape, theta_shape, span_shape, span_shape, sds((PAD, LANES), F32)),
        in_specs=[smem_spec(), smem_spec()] + [vmem_spec()] * 5,
        out_specs=(vmem_spec(),) * 5,
        scratch_shapes=[
            pltpu.VMEM((9, tiles, LANES, LANES), F32),
            pltpu.VMEM((VALS * PAD, elems), BF),
            pltpu.VMEM((VALS * PAD, elems), BF),
            pltpu.VMEM((8 * PAD, LANES), BF),
            pltpu.VMEM((8 * PAD, LANES), BF),
        ],
        compiler_params=params(),
        name="pack",
    )(element_slot, face_turn, slot_row, fields, mean_velocity, sound_speed, jnp.asarray(turn_matrix(True)))

    pieces = [iface]
    near = lax.ppermute(iface, "blk", [(i, i ^ 1) for i in range(sectors)])
    near_a = lax.ppermute(th_a, "blk", [(i, i ^ 1) for i in range(sectors)])
    pairs = [(i, i + 1 if i % 2 else i - 1) for i in range(sectors)]
    near_b = lax.ppermute(th_b, "blk", [(i, j % sectors) for i, j in pairs])
    span_a = lax.ppermute(sp_a, "span", [(i, i ^ 1) for i in range(slabs) if i ^ 1 < slabs])
    pairs = [(i, i + 1 if i % 2 else i - 1) for i in range(slabs)]
    span_b = lax.ppermute(sp_b, "span", [(i, j) for i, j in pairs if 0 <= j < slabs])
    pieces.append(near)
    reach = 2
    while reach < sectors:
        block = jnp.concatenate(pieces, 0)
        pieces.append(lax.ppermute(block, "blk", [(i, i ^ reach) for i in range(sectors)]))
        reach *= 2

    width = 2 * LANES
    state = lambda: pl.BlockSpec((5, VOL, width), lambda i: (0, 0, i))
    part = pl.pallas_call(
        volume_kernel,
        grid=(elems // width,),
        out_shape=sds((5, VOL, elems), F32),
        in_specs=[
            state(),
            pl.BlockSpec((3, VOL, width), lambda i: (0, 0, i)),
            pl.BlockSpec((VOL, width), lambda i: (0, i)),
            state(),
            pl.BlockSpec((2 * LANES, 3 * LANES), lambda i: (0, 0)),
        ],
        out_specs=state(),
        scratch_shapes=[pltpu.VMEM((5, 3 * LANES, width), BF), pltpu.VMEM((5, 3 * LANES, width), BF)],
        compiler_params=params(),
        cost_estimate=pl.CostEstimate(flops=2 * 5 * 384 * 384 * elems, bytes_accessed=6 * 10**6, transcendentals=0),
        name="volume",
    )(fields, mean_velocity, sound_speed, section_store, jnp.asarray(volume_matrix()))

    whole = sds((5, VOL, elems), F32)
    fields_part, store_part = pl.pallas_call(
        functools.partial(face_kernel, per_span, axial, sectors, slabs, len(pieces)),
        out_shape=(whole, whole),
        in_specs=[smem_spec(), smem_spec()] + [vmem_spec()] * (9 + len(pieces)),
        out_specs=(vmem_spec(),) * 2,
        scratch_shapes=[
            pltpu.VMEM((9, tiles, LANES, LANES), F32),
            pltpu.VMEM((5, tiles, LANES, LANES), F32),
            pltpu.VMEM((VALS * PAD, elems + LANES), BF),
            pltpu.VMEM((VALS * PAD, elems + LANES), BF),
            pltpu.VMEM((8 * PAD, LANES), BF),
            pltpu.VMEM((8 * PAD, LANES), BF),
            pltpu.VMEM((VALS * PAD, elems), F32),
        ],
        compiler_params=params(),
        name="faces",
    )(
        rotor_offset, face_turn, slot_row, fields, mean_velocity, sound_speed, part, near_a, span_a, span_b,
        jnp.asarray(turn_matrix(False)), *pieces,
    )

    odd = lax.rem(lax.axis_index("blk"), 2).astype(jnp.int32).reshape(1)
    last = (VOL - 1) // PAD

    def window(lead):
        return pl.BlockSpec(lead + (PAD, elems), lambda i, o: (0,) * len(lead) + (o[0] * last, 0))

    return pl.pallas_call(
        last_kernel,
        out_shape=(whole, whole),
        grid_spec=pltpu.PrefetchScalarGridSpec(
            num_scalar_prefetch=1,
            grid=(1,),
            in_specs=[
                pl.BlockSpec((1, elems), lambda i, o: (0, 0)),
                window((5,)),
                window((1,)),
                window(()),
                window((5,)),
                pl.BlockSpec(memory_space=pl.ANY),
                pl.BlockSpec((VALS * FACE + 1, elems), lambda i, o: (0, 0)),
            ],
            out_specs=(window((5,)), window((5,))),
            scratch_shapes=[pltpu.VMEM((VALS * FACE + 1, elems), F32)],
        ),
        input_output_aliases={5: 1, 6: 0},
        compiler_params=params(),
        name="last",
    )(odd, slot_row, fields, mean_velocity, sound_speed, store_part, fields_part, near_b)


def solution(mesh):
    both = ("blk", "span")
    in_specs = (
        P(None, None, both),
        P(None, None, both),
        P(None, None, both),
        P(None, both),
        P(both),
        P("blk", "span"),
        P("span"),
    )
    out_specs = (P(None, None, both), P(None, None, both))
    return jax.shard_map(on_device, mesh=mesh, in_specs=in_specs, out_specs=out_specs, check_vma=False)
```

profile of v0, /device:TPU:0, one launch (start us, length us, event | category | flops | bytes accessed | tf_op | source)
XLA Modules:
  0.0 48.6 jit_solution(6778634375137976118)
XLA Ops:
  0.6 1.3 %copy-done = f32[5,125,512]{2,1,0:T(8,128)S(1)} copy-done((f32[5,125,512]{2,1,0:T(8,128)S(1)}, f32[5,125,512]{2,1,0:T(8,128)}, u32[]{:S(2)}) %copy-start) | copy-done | bytes 1280024
  1.9 1.1 %copy-done.2 = f32[3,125,512]{2,1,0:T(8,128)S(1)} copy-done((f32[3,125,512]{2,1,0:T(8,128)S(1)}, f32[3,125,512]{2,1,0:T(8,128)}, u32[]{:S(2)}) %copy-start.2) | copy-done | bytes 768024
  3.1 0.9 %copy-done.4 = f32[125,512]{1,0:T(8,128)S(1)} copy-done((f32[125,512]{1,0:T(8,128)S(1)}, f32[125,512]{1,0:T(8,128)}, u32[]{:S(2)}) %copy-start.4) | copy-done | bytes 256024
  4.0 0.7 %copy-done.8 = s32[512]{0:T(512)S(1)} copy-done((s32[512]{0:T(512)S(1)}, s32[512]{0:T(512)}, u32[]{:S(2)}) %copy-start.8) | copy-done | bytes 2072
  4.7 0.7 %copy-done.11 = bf16[32,256]{1,0:T(8,128)(2,1)S(1)} copy-done((bf16[32,256]{1,0:T(8,128)(2,1)S(1)}, bf16[32,256]{1,0:T(8,128)(2,1)}, u32[]{:S(2)}) %copy-start.11) | copy-done | bytes 16408
  5.4 0.7 %copy-done.12 = s32[1,4]{1,0:T(1,128)S(1)} copy-done((s32[1,4]{1,0:T(1,128)S(1)}, s32[1,4]{1,0:T(1,128)}, u32[]{:S(2)}) %copy-start.12) | copy-done | bytes 40
  6.1 2.8 %pack.1 = (f32[176,512]{1,0:T(8,128)}, f32[176,512]{1,0:T(8,128)}, f32[224,128]{1,0:T(8,128)}, f32[224,128]{1,0:T(8,128)}, f32[32,128]{1,0:T(8,128)S(1)}) custom-call(s32[512]{0:T(512)S(1)} %copy-done.8, s32[1,4]{1,0:T(1,128)S(1)} %copy-done.12, s32[1,512]{1,0:T(1,128)S(1)} %bitcast.2, f32[5,125,512]{2,1,0:T(8,128)S(1)} %copy-done, ...), custom_call_target="tpu_custom_call" | custom-call | tf_op jit(solution)/shard_map/pack/pallas_call | solution.py:474
  8.9 3.0 %collective-permute-start = (f32[176,512]{1,0:T(8,128)}, f32[176,512]{1,0:T(8,128)S(1)}, u32[]{:S(2)}, u32[]{:S(2)}) collective-permute-start(f32[176,512]{1,0:T(8,128)} %get-tuple-element.9), channel_id=1, source_target_pairs={{0,4},{4,0},{8,12},{12,8},{16,20},{20,16},{24,28},{28,24},{1,5},{5... | collective-permute-start | bytes 1081352 | tf_op jit(solution)/shard_map/ppermute | solution.py:492
  11.9 3.6 %collective-permute-start.6 = (f32[176,512]{1,0:T(8,128)}, f32[176,512]{1,0:T(8,128)S(1)}, u32[]{:S(2)}, u32[]{:S(2)}) collective-permute-start(f32[176,512]{1,0:T(8,128)} %get-tuple-element.15), channel_id=1, source_target_pairs={{0,28},{4,8},{8,4},{12,16},{16,12},{20,24},{24,20},{28,0},{1,29},{... | collective-permute-start | bytes 1081352 | tf_op jit(solution)/shard_map/ppermute | solution.py:494
  15.4 0.0 collective-permute-start.3
  15.4 13.1 %collective-permute-done.3.rest_1_ = f32[32,128]{1,0:T(8,128)S(1)} collective-permute-done((f32[32,128]{1,0:T(8,128)S(1)}, f32[32,128]{1,0:T(8,128)S(1)}, u32[]{:S(2)}, u32[]{:S(2)}) %collective-permute-start.3) | collective-permute-done | bytes 16416 | tf_op jit(solution)/shard_map/ppermute | solution.py:491
  28.6 1.8 %collective-permute-start.4 = (f32[64,128]{1,0:T(8,128)S(1)}, f32[64,128]{1,0:T(8,128)S(1)}, u32[]{:S(2)}, u32[]{:S(2)}) collective-permute-start(f32[64,128]{1,0:T(8,128)S(1)} %pad_maximum_fusion.1), channel_id=1, source_target_pairs={{0,8},{4,12},{8,0},{12,4},{16,24},{20,28},{24,16},{28,20},{1,9},{5... | collective-permute-start | bytes 98312 | tf_op jit(solution)/shard_map/ppermute | solution.py:502
  30.4 0.0 collective-permute-start.1
  30.4 1.3 %collective-permute-start.2 = (f32[224,128]{1,0:T(8,128)}, f32[224,128]{1,0:T(8,128)}, u32[]{:S(2)}, u32[]{:S(2)}) collective-permute-start(f32[224,128]{1,0:T(8,128)} %get-tuple-element.11), channel_id=1, source_target_pairs={{1,2},{2,1},{5,6},{6,5},{9,10},{10,9},{13,14},{14,13},{17,18},{18,... | collective-permute-start | bytes 344072 | tf_op jit(solution)/shard_map/ppermute | solution.py:497
  31.7 0.8 %collective-permute-done.4.rest_2_ = f32[64,128]{1,0:T(8,128)S(1)} collective-permute-done((f32[64,128]{1,0:T(8,128)S(1)}, f32[64,128]{1,0:T(8,128)S(1)}, u32[]{:S(2)}, u32[]{:S(2)}) %collective-permute-start.4) | collective-permute-done | bytes 32800 | tf_op jit(solution)/shard_map/ppermute | solution.py:502
  32.5 2.8 %collective-permute-start.5 = (f32[128,128]{1,0:T(8,128)S(1)}, f32[128,128]{1,0:T(8,128)S(1)}, u32[]{:S(2)}, u32[]{:S(2)}) collective-permute-start(f32[128,128]{1,0:T(8,128)S(1)} %pad_maximum_fusion), channel_id=1, source_target_pairs={{0,16},{4,20},{8,24},{12,28},{16,0},{20,4},{24,8},{28,12},{1,17},{... | collective-permute-start | bytes 196616 | tf_op jit(solution)/shard_map/ppermute | solution.py:502
  35.3 0.0 copy-done.3
  35.3 0.0 copy-done.7
  35.3 0.0 copy-start.6
  35.4 1.3 %copy-done.6 = f32[5,125,512]{2,1,0:T(8,128)S(1)} copy-done((f32[5,125,512]{2,1,0:T(8,128)S(1)}, f32[5,125,512]{2,1,0:T(8,128)}, u32[]{:S(2)}) %copy-start.6) | copy-done | bytes 1280024
  36.7 1.9 %volume.1.part = f32[5,125,512]{2,1,0:T(8,128)S(1)} custom-call(f32[5,125,512]{2,1,0:T(8,128)S(1)} %copy-done.1, f32[3,125,512]{2,1,0:T(8,128)S(1)} %copy-done.3, f32[125,512]{1,0:T(8,128)S(1)} %copy-done.5, f32[5,125,512]{2,1,0:T(8,128)S(1)} %copy-done.6, bf16[256,384]{1,0:T(8,128)(2,1)S(1)} %copy-done.7), custom_call_target="tpu_custom_call" | custom-call | flops 754974720 | bytes 6000000 | tf_op jit(solution)/shard_map/volume/pallas_call | solution.py:507
  38.5 0.7 %collective-permute-done.5.rest_3_ = f32[128,128]{1,0:T(8,128)S(1)} collective-permute-done((f32[128,128]{1,0:T(8,128)S(1)}, f32[128,128]{1,0:T(8,128)S(1)}, u32[]{:S(2)}, u32[]{:S(2)}) %collective-permute-start.5) | collective-permute-done | bytes 65568 | tf_op jit(solution)/shard_map/ppermute | solution.py:502
  39.2 0.0 collective-permute-done.1.sp_a
  39.2 0.0 collective-permute-done.2.sp_b
  39.2 0.0 collective-permute-done.th_a
  39.2 0.0 copy-done.9
  39.2 0.0 copy-done.10
  39.2 0.0 copy-done.13
  39.2 0.0 copy-done.14
  39.3 6.6 %faces.1 = (f32[5,125,512]{2,1,0:T(8,128)}, f32[5,125,512]{2,1,0:T(8,128)}) custom-call(s32[4]{0:T(128)S(1)} %copy-done.14, s32[1,4]{1,0:T(1,128)S(1)} %copy-done.13, s32[1,512]{1,0:T(1,128)S(1)} %bitcast.3, f32[5,125,512]{2,1,0:T(8,128)S(1)} %copy-done.1, f32[3,125,512]{2,1,0:T(8,128)S(1)} %copy-done.3, f32[125,512]{1,0:T(8,128)S(1)} %copy-done.5, ...), custom_call_target="tpu_custom_call" | custom-call | tf_op jit(solution)/shard_map/faces/pallas_call | solution.py:526
  45.9 0.0 collective-permute-done.6.th_b
  45.9 2.7 %last.1 = (f32[5,125,512]{2,1,0:T(8,128)}, f32[5,125,512]{2,1,0:T(8,128)}) custom-call(s32[1]{0:T(128)} %bitcast.odd_s, s32[1,512]{1,0:T(1,128)S(1)} %bitcast.4, f32[5,125,512]{2,1,0:T(8,128)S(1)} %copy-done.1, f32[3,125,512]{2,1,0:T(8,128)S(1)} %copy-done.3, f32[125,512]{1,0:T(8,128)S(1)} %copy-done.5, ...), custom_call_target="tpu_custom_call", output_to_operand_aliasing={{1}: (5, {}), {0}: (6, {})} | custom-call | tf_op jit(solution)/shard_map/last/pallas_call | solution.py:553
  (18 shorter events, 0.0 us)
Async XLA Ops:
  0.6 1.3 %copy-start = (f32[5,125,512]{2,1,0:T(8,128)S(1)}, f32[5,125,512]{2,1,0:T(8,128)}, u32[]{:S(2)}) copy-start(f32[5,125,512]{2,1,0:T(8,128)} %fields.7) | copy-start | bytes 3840004
  1.9 1.1 %copy-start.2 = (f32[3,125,512]{2,1,0:T(8,128)S(1)}, f32[3,125,512]{2,1,0:T(8,128)}, u32[]{:S(2)}) copy-start(f32[3,125,512]{2,1,0:T(8,128)} %velocity.7) | copy-start | bytes 2304004
  3.1 0.9 %copy-start.4 = (f32[125,512]{1,0:T(8,128)S(1)}, f32[125,512]{1,0:T(8,128)}, u32[]{:S(2)}) copy-start(f32[125,512]{1,0:T(8,128)} %sound.7) | copy-start | bytes 768004
  4.0 0.7 %copy-start.8 = (s32[512]{0:T(512)S(1)}, s32[512]{0:T(512)}, u32[]{:S(2)}) copy-start(s32[512]{0:T(512)} %slot_s.1) | copy-start | bytes 6148
  4.7 0.7 %copy-start.11 = (bf16[32,256]{1,0:T(8,128)(2,1)S(1)}, bf16[32,256]{1,0:T(8,128)(2,1)}, u32[]{:S(2)}) copy-start(bf16[32,256]{1,0:T(8,128)(2,1)} %constant.17.clone.turn_t) | copy-start | bytes 49156
  5.4 0.7 %copy-start.12 = (s32[1,4]{1,0:T(1,128)S(1)}, s32[1,4]{1,0:T(1,128)}, u32[]{:S(2)}) copy-start(s32[1,4]{1,0:T(1,128)} %turn_s.3) | copy-start | bytes 52
  6.1 29.2 %copy-start.1 = (f32[5,125,512]{2,1,0:T(8,128)S(1)}, f32[5,125,512]{2,1,0:T(8,128)}, u32[]{:S(2)}) copy-start(f32[5,125,512]{2,1,0:T(8,128)} %fields.7) | copy-start | bytes 3840004
  6.1 29.2 %copy-start.3 = (f32[3,125,512]{2,1,0:T(8,128)S(1)}, f32[3,125,512]{2,1,0:T(8,128)}, u32[]{:S(2)}) copy-start(f32[3,125,512]{2,1,0:T(8,128)} %velocity.7) | copy-start | bytes 2304004
  6.1 29.2 %copy-start.5 = (f32[125,512]{1,0:T(8,128)S(1)}, f32[125,512]{1,0:T(8,128)}, u32[]{:S(2)}) copy-start(f32[125,512]{1,0:T(8,128)} %sound.7) | copy-start | bytes 768004
  6.1 29.2 %copy-start.7 = (bf16[256,384]{1,0:T(8,128)(2,1)S(1)}, bf16[256,384]{1,0:T(8,128)(2,1)}, u32[]{:S(2)}) copy-start(bf16[256,384]{1,0:T(8,128)(2,1)} %constant.18.clone.matrix) | copy-start | bytes 589828
  8.9 30.3 %collective-permute-start = (f32[176,512]{1,0:T(8,128)}, f32[176,512]{1,0:T(8,128)S(1)}, u32[]{:S(2)}, u32[]{:S(2)}) collective-permute-start(f32[176,512]{1,0:T(8,128)} %get-tuple-element.9), channel_id=1, source_target_pairs={{0,4},{4,0},{8,12},{12,8},{16,20},{20,16},{24,28},{28,24},{1,5},{5... | collective-permute-start | bytes 1081352 | tf_op jit(solution)/shard_map/ppermute | solution.py:492
  11.9 34.0 %collective-permute-start.6 = (f32[176,512]{1,0:T(8,128)}, f32[176,512]{1,0:T(8,128)S(1)}, u32[]{:S(2)}, u32[]{:S(2)}) collective-permute-start(f32[176,512]{1,0:T(8,128)} %get-tuple-element.15), channel_id=1, source_target_pairs={{0,28},{4,8},{8,4},{12,16},{16,12},{20,24},{24,20},{28,0},{1,29},{... | collective-permute-start | bytes 1081352 | tf_op jit(solution)/shard_map/ppermute | solution.py:494
  15.4 13.1 %collective-permute-start.3 = (f32[32,128]{1,0:T(8,128)S(1)}, f32[32,128]{1,0:T(8,128)S(1)}, u32[]{:S(2)}, u32[]{:S(2)}) collective-permute-start(f32[32,128]{1,0:T(8,128)S(1)} %get-tuple-element.12.rest_0_), channel_id=1, source_target_pairs={{0,4},{4,0},{8,12},{12,8},{16,20},{20,16},{24,28},{28,24},{1,5},{5... | collective-permute-start | bytes 49160 | tf_op jit(solution)/shard_map/ppermute | solution.py:491
  28.6 3.9 %collective-permute-start.4 = (f32[64,128]{1,0:T(8,128)S(1)}, f32[64,128]{1,0:T(8,128)S(1)}, u32[]{:S(2)}, u32[]{:S(2)}) collective-permute-start(f32[64,128]{1,0:T(8,128)S(1)} %pad_maximum_fusion.1), channel_id=1, source_target_pairs={{0,8},{4,12},{8,0},{12,4},{16,24},{20,28},{24,16},{28,20},{1,9},{5... | collective-permute-start | bytes 98312 | tf_op jit(solution)/shard_map/ppermute | solution.py:502
  30.4 8.8 %collective-permute-start.1 = (f32[224,128]{1,0:T(8,128)}, f32[224,128]{1,0:T(8,128)S(1)}, u32[]{:S(2)}, u32[]{:S(2)}) collective-permute-start(f32[224,128]{1,0:T(8,128)} %get-tuple-element.10), channel_id=1, source_target_pairs={{0,1},{1,0},{2,3},{3,2},{4,5},{5,4},{6,7},{7,6},{8,9},{9,8},{10,11... | collective-permute-start | bytes 344072 | tf_op jit(solution)/shard_map/ppermute | solution.py:495
  30.4 8.8 %collective-permute-start.2 = (f32[224,128]{1,0:T(8,128)}, f32[224,128]{1,0:T(8,128)}, u32[]{:S(2)}, u32[]{:S(2)}) collective-permute-start(f32[224,128]{1,0:T(8,128)} %get-tuple-element.11), channel_id=1, source_target_pairs={{1,2},{2,1},{5,6},{6,5},{9,10},{10,9},{13,14},{14,13},{17,18},{18,... | collective-permute-start | bytes 344072 | tf_op jit(solution)/shard_map/ppermute | solution.py:497
  32.5 6.7 %collective-permute-start.5 = (f32[128,128]{1,0:T(8,128)S(1)}, f32[128,128]{1,0:T(8,128)S(1)}, u32[]{:S(2)}, u32[]{:S(2)}) collective-permute-start(f32[128,128]{1,0:T(8,128)S(1)} %pad_maximum_fusion), channel_id=1, source_target_pairs={{0,16},{4,20},{8,24},{12,28},{16,0},{20,4},{24,8},{28,12},{1,17},{... | collective-permute-start | bytes 196616 | tf_op jit(solution)/shard_map/ppermute | solution.py:502
  35.3 1.3 %copy-start.6 = (f32[5,125,512]{2,1,0:T(8,128)S(1)}, f32[5,125,512]{2,1,0:T(8,128)}, u32[]{:S(2)}) copy-start(f32[5,125,512]{2,1,0:T(8,128)} %store.1) | copy-start | bytes 3840004
  36.7 2.6 %copy-start.9 = (s32[512]{0:T(512)S(1)}, s32[512]{0:T(512)}, u32[]{:S(2)}) copy-start(s32[512]{0:T(512)} %slot_s.1) | copy-start | bytes 6148
  36.7 2.6 %copy-start.10 = (bf16[32,256]{1,0:T(8,128)(2,1)S(1)}, bf16[32,256]{1,0:T(8,128)(2,1)}, u32[]{:S(2)}) copy-start(bf16[32,256]{1,0:T(8,128)(2,1)} %constant.19.clone.turn_t) | copy-start | bytes 49156
  36.7 2.6 %copy-start.13 = (s32[1,4]{1,0:T(1,128)S(1)}, s32[1,4]{1,0:T(1,128)}, u32[]{:S(2)}) copy-start(s32[1,4]{1,0:T(1,128)} %turn_s.3) | copy-start | bytes 52
  36.7 2.6 %copy-start.14 = (s32[4]{0:T(128)S(1)}, s32[4]{0:T(128)}, u32[]{:S(2)}) copy-start(s32[4]{0:T(128)} %offset_s.1) | copy-start | bytes 52
where the time goes:
time: 49 us; the launch traced here: 48.6 us
  waiting for transfers between devices  14.6 us (30%)
  Pallas kernels  14 us (29%)
  starting transfers between devices  12.5 us (26%)
  local copies, waits for them, and re-layouts  6.79 us (14%)
  between operations  0.72 us (1%)
    ppermute x1, waiting for transfers between devices, on_device(): near = lax.ppermute(iface, 'blk', [(i, i ^ 1) for i in range(sectors)])  13.1 us
    unnamed x30, local copies, waits for them, and re-layouts  6.79 us
    pallas_call x1, Pallas kernels, on_device(): pl.pallas_call(functools.partial(face_kernel, per_span, axial, sectors, s...  6.61 us
    ppermute x2, starting transfers between devices, on_device(): lax.ppermute(block, 'blk', [(i, i ^ reach) for i in range(sectors)])  4.66 us
    ppermute x1, starting transfers between devices, on_device(): near_b = lax.ppermute(th_b, 'blk', [(i, j % sectors) for i, j in pairs])  3.57 us
    ppermute x1, starting transfers between devices, on_device(): near_a = lax.ppermute(th_a, 'blk', [(i, i ^ 1) for i in range(sectors)])  2.97 us
    pallas_call x1, Pallas kernels, on_device(): pl.pallas_call(functools.partial(pack_kernel, per_span, axial), out_shape...  2.79 us
    pallas_call x1, Pallas kernels, on_device(): pl.pallas_call(last_kernel, out_shape=(whole, whole), grid_spec=pltpu.Pre...  2.72 us
  transfers between devices with their start and end apart: 7, of which 3 were waited for; matrix products, arithmetic and copies ran while one was open for 0% of the time, Pallas kernels for 17%

commit v1 on v0

v1 whole, which is shorter than its diff:
```python
import functools

import jax
import jax.numpy as jnp
import numpy as np
from jax import lax
from jax.experimental import pallas as pl
from jax.experimental.pallas import tpu as pltpu
from jax.sharding import PartitionSpec as P


ORDER = 4
NODE = ORDER + 1
FACE = NODE * NODE
VOL = NODE**3
LANES = 128
PAD = 32
VALS = 7

section_decay = -567301805773.0 / 1357537059087.0
section_gain = 5161836677717.0 / 13612068292357.0
time_step = 0.05
metric_scale = (1.0, 1.5, 0.75)
end_weight = 0.1

BF = jnp.bfloat16
F32 = jnp.float32
VMEM_LIMIT = 24 * 1024 * 1024


def lobatto_slopes():
    inner_root = np.sqrt(3.0 / 7.0)
    points = np.array([-1.0, -inner_root, 0.0, inner_root, 1.0])
    count = points.shape[0]
    slopes = np.zeros((count, count))
    for r in range(count):
        for c in range(count):
            if r == c:
                slopes[r, c] = sum(1.0 / (points[r] - points[o]) for o in range(count) if o != r)
            else:
                top = np.prod([points[r] - points[o] for o in range(count) if o != r])
                low = np.prod([points[c] - points[o] for o in range(count) if o != c])
                slopes[r, c] = top / (low * (points[r] - points[c]))
    return slopes


def split_np(table):
    high = np.asarray(table, np.float32).astype(BF)
    low = (np.asarray(table, np.float64) - high.astype(np.float64)).astype(BF)
    return high, low


def volume_matrix():
    slopes = lobatto_slopes()
    eye = np.eye(NODE)
    parts = (
        np.kron(np.kron(slopes, eye), eye),
        np.kron(np.kron(eye, slopes), eye),
        np.kron(np.kron(eye, eye), slopes),
    )
    full = np.zeros((LANES, 3 * LANES))
    for d in range(3):
        full[:VOL, d * LANES : d * LANES + VOL] = -time_step * metric_scale[d] * parts[d]
    high, low = split_np(full)
    return np.concatenate([high, low], 0)


def turn_matrix(inverse):
    table = np.zeros((PAD, 8 * PAD), np.float32)
    for code in range(8):
        index = np.arange(FACE).reshape(NODE, NODE)
        if inverse:
            if code & 2:
                index = index[:, ::-1]
            if code & 1:
                index = index[::-1, :]
            if code & 4:
                index = index.T
        else:
            if code & 4:
                index = index.T
            if code & 1:
                index = index[::-1, :]
            if code & 2:
                index = index[:, ::-1]
        for n, o in enumerate(index.reshape(-1)):
            table[n, code * PAD + o] = 1.0
    return table.astype(BF)


def dot(a, b):
    return jnp.dot(a, b, preferred_element_type=F32)


def dot_t(a, b):
    return lax.dot_general(a, b, (((1,), (1,)), ((), ())), preferred_element_type=F32)


def halves(x):
    high = x.astype(BF)
    return high, (x - high.astype(F32)).astype(BF)


def lane_iota(shape):
    return lax.broadcasted_iota(jnp.int32, shape, len(shape) - 1)


def row_iota(shape):
    return lax.broadcasted_iota(jnp.int32, shape, 0)


def face_rows(ref, v, tile, d, end):
    if d == 0:
        return ref[v, tile, pl.ds(end * FACE, FACE), :]
    if d == 1:
        starts = [i * FACE + end * NODE for i in range(NODE)]
        return jnp.concatenate([ref[v, tile, pl.ds(s, NODE), :] for s in starts], axis=0)
    return ref[v, tile, pl.ds(end, FACE, NODE), :]


def add_face_rows(ref, v, tile, d, end, value):
    if d == 0:
        ref[v, tile, pl.ds(end * FACE, FACE), :] += value
    elif d == 1:
        for i in range(NODE):
            ref[v, tile, pl.ds(i * FACE + end * NODE, NODE), :] += value[i * NODE : (i + 1) * NODE]
    else:
        ref[v, tile, pl.ds(end, FACE, NODE), :] += value


def value_index(f, d):
    return f if f < 5 else (5 + d if f == 5 else 8)


def surface(own, other, d, side):
    qo, mo, co = own[:5], own[5], own[6]
    qn, mn, cn = other[:5], other[5], other[6]
    reach = jnp.maximum(jnp.abs(mo) + co, jnp.abs(mn) + cn)
    weight = side * 0.5 * time_step * metric_scale[d] / end_weight
    if side > 0:
        ao, an = mo - reach, mn - reach
    else:
        ao, an = mo + reach, mn + reach
    velocity_part = co * qo[1 + d] - cn * qn[1 + d]
    pressure_part = co * qo[4] - cn * qn[4]
    out = []
    for f in range(5):
        x = ao * qo[f] - an * qn[f]
        if f in (0, 4):
            x = x + velocity_part
        elif f == 1 + d:
            x = x + pressure_part
        out.append(weight * x)
    return out


def axis_parity(axis):
    return lax.rem(lax.axis_index(axis), 2)


def one_hot(index_row, count):
    return (row_iota((count, index_row.shape[1])) == index_row).astype(BF)


def store_halves(ref_hi, ref_lo, at, cols, value):
    hi, lo = halves(jnp.concatenate([value, jnp.zeros((PAD - FACE, value.shape[1]), F32)], 0))
    ref_hi[at : at + PAD, cols] = hi
    ref_lo[at : at + PAD, cols] = lo


def turned(packed, code, turn_t, stack_hi, stack_lo):
    hi = packed.astype(BF).astype(F32)
    lo = packed - hi
    for c in range(8):
        stack_hi[c * PAD : (c + 1) * PAD, :] = jnp.where(code == c, hi, 0.0).astype(BF)
        stack_lo[c * PAD : (c + 1) * PAD, :] = jnp.where(code == c, lo, 0.0).astype(BF)
    return dot(turn_t[...], stack_hi[...]) + dot(turn_t[...], stack_lo[...])


def tile_cols(t):
    return slice(t * LANES, (t + 1) * LANES)


def neighbour_index(rows, slot_v):
    elems = slot_v.shape[1]
    own = (row_iota((elems, elems)) == slot_v[...]).astype(BF)
    base = 256.0
    table = jnp.concatenate(rows + [jnp.zeros((8 - len(rows), elems), F32)], 0)
    upper = jnp.floor(table * (1.0 / base))
    lower = table - upper * base
    both = jnp.concatenate([upper, lower], 0).astype(BF)
    moved = dot_t(both, own)
    return (moved[0:8] * base + moved[8:16]).astype(jnp.int32)


def first_kernel(
    per_span, axial, slot_s, turn_s, slot_h, fields, velocity, sound, turn_h,
    staged, th_a, iface, slot_v, theta, turn_t, rows_hi, rows_lo, stack_hi, stack_lo, sems, small_sems, out_sem,
):
    elems = slot_v.shape[1]
    tiles = elems // LANES
    half = axial // 2
    rows = VALS * PAD
    small = [
        pltpu.make_async_copy(slot_h, slot_v, small_sems.at[0]),
        pltpu.make_async_copy(turn_h, turn_t, small_sems.at[1]),
    ]
    loads = []
    for t in range(tiles):
        cols = pl.ds(t * LANES, LANES)
        loads.append([
            pltpu.make_async_copy(fields.at[:, :, cols], staged.at[0:5, t, 0:VOL, :], sems.at[t, 0]),
            pltpu.make_async_copy(velocity.at[:, :, cols], staged.at[5:8, t, 0:VOL, :], sems.at[t, 1]),
            pltpu.make_async_copy(sound.at[:, cols], staged.at[8, t, 0:VOL, :], sems.at[t, 2]),
        ])
        for copy in loads[-1]:
            copy.start()
    for copy in small:
        copy.start()
    lane = lane_iota((1, LANES))
    column = lane % (2 * per_span)
    target = jnp.full((1, LANES), -1, jnp.int32)
    code = jnp.zeros((1, LANES), jnp.int32)
    for s in range(per_span):
        target = jnp.where(lane == s, slot_s[s * axial + half - 1], target)
        target = jnp.where(lane == per_span + s, slot_s[s * axial + half], target)
        code = jnp.where(column == per_span + s, turn_s[0, s], code)
    one = one_hot(target, elems)
    theta[VALS * FACE : VALS * FACE + 1, :] = jnp.zeros((1, elems), F32)
    odd = axis_parity("blk")

    for t in range(tiles):
        for copy in loads[t]:
            copy.wait()
        cols = tile_cols(t)

        @pl.when(odd == 0)
        def _():
            for f in range(VALS):
                theta[f * FACE : (f + 1) * FACE, cols] = face_rows(staged, value_index(f, 0), t, 0, ORDER)

        @pl.when(odd == 1)
        def _():
            for f in range(VALS):
                theta[f * FACE : (f + 1) * FACE, cols] = face_rows(staged, value_index(f, 0), t, 0, 0)

        for n, end in enumerate((ORDER, 0)):
            for f in range(VALS):
                at = n * rows + f * PAD
                store_halves(rows_hi, rows_lo, at, cols, face_rows(staged, value_index(f, 2), t, 2, end))
    out = pltpu.make_async_copy(theta, th_a, out_sem)
    out.start()
    for copy in small:
        copy.wait()
    both = dot(rows_hi[...], one) + dot(rows_lo[...], one)
    both = jnp.where(lane < per_span, both[0:rows], jnp.where(lane < 2 * per_span, both[rows:], 0.0))
    packed = both[0:PAD]
    for f in range(1, VALS):
        packed = packed + pltpu.roll(both[f * PAD : (f + 1) * PAD], f * 2 * per_span, 1)
    iface[...] = turned(packed, code, turn_t, stack_hi, stack_lo)
    for t in range(tiles):
        iface[PAD - tiles + t : PAD - tiles + t + 1, :] = slot_v[:, tile_cols(t)].astype(F32)
    out.wait()


LOCAL_FACES = ((1, 1), (1, 0), (2, 1), (2, 0))


def second_kernel(
    per_span, axial, slot_v, staged, th_b, sp_a, sp_b, index, rows_hi, rows_lo, theta, out_sem,
):
    elems = slot_v.shape[1]
    tiles = elems // LANES
    half = axial // 2
    rows = VALS * PAD
    theta[VALS * FACE : VALS * FACE + 1, :] = jnp.zeros((1, elems), F32)
    odd = axis_parity("blk")

    @pl.when(odd == 0)
    def _():
        for t in range(tiles):
            for f in range(VALS):
                theta[f * FACE : (f + 1) * FACE, tile_cols(t)] = face_rows(staged, value_index(f, 0), t, 0, 0)

    @pl.when(odd == 1)
    def _():
        for t in range(tiles):
            for f in range(VALS):
                theta[f * FACE : (f + 1) * FACE, tile_cols(t)] = face_rows(staged, value_index(f, 0), t, 0, ORDER)

    out = pltpu.make_async_copy(theta, th_b, out_sem)
    out.start()
    for n, (d, end) in enumerate(LOCAL_FACES):
        for t in range(tiles):
            for f in range(VALS):
                x = face_rows(staged, value_index(f, d), t, d, end * ORDER)
                store_halves(rows_hi, rows_lo, n * rows + f * PAD, tile_cols(t), x)

    def gathered(start, row):
        one = one_hot(row, elems)
        return dot(rows_hi[start : start + rows, :], one) + dot(rows_lo[start : start + rows, :], one)

    high = gathered(0, slot_v[:, elems - axial : elems])
    low = gathered(rows, slot_v[:, 0:axial])
    span_odd = axis_parity("span")

    @pl.when(span_odd == 0)
    def _():
        sp_a[...] = high
        sp_b[...] = low

    @pl.when(span_odd == 1)
    def _():
        sp_a[...] = low
        sp_b[...] = high

    slots = slot_v[...].astype(F32)
    lane = lane_iota((1, elems))
    position = lane % axial
    row = (lane // axial).astype(F32)
    lanes_f = lane.astype(F32)
    span_low = jnp.where(lane < axial, elems + lanes_f, pltpu.roll(slots, axial, 1))
    span_high = jnp.where(lane >= elems - axial, axial + lanes_f, pltpu.roll(slots, elems - axial, 1))
    none = elems + LANES - 1.0
    ax_low = jnp.where(position == half, elems + row, pltpu.roll(slots, 1, 1))
    ax_low = jnp.where(position == 0, none, ax_low)
    ax_high = jnp.where(position == half - 1, elems + per_span + row, pltpu.roll(slots, elems - 1, 1))
    ax_high = jnp.where(position == axial - 1, none, ax_high)
    index[...] = neighbour_index([span_low, span_high, ax_low, ax_high], slot_v)
    out.wait()


def local_kernel(index, rows_hi, rows_lo, ghosts):
    elems = index.shape[1]
    rows = VALS * PAD
    for n in range(len(LOCAL_FACES)):
        one = one_hot(index[n : n + 1, :], elems)
        at = slice(n * rows, (n + 1) * rows)
        ghosts[n] = dot(rows_hi[at, :], one) + dot(rows_lo[at, :], one)


def volume_kernel(staged, store_h, matrix_h, out, store, matrix, flux_hi, flux_lo, sems):
    tiles = staged.shape[1]
    loads = [pltpu.make_async_copy(matrix_h, matrix, sems.at[tiles])]
    for t in range(tiles):
        loads.append(pltpu.make_async_copy(store_h.at[:, :, pl.ds(t * LANES, LANES)], store.at[:, t, 0:VOL, :], sems.at[t]))
    for copy in loads:
        copy.start()
    step = 16
    for pair in range(tiles // 2):
        for half in range(2):
            t = 2 * pair + half
            cols = tile_cols(half)
            for r in range(0, VOL, step):
                n = min(step, VOL - r)
                rows = slice(r, r + n)
                q = [staged[f, t, rows, :] for f in range(5)]
                c = staged[8, t, rows, :]
                cp = c * q[4]
                for d in range(3):
                    m = staged[5 + d, t, rows, :]
                    cu = c * q[1 + d]
                    for f in range(5):
                        x = m * q[f]
                        if f in (0, 4):
                            x = x + cu
                        elif f == 1 + d:
                            x = x + cp
                        if n < step:
                            x = jnp.concatenate([x, jnp.zeros((step - n, LANES), F32)], 0)
                        hi, lo = halves(x)
                        flux_hi[f, d * LANES + r : d * LANES + r + step, cols] = hi
                        flux_lo[f, d * LANES + r : d * LANES + r + step, cols] = lo
        if pair == 0:
            for copy in loads:
                copy.wait()
        for f in range(5):
            a = dot(matrix[...], flux_hi[f])
            b = dot(matrix[0:LANES, :], flux_lo[f])
            total = a[0:LANES] + a[LANES : 2 * LANES] + b
            for half in range(2):
                t = 2 * pair + half
                out[f, t, 0:VOL, :] = section_decay * store[f, t, 0:VOL, :] + total[0:VOL, tile_cols(half)]


def theta_ghost(recv, index_row):
    one = one_hot(index_row, recv.shape[1])
    hi, lo = halves(recv[...])
    return dot(hi, one) + dot(lo, one)


def theta_side(staged, ghost, acc, shift, side):
    start = ORDER * FACE if side > 0 else 0
    for t in range(staged.shape[1]):
        own = [staged[value_index(f, 0), t, start : start + FACE, :] for f in range(VALS)]
        other = [ghost[f * FACE : (f + 1) * FACE, tile_cols(t)] for f in range(VALS)]
        for f, x in enumerate(surface(own, other, 0, side)):
            acc[f, t, start - shift : start - shift + FACE, :] += x


HIGH_ROW = (ORDER * FACE) // PAD * PAD


def face_kernel(
    per_span, sectors, slabs, pieces,
    offset_s, turn_s, slot_v, staged, part, index, ghosts, th_a, sp_a, sp_b, turn_h, *rest,
):
    iface = rest[:pieces]
    fields_out, store_out, window, index_b = rest[pieces : pieces + 4]
    acc, fresh, turn_t, stack_hi, stack_lo, ghost, sems, small_sem = rest[pieces + 4 :]
    elems = slot_v.shape[1]
    tiles = elems // LANES
    load = pltpu.make_async_copy(turn_h, turn_t, small_sem)
    load.start()
    sector = lax.axis_index("blk")
    odd = lax.rem(sector, 2)

    partner = lax.rem(sector + jnp.where(odd == 1, 1, sectors - 1), sectors)
    slots_a = iface[1][PAD - tiles : PAD, :]
    slots_b = jnp.zeros((tiles, LANES), F32)
    small = lane_iota((1, LANES))
    column = small % (2 * per_span)
    want = jnp.zeros((1, LANES), jnp.int32)
    code = jnp.zeros((1, LANES), jnp.int32)
    for s in range(per_span):
        shift = lax.rem(offset_s[s], sectors)
        want = jnp.where(column == s, lax.rem(sector - shift + sectors, sectors), want)
        want = jnp.where(column == per_span + s, lax.rem(sector + shift, sectors), want)
        code = jnp.where(column == s, turn_s[0, s], code)
    near = jnp.zeros((PAD, LANES), F32)
    k = 0
    for piece in iface:
        for b in range(piece.shape[0] // PAD):
            block = piece[b * PAD : (b + 1) * PAD, :]
            near = jnp.where(want == (sector ^ k), block, near)
            slots_b = jnp.where(partner == (sector ^ k), block[PAD - tiles :], slots_b)
            k += 1
    flat = lambda x: jnp.concatenate([x[t : t + 1] for t in range(tiles)], 1)
    theta_index = neighbour_index([flat(slots_a), flat(slots_b)], slot_v)
    index_b[...] = theta_index

    for t in range(tiles):
        for f in range(5):
            acc[f, t, 0:VOL, :] = part[f, t, 0:VOL, :]
    ghost[...] = theta_ghost(th_a, theta_index[0:1])

    @pl.when(odd == 0)
    def _():
        theta_side(staged, ghost, acc, 0, 1)

    @pl.when(odd == 1)
    def _():
        theta_side(staged, ghost, acc, 0, -1)

    def one_side(n, d, side, extra, wall, after=None):
        end = ORDER if side > 0 else 0
        index_row = index[n : n + 1, :]
        hi, lo = halves(extra)
        one = one_hot(index_row - elems, LANES)
        other_all = ghosts[n] + (dot(hi, one) + dot(lo, one))
        for t in range(tiles):
            cols = tile_cols(t)
            own = [face_rows(staged, value_index(f, d), t, d, end) for f in range(VALS)]
            other = [other_all[f * PAD : f * PAD + FACE, cols] for f in range(VALS)]
            if wall is not None:
                at_wall = jnp.logical_and(index_row[:, cols] >= elems, wall)
                for f in range(VALS):
                    other[f] = jnp.where(at_wall, -own[f] if f == 1 + d else own[f], other[f])
            for f, x in enumerate(surface(own, other, d, side)):
                add_face_rows(acc, f, t, d, end, x)
            if after is not None:
                after(t)

    slab = lax.axis_index("span")
    slab_odd = lax.rem(slab, 2) == 1
    one_side(0, 1, -1, jnp.where(slab_odd, sp_a[...], sp_b[...]), slab == 0)
    one_side(1, 1, 1, jnp.where(slab_odd, sp_b[...], sp_a[...]), slab == slabs - 1)

    load.wait()
    near = turned(near, code, turn_t, stack_hi, stack_lo)
    used = small < 2 * per_span
    extra = jnp.concatenate(
        [
            jnp.where(used, near if f == 0 else pltpu.roll(near, LANES - f * 2 * per_span, 1), 0.0)
            for f in range(VALS)
        ],
        0,
    )
    one_side(2, 2, -1, extra, None)

    def copies(t, low, high):
        cols = pl.ds(t * LANES, LANES)
        return (
            pltpu.make_async_copy(acc.at[:, t, low:high, :], store_out.at[:, low:high, cols], sems.at[t, 0]),
            pltpu.make_async_copy(fresh.at[:, t, low:high, :], fields_out.at[:, low:high, cols], sems.at[t, 1]),
        )

    def finish(t):
        for f in range(5):
            fresh[f, t, 0:VOL, :] = staged[f, t, 0:VOL, :] + section_gain * acc[f, t, 0:VOL, :]

        @pl.when(odd == 0)
        def _():
            for f in range(5):
                window[f, t] = acc[f, t, 0:PAD, :]
            for copy in copies(t, PAD, VOL):
                copy.start()

        @pl.when(odd == 1)
        def _():
            for f in range(5):
                window[f, t, 0 : VOL - HIGH_ROW] = acc[f, t, HIGH_ROW:VOL, :]
            for copy in copies(t, 0, HIGH_ROW):
                copy.start()

    one_side(3, 2, 1, extra, None, finish)

    @pl.when(odd == 0)
    def _():
        for t in range(tiles):
            for copy in copies(t, PAD, VOL):
                copy.wait()

    @pl.when(odd == 1)
    def _():
        for t in range(tiles):
            for copy in copies(t, 0, HIGH_ROW):
                copy.wait()


def last_kernel(index_b, staged, window, th_b, fields_in, store_in, fields_out, store_out, ghost, acc, fresh, sems):
    del fields_in, store_in
    tiles = staged.shape[1]
    ghost[...] = theta_ghost(th_b, index_b[1:2])
    acc[...] = window[...]

    def finish(side, low, high):
        theta_side(staged, ghost, acc, low, side)
        copies = []
        for t in range(tiles):
            for f in range(5):
                fresh[f, t, 0 : high - low, :] = (
                    staged[f, t, low:high, :] + section_gain * acc[f, t, 0 : high - low, :]
                )
            cols = pl.ds(t * LANES, LANES)
            pair = (
                pltpu.make_async_copy(acc.at[:, t, 0 : high - low, :], store_out.at[:, low:high, cols], sems.at[t, 0]),
                pltpu.make_async_copy(fresh.at[:, t, 0 : high - low, :], fields_out.at[:, low:high, cols], sems.at[t, 1]),
            )
            for copy in pair:
                copy.start()
            copies.extend(pair)
        for copy in copies:
            copy.wait()

    odd = axis_parity("blk")

    @pl.when(odd == 0)
    def _():
        finish(-1, 0, PAD)

    @pl.when(odd == 1)
    def _():
        finish(1, HIGH_ROW, VOL)


def params(limit=VMEM_LIMIT):
    return pltpu.CompilerParams(vmem_limit_bytes=limit)


def vmem_spec():
    return pl.BlockSpec(memory_space=pltpu.VMEM)


def hbm_spec():
    return pl.BlockSpec(memory_space=pltpu.HBM)


def smem_spec():
    return pl.BlockSpec(memory_space=pltpu.SMEM)


def in_hbm(x):
    return pltpu.with_memory_space_constraint(x, pltpu.HBM)


def in_vmem(x):
    return pltpu.with_memory_space_constraint(x, pltpu.VMEM)


def on_device(fields, section_store, mean_velocity, sound_speed, element_slot, face_turn, rotor_offset):
    per_theta, per_span = face_turn.shape
    elems = element_slot.shape[0]
    axial = elems // (per_theta * per_span)
    sectors, slabs = lax.axis_size("blk"), lax.axis_size("span")
    tiles = elems // LANES
    rows = VALS * PAD
    assert per_theta == 1 and axial == LANES and sectors % 2 == 0 and sectors & (sectors - 1) == 0
    assert 2 * per_span * VALS < LANES and FACE + tiles <= PAD
    dma = pltpu.SemaphoreType.DMA
    theta_rows = VALS * FACE + 1
    vmem, hbm = pltpu.VMEM, pltpu.HBM
    slot_h = in_hbm(element_slot.reshape(1, elems))
    stack = [vmem((8 * PAD, LANES), BF), vmem((8 * PAD, LANES), BF)]
    staged, th_a, iface, slot_v = pl.pallas_call(
        functools.partial(first_kernel, per_span, axial),
        out_shape=(
            vmem((9, tiles, LANES, LANES), F32),
            hbm((theta_rows, elems), F32),
            vmem((PAD, LANES), F32),
            vmem((1, elems), jnp.int32),
        ),
        in_specs=[smem_spec(), smem_spec()] + [hbm_spec()] * 5,
        out_specs=(vmem_spec(), hbm_spec(), vmem_spec(), vmem_spec()),
        scratch_shapes=[
            vmem((theta_rows, elems), F32),
            vmem((PAD, 8 * PAD), BF),
            vmem((2 * rows, elems), BF),
            vmem((2 * rows, elems), BF),
            *stack,
            dma((tiles, 3)),
            dma((2,)),
            dma(()),
        ],
        compiler_params=params(),
        name="first",
    )(
        in_hbm(element_slot), in_hbm(face_turn), slot_h, in_hbm(fields), in_hbm(mean_velocity), in_hbm(sound_speed),
        in_hbm(jnp.asarray(turn_matrix(True))),
    )

    pieces = [iface]
    pieces.append(lax.ppermute(iface, "blk", [(i, i ^ 1) for i in range(sectors)]))
    near_a = lax.ppermute(th_a, "blk", [(i, i ^ 1) for i in range(sectors)])
    reach = 2
    while reach < sectors:
        block = jnp.concatenate(pieces, 0)
        pieces.append(lax.ppermute(block, "blk", [(i, i ^ reach) for i in range(sectors)]))
        reach *= 2

    th_b, sp_a, sp_b, index, rows_hi, rows_lo = pl.pallas_call(
        functools.partial(second_kernel, per_span, axial),
        out_shape=(
            hbm((theta_rows, elems), F32),
            vmem((rows, LANES), F32),
            vmem((rows, LANES), F32),
            vmem((8, elems), jnp.int32),
            vmem((len(LOCAL_FACES) * rows, elems), BF),
            vmem((len(LOCAL_FACES) * rows, elems), BF),
        ),
        in_specs=[vmem_spec()] * 2,
        out_specs=(hbm_spec(),) + (vmem_spec(),) * 5,
        scratch_shapes=[vmem((theta_rows, elems), F32), dma(())],
        compiler_params=params(),
        name="second",
    )(in_vmem(slot_v), in_vmem(staged))
    pairs = [(i, (i + 1 if i % 2 else i - 1) % sectors) for i in range(sectors)]
    near_b = lax.ppermute(th_b, "blk", pairs)
    span_a = lax.ppermute(sp_a, "span", [(i, i ^ 1) for i in range(slabs) if i ^ 1 < slabs])
    pairs = [(i, i + 1 if i % 2 else i - 1) for i in range(slabs)]
    span_b = lax.ppermute(sp_b, "span", [(i, j) for i, j in pairs if 0 <= j < slabs])

    ghosts = pl.pallas_call(
        local_kernel,
        out_shape=vmem((len(LOCAL_FACES), rows, elems), F32),
        in_specs=[vmem_spec()] * 3,
        out_specs=vmem_spec(),
        compiler_params=params(),
        name="local",
    )(in_vmem(index), in_vmem(rows_hi), in_vmem(rows_lo))

    part = pl.pallas_call(
        volume_kernel,
        out_shape=vmem((5, tiles, LANES, LANES), F32),
        in_specs=[vmem_spec()] + [hbm_spec()] * 2,
        out_specs=vmem_spec(),
        scratch_shapes=[
            vmem((5, tiles, LANES, LANES), F32),
            vmem((2 * LANES, 3 * LANES), BF),
            vmem((5, 3 * LANES, 2 * LANES), BF),
            vmem((5, 3 * LANES, 2 * LANES), BF),
            dma((tiles + 1,)),
        ],
        compiler_params=params(),
        name="volume",
    )(in_vmem(staged), in_hbm(section_store), in_hbm(jnp.asarray(volume_matrix())))

    whole = hbm((5, VOL, elems), F32)
    fields_part, store_part, window, index_b = pl.pallas_call(
        functools.partial(face_kernel, per_span, sectors, slabs, len(pieces)),
        out_shape=(whole, whole, vmem((5, tiles, PAD, LANES), F32), vmem((8, elems), jnp.int32)),
        in_specs=[smem_spec(), smem_spec()] + [vmem_spec()] * 8 + [hbm_spec()] + [vmem_spec()] * len(pieces),
        out_specs=(hbm_spec(),) * 2 + (vmem_spec(),) * 2,
        scratch_shapes=[
            vmem((5, tiles, LANES, LANES), F32),
            vmem((5, tiles, LANES, LANES), F32),
            vmem((PAD, 8 * PAD), BF),
            *stack,
            vmem((theta_rows, elems), F32),
            dma((tiles, 2)),
            dma(()),
        ],
        compiler_params=params(),
        name="faces",
    )(
        in_hbm(rotor_offset), in_hbm(face_turn), in_vmem(slot_v), in_vmem(staged), in_vmem(part), in_vmem(index),
        in_vmem(ghosts), in_vmem(near_a), in_vmem(span_a), in_vmem(span_b), in_hbm(jnp.asarray(turn_matrix(False))),
        *[in_vmem(piece) for piece in pieces],
    )

    return pl.pallas_call(
        last_kernel,
        out_shape=(whole, whole),
        in_specs=[vmem_spec()] * 4 + [hbm_spec()] * 2,
        out_specs=(hbm_spec(),) * 2,
        scratch_shapes=[
            vmem((theta_rows, elems), F32),
            vmem((5, tiles, PAD, LANES), F32),
            vmem((5, tiles, PAD, LANES), F32),
            dma((tiles, 2)),
        ],
        input_output_aliases={4: 0, 5: 1},
        compiler_params=params(),
        name="last",
    )(in_vmem(index_b), in_vmem(staged), in_vmem(window), in_vmem(near_b), fields_part, store_part)


def solution(mesh):
    both = ("blk", "span")
    in_specs = (
        P(None, None, both),
        P(None, None, both),
        P(None, None, both),
        P(None, both),
        P(both),
        P("blk", "span"),
        P("span"),
    )
    out_specs = (P(None, None, both), P(None, None, both))
    return jax.shard_map(on_device, mesh=mesh, in_specs=in_specs, out_specs=out_specs, check_vma=False)
```

time: 49 us -> 41.3 us (0.84)
  local copies, waits for them, and re-layouts: 6.79 us -> 0 us
  waiting for transfers between devices: 14.6 us -> 13.1 us
  Pallas kernels: 14 us -> 14.8 us
  starting transfers between devices: 12.5 us -> 12 us
    unnamed x30 -> x0, local copies, waits for them, and re-layouts: 6.79 us -> none
    ppermute x2, waiting for transfers between devices: 13.1 us -> 11.6 us  [the longest x1 11.6 us: on_device(): lax.ppermute(iface, 'blk', [(i, i ^ 1) for i in range(sectors)])]
    pallas_call x4 -> x6, Pallas kernels: 14 us -> 14.8 us  [the longest x1 4.25 us: on_device(): pl.pallas_call(functools.partial(face_kernel, per_span, sectors, slabs, l...]
    ppermute x1, starting transfers between devices: 1.29 us -> 0.66 us  [on_device(): lax.ppermute(sp_b, 'span', [(i, j) for i, j in pairs if 0 <= j < slabs])]
  transfers between devices with their start and end apart: 7 -> 7, of which waited for: 3 -> 2; matrix products, arithmetic and copies ran while one was open for 0% -> 0% of each run, Pallas kernels for 17% -> 25%
where the time goes in v1:
time: 41.3 us; the launch traced here: 40.6 us
  Pallas kernels  14.8 us (36%)
  waiting for transfers between devices  13.1 us (32%)
  starting transfers between devices  12 us (29%)
  between operations  0.72 us (2%)
    ppermute x1, waiting for transfers between devices, on_device(): lax.ppermute(iface, 'blk', [(i, i ^ 1) for i in range(sectors)])  11.6 us
    ppermute x2, starting transfers between devices, on_device(): lax.ppermute(block, 'blk', [(i, i ^ reach) for i in range(sectors)])  4.66 us
    pallas_call x1, Pallas kernels, on_device(): pl.pallas_call(functools.partial(face_kernel, per_span, sectors, slabs, l...  4.25 us
    ppermute x1, starting transfers between devices, on_device(): near_b = lax.ppermute(th_b, 'blk', pairs)  3.64 us
    pallas_call x1, Pallas kernels, on_device(): pl.pallas_call(functools.partial(first_kernel, per_span, axial), out_shap...  3.28 us
    ppermute x1, starting transfers between devices, on_device(): near_a = lax.ppermute(th_a, 'blk', [(i, i ^ 1) for i in range(sectors)])  3.03 us
    pallas_call x1, Pallas kernels, on_device(): pl.pallas_call(volume_kernel, out_shape=vmem((5, tiles, LANES, LANES), F3...  3 us
    pallas_call x1, Pallas kernels, on_device(): pl.pallas_call(last_kernel, out_shape=(whole, whole), in_specs=[vmem_spec...  1.49 us
  transfers between devices with their start and end apart: 7, of which 2 were waited for; matrix products, arithmetic and copies ran while one was open for 0% of the time, Pallas kernels for 25%

profile of v1, /device:TPU:0, one launch (start us, length us, event | category | flops | bytes accessed | tf_op | source)
XLA Modules:
  0.0 40.6 jit_solution(3144483136076552739)
XLA Ops:
  0.6 3.3 %first.1 = (f32[9,4,128,128]{3,2,1,0:T(8,128)S(1)}, f32[176,512]{1,0:T(8,128)}, f32[32,128]{1,0:T(8,128)S(1)}, s32[1,512]{1,0:T(1,128)S(1)}) custom-call(s32[512]{0:T(512)} %slot_s.1, s32[1,4]{1,0:T(1,128)} %turn_s.3, s32[1,512]{1,0:T(1,128)} %bitcast.1, f32[5,125,512]{2,1,0:T(8,128)} %fields.1, f32[3,125,512]{2,1,0:T(8,128)} %velocity.1, f32[125,512]{1,0:T(8,128)} %sound.1, ...), custom_call_target="tpu_custom_call" | custom-call | tf_op jit(solution)/shard_map/first/pallas_call | solution.py:605
  3.9 3.0 %collective-permute-start = (f32[176,512]{1,0:T(8,128)}, f32[176,512]{1,0:T(8,128)S(1)}, u32[]{:S(2)}, u32[]{:S(2)}) collective-permute-start(f32[176,512]{1,0:T(8,128)} %get-tuple-element.21), channel_id=1, source_target_pairs={{0,4},{4,0},{8,12},{12,8},{16,20},{20,16},{24,28},{28,24},{1,5},{5... | collective-permute-start | bytes 1081352 | tf_op jit(solution)/shard_map/ppermute | solution.py:634
  7.0 1.4 %second.1 = (f32[176,512]{1,0:T(8,128)}, f32[224,128]{1,0:T(8,128)S(1)}, f32[224,128]{1,0:T(8,128)S(1)}, s32[8,512]{1,0:T(8,128)S(1)}, bf16[896,512]{1,0:T(8,128)(2,1)S(1)}, /*index=5*/bf16[896,512]{1,0:T(8,128)(2,1)S(1)}) custom-call(s32[1,512]{1,0:T(1,128)S(1)} %get-tuple-element.16.slot_v, f32[9,4,128,128]{3,2,1,0:T(8,128)S(1)} %get-tuple-element.17.staged), custom_call_target="tpu_custom_call" | custom-call | tf_op jit(solution)/shard_map/second/pallas_call | solution.py:641
  8.4 3.6 %collective-permute-start.6 = (f32[176,512]{1,0:T(8,128)}, f32[176,512]{1,0:T(8,128)S(1)}, u32[]{:S(2)}, u32[]{:S(2)}) collective-permute-start(f32[176,512]{1,0:T(8,128)} %get-tuple-element.27), channel_id=1, source_target_pairs={{0,28},{4,8},{8,4},{12,16},{16,12},{20,24},{24,20},{28,0},{1,29},{... | collective-permute-start | bytes 1081352 | tf_op jit(solution)/shard_map/ppermute | solution.py:658
  12.0 0.0 collective-permute-start.3
  12.0 11.6 %collective-permute-done.3.rest_1_ = f32[32,128]{1,0:T(8,128)S(1)} collective-permute-done((f32[32,128]{1,0:T(8,128)S(1)}, f32[32,128]{1,0:T(8,128)S(1)}, u32[]{:S(2)}, u32[]{:S(2)}) %collective-permute-start.3) | collective-permute-done | bytes 16416 | tf_op jit(solution)/shard_map/ppermute | solution.py:633
  23.7 1.8 %collective-permute-start.4 = (f32[64,128]{1,0:T(8,128)S(1)}, f32[64,128]{1,0:T(8,128)S(1)}, u32[]{:S(2)}, u32[]{:S(2)}) collective-permute-start(f32[64,128]{1,0:T(8,128)S(1)} %pad_maximum_fusion.1), channel_id=1, source_target_pairs={{0,8},{4,12},{8,0},{12,4},{16,24},{20,28},{24,16},{28,20},{1,9},{5... | collective-permute-start | bytes 98312 | tf_op jit(solution)/shard_map/ppermute | solution.py:638
  25.5 0.0 collective-permute-start.1
  25.5 0.7 %collective-permute-start.2 = (f32[224,128]{1,0:T(8,128)S(1)}, f32[224,128]{1,0:T(8,128)S(1)}, u32[]{:S(2)}, u32[]{:S(2)}) collective-permute-start(f32[224,128]{1,0:T(8,128)S(1)} %get-tuple-element.23), channel_id=1, source_target_pairs={{1,2},{2,1},{5,6},{6,5},{9,10},{10,9},{13,14},{14,13},{17,18},{18,... | collective-permute-start | bytes 344072 | tf_op jit(solution)/shard_map/ppermute | solution.py:661
  26.1 1.4 %collective-permute-done.4.rest_2_ = f32[64,128]{1,0:T(8,128)S(1)} collective-permute-done((f32[64,128]{1,0:T(8,128)S(1)}, f32[64,128]{1,0:T(8,128)S(1)}, u32[]{:S(2)}, u32[]{:S(2)}) %collective-permute-start.4) | collective-permute-done | bytes 32800 | tf_op jit(solution)/shard_map/ppermute | solution.py:638
  27.6 2.8 %collective-permute-start.5 = (f32[128,128]{1,0:T(8,128)S(1)}, f32[128,128]{1,0:T(8,128)S(1)}, u32[]{:S(2)}, u32[]{:S(2)}) collective-permute-start(f32[128,128]{1,0:T(8,128)S(1)} %pad_maximum_fusion), channel_id=1, source_target_pairs={{0,16},{4,20},{8,24},{12,28},{16,0},{20,4},{24,8},{28,12},{1,17},{... | collective-permute-start | bytes 196616 | tf_op jit(solution)/shard_map/ppermute | solution.py:638
  30.4 3.0 %volume.1.part = f32[5,4,128,128]{3,2,1,0:T(8,128)S(1)} custom-call(f32[9,4,128,128]{3,2,1,0:T(8,128)S(1)} %get-tuple-element.17.staged, f32[5,125,512]{2,1,0:T(8,128)} %store_h.1, bf16[256,384]{1,0:T(8,128)(2,1)} %constant.7.clone.matrix_h), custom_call_target="tpu_custom_call" | custom-call | tf_op jit(solution)/shard_map/volume/pallas_call | solution.py:672
  33.4 1.3 %local.1.ghosts = f32[4,224,512]{2,1,0:T(8,128)S(1)} custom-call(s32[8,512]{1,0:T(8,128)S(1)} %get-tuple-element.18.index, bf16[896,512]{1,0:T(8,128)(2,1)S(1)} %get-tuple-element.19.rows_hi, bf16[896,512]{1,0:T(8,128)(2,1)S(1)} %get-tuple-element.20.rows_lo), custom_call_target="tpu_custom_call" | custom-call | tf_op jit(solution)/shard_map/local/pallas_call | solution.py:663
  34.8 0.0 collective-permute-done.5.rest_3_
  34.8 0.0 collective-permute-done.1.sp_a
  34.8 0.0 collective-permute-done.2.sp_b
  34.8 0.0 collective-permute-done.th_a
  34.8 4.3 %faces.1 = (f32[5,125,512]{2,1,0:T(8,128)}, f32[5,125,512]{2,1,0:T(8,128)}, f32[5,4,32,128]{3,2,1,0:T(8,128)S(1)}, s32[8,512]{1,0:T(8,128)S(1)}) custom-call(s32[4]{0:T(128)} %offset_s.1, s32[1,4]{1,0:T(1,128)} %turn_s.3, s32[1,512]{1,0:T(1,128)S(1)} %get-tuple-element.16.slot_v, f32[9,4,128,128]{3,2,1,0:T(8,128)S(1)} %get-tuple-element.17.staged, ...), custom_call_target="tpu_custom_call" | custom-call | tf_op jit(solution)/shard_map/faces/pallas_call | solution.py:689
  39.1 0.0 collective-permute-done.6.th_b
  39.1 1.5 %last.1 = (f32[5,125,512]{2,1,0:T(8,128)}, f32[5,125,512]{2,1,0:T(8,128)}) custom-call(s32[8,512]{1,0:T(8,128)S(1)} %get-tuple-element.25.index_b, f32[9,4,128,128]{3,2,1,0:T(8,128)S(1)} %get-tuple-element.17.staged, f32[5,4,32,128]{3,2,1,0:T(8,128)S(1)} %get-tuple-element.26.window, ...), custom_call_target="tpu_custom_call", output_to_operand_aliasing={{0}: (4, {}), {1}: (5, {})} | custom-call | tf_op jit(solution)/shard_map/last/pallas_call | solution.py:711
  (2 shorter events, 0.0 us)
Async XLA Ops:
  3.9 30.9 %collective-permute-start = (f32[176,512]{1,0:T(8,128)}, f32[176,512]{1,0:T(8,128)S(1)}, u32[]{:S(2)}, u32[]{:S(2)}) collective-permute-start(f32[176,512]{1,0:T(8,128)} %get-tuple-element.21), channel_id=1, source_target_pairs={{0,4},{4,0},{8,12},{12,8},{16,20},{20,16},{24,28},{28,24},{1,5},{5... | collective-permute-start | bytes 1081352 | tf_op jit(solution)/shard_map/ppermute | solution.py:634
  8.4 30.7 %collective-permute-start.6 = (f32[176,512]{1,0:T(8,128)}, f32[176,512]{1,0:T(8,128)S(1)}, u32[]{:S(2)}, u32[]{:S(2)}) collective-permute-start(f32[176,512]{1,0:T(8,128)} %get-tuple-element.27), channel_id=1, source_target_pairs={{0,28},{4,8},{8,4},{12,16},{16,12},{20,24},{24,20},{28,0},{1,29},{... | collective-permute-start | bytes 1081352 | tf_op jit(solution)/shard_map/ppermute | solution.py:658
  12.0 11.6 %collective-permute-start.3 = (f32[32,128]{1,0:T(8,128)S(1)}, f32[32,128]{1,0:T(8,128)S(1)}, u32[]{:S(2)}, u32[]{:S(2)}) collective-permute-start(f32[32,128]{1,0:T(8,128)S(1)} %get-tuple-element.24.rest_0_), channel_id=1, source_target_pairs={{0,4},{4,0},{8,12},{12,8},{16,20},{20,16},{24,28},{28,24},{1,5},{5... | collective-permute-start | bytes 49160 | tf_op jit(solution)/shard_map/ppermute | solution.py:633
  23.7 3.9 %collective-permute-start.4 = (f32[64,128]{1,0:T(8,128)S(1)}, f32[64,128]{1,0:T(8,128)S(1)}, u32[]{:S(2)}, u32[]{:S(2)}) collective-permute-start(f32[64,128]{1,0:T(8,128)S(1)} %pad_maximum_fusion.1), channel_id=1, source_target_pairs={{0,8},{4,12},{8,0},{12,4},{16,24},{20,28},{24,16},{28,20},{1,9},{5... | collective-permute-start | bytes 98312 | tf_op jit(solution)/shard_map/ppermute | solution.py:638
  25.5 9.3 %collective-permute-start.1 = (f32[224,128]{1,0:T(8,128)S(1)}, f32[224,128]{1,0:T(8,128)S(1)}, u32[]{:S(2)}, u32[]{:S(2)}) collective-permute-start(f32[224,128]{1,0:T(8,128)S(1)} %get-tuple-element.22), channel_id=1, source_target_pairs={{0,1},{1,0},{2,3},{3,2},{4,5},{5,4},{6,7},{7,6},{8,9},{9,8},{10,11... | collective-permute-start | bytes 344072 | tf_op jit(solution)/shard_map/ppermute | solution.py:659
  25.5 9.3 %collective-permute-start.2 = (f32[224,128]{1,0:T(8,128)S(1)}, f32[224,128]{1,0:T(8,128)S(1)}, u32[]{:S(2)}, u32[]{:S(2)}) collective-permute-start(f32[224,128]{1,0:T(8,128)S(1)} %get-tuple-element.23), channel_id=1, source_target_pairs={{1,2},{2,1},{5,6},{6,5},{9,10},{10,9},{13,14},{14,13},{17,18},{18,... | collective-permute-start | bytes 344072 | tf_op jit(solution)/shard_map/ppermute | solution.py:661
  27.6 7.2 %collective-permute-start.5 = (f32[128,128]{1,0:T(8,128)S(1)}, f32[128,128]{1,0:T(8,128)S(1)}, u32[]{:S(2)}, u32[]{:S(2)}) collective-permute-start(f32[128,128]{1,0:T(8,128)S(1)} %pad_maximum_fusion), channel_id=1, source_target_pairs={{0,16},{4,20},{8,24},{12,28},{16,0},{20,4},{24,8},{28,12},{1,17},{... | collective-permute-start | bytes 196616 | tf_op jit(solution)/shard_map/ppermute | solution.py:638

commit v2 on v1

--- a/solution.py
+++ b/solution.py
@@ -105,10 +105,6 @@
     return lax.broadcasted_iota(jnp.int32, shape, len(shape) - 1)
 
 
-def row_iota(shape):
-    return lax.broadcasted_iota(jnp.int32, shape, 0)
-
-
 def face_rows(ref, v, tile, d, end):
     if d == 0:
         return ref[v, tile, pl.ds(end * FACE, FACE), :]
@@ -159,7 +155,10 @@
 
 
 def one_hot(index_row, count):
-    return (row_iota((count, index_row.shape[1])) == index_row).astype(BF)
+    short = jnp.broadcast_to(index_row, (16, index_row.shape[1])).astype(jnp.int16)
+    rows = lax.broadcasted_iota(jnp.int16, (16, index_row.shape[1]), 0)
+    one, zero = jnp.ones(short.shape, BF), jnp.zeros(short.shape, BF)
+    return jnp.concatenate([jnp.where(rows == short - r, one, zero) for r in range(0, count, 16)], 0)
 
 
 def store_halves(ref_hi, ref_lo, at, cols, value):
@@ -183,7 +182,7 @@
 
 def neighbour_index(rows, slot_v):
     elems = slot_v.shape[1]
-    own = (row_iota((elems, elems)) == slot_v[...]).astype(BF)
+    own = one_hot(slot_v[...], elems)
     base = 256.0
     table = jnp.concatenate(rows + [jnp.zeros((8 - len(rows), elems), F32)], 0)
     upper = jnp.floor(table * (1.0 / base))
@@ -194,8 +193,9 @@
 
 
 def first_kernel(
-    per_span, axial, slot_s, turn_s, slot_h, fields, velocity, sound, turn_h,
-    staged, th_a, iface, slot_v, theta, turn_t, rows_hi, rows_lo, stack_hi, stack_lo, sems, small_sems, out_sem,
+    per_span, axial, sectors, slot_l, turn_l, offset_l, slot_h, fields, velocity, sound, turn_h, forward_h,
+    staged, th_a, iface, slot_v, plan, own_packed, forward_t, theta, turn_t, rows_hi, rows_lo, stack_hi, stack_lo, slot_s, turn_s, offset_s,
+    sems, small_sems, out_sem,
 ):
     elems = slot_v.shape[1]
     tiles = elems // LANES
@@ -204,6 +204,10 @@
     small = [
         pltpu.make_async_copy(slot_h, slot_v, small_sems.at[0]),
         pltpu.make_async_copy(turn_h, turn_t, small_sems.at[1]),
+        pltpu.make_async_copy(slot_l, slot_s, small_sems.at[2]),
+        pltpu.make_async_copy(turn_l, turn_s, small_sems.at[3]),
+        pltpu.make_async_copy(offset_l, offset_s, small_sems.at[4]),
+        pltpu.make_async_copy(forward_h, forward_t, small_sems.at[5]),
     ]
     loads = []
     for t in range(tiles):
@@ -217,14 +221,25 @@
             copy.start()
     for copy in small:
         copy.start()
+    for copy in small:
+        copy.wait()
+    sector = lax.axis_index("blk")
     lane = lane_iota((1, LANES))
     column = lane % (2 * per_span)
     target = jnp.full((1, LANES), -1, jnp.int32)
     code = jnp.zeros((1, LANES), jnp.int32)
+    want = jnp.zeros((1, LANES), jnp.int32)
+    forward = jnp.zeros((1, LANES), jnp.int32)
     for s in range(per_span):
         target = jnp.where(lane == s, slot_s[s * axial + half - 1], target)
         target = jnp.where(lane == per_span + s, slot_s[s * axial + half], target)
         code = jnp.where(column == per_span + s, turn_s[0, s], code)
+        forward = jnp.where(column == s, turn_s[0, s], forward)
+        shift = lax.rem(offset_s[s], sectors)
+        want = jnp.where(column == s, lax.rem(sector - shift + sectors, sectors), want)
+        want = jnp.where(column == per_span + s, lax.rem(sector + shift, sectors), want)
+    plan[0:1, :] = want
+    plan[1:2, :] = forward
     one = one_hot(target, elems)
     theta[VALS * FACE : VALS * FACE + 1, :] = jnp.zeros((1, elems), F32)
     odd = axis_parity("blk")
@@ -250,13 +265,12 @@
                 store_halves(rows_hi, rows_lo, at, cols, face_rows(staged, value_index(f, 2), t, 2, end))
     out = pltpu.make_async_copy(theta, th_a, out_sem)
     out.start()
-    for copy in small:
-        copy.wait()
     both = dot(rows_hi[...], one) + dot(rows_lo[...], one)
     both = jnp.where(lane < per_span, both[0:rows], jnp.where(lane < 2 * per_span, both[rows:], 0.0))
     packed = both[0:PAD]
     for f in range(1, VALS):
         packed = packed + pltpu.roll(both[f * PAD : (f + 1) * PAD], f * 2 * per_span, 1)
+    own_packed[...] = packed
     iface[...] = turned(packed, code, turn_t, stack_hi, stack_lo)
     for t in range(tiles):
         iface[PAD - tiles + t : PAD - tiles + t + 1, :] = slot_v[:, tile_cols(t)].astype(F32)
@@ -339,13 +353,43 @@
         ghosts[n] = dot(rows_hi[at, :], one) + dot(rows_lo[at, :], one)
 
 
-def volume_kernel(staged, store_h, matrix_h, out, store, matrix, flux_hi, flux_lo, sems):
+def work_kernel(place, per_span, staged, index, ghosts, matrix_h, store_h, earlier, out, store, sems, *scratch):
+    del earlier
+
+    @pl.when(work_place() == place)
+    def _():
+        tiles = staged.shape[1]
+        elems = tiles * LANES
+        stores = [
+            pltpu.make_async_copy(store_h.at[:, :, pl.ds(t * LANES, LANES)], store.at[:, t, 0:VOL, :], sems.at[t])
+            for t in range(tiles)
+        ]
+        for copy in stores:
+            copy.start()
+        volume_terms(staged, matrix_h, out, *scratch)
+        for copy in stores:
+            copy.wait()
+        for t in range(tiles):
+            for f in range(5):
+                out[f, t, 0:VOL, :] += section_decay * store[f, t, 0:VOL, :]
+            for n, side in ((2, -1), (3, 1)):
+                at = index[n : n + 1, tile_cols(t)]
+                keep = jnp.logical_or(at < elems, at >= elems + 2 * per_span)
+                side_terms(staged, ghosts.at[n], out, 2, side, t, keep=keep)
+
+
+def work_start(place, per_span, staged, index, ghosts, matrix_h, store_h, out, *scratch):
+    work_kernel(place, per_span, staged, index, ghosts, matrix_h, store_h, None, out, *scratch)
+
+
+def work_place():
+    return jnp.where(axis_parity("span") == 1, 0, 1)
+
+
+def volume_terms(staged, matrix_h, out, matrix, flux_hi, flux_lo, sem):
     tiles = staged.shape[1]
-    loads = [pltpu.make_async_copy(matrix_h, matrix, sems.at[tiles])]
-    for t in range(tiles):
-        loads.append(pltpu.make_async_copy(store_h.at[:, :, pl.ds(t * LANES, LANES)], store.at[:, t, 0:VOL, :], sems.at[t]))
-    for copy in loads:
-        copy.start()
+    load = pltpu.make_async_copy(matrix_h, matrix, sem)
+    load.start()
     step = 16
     for pair in range(tiles // 2):
         for half in range(2):
@@ -369,18 +413,16 @@
                         if n < step:
                             x = jnp.concatenate([x, jnp.zeros((step - n, LANES), F32)], 0)
                         hi, lo = halves(x)
-                        flux_hi[f, d * LANES + r : d * LANES + r + step, cols] = hi
-                        flux_lo[f, d * LANES + r : d * LANES + r + step, cols] = lo
+                        flux_hi[pair, f, d * LANES + r : d * LANES + r + step, cols] = hi
+                        flux_lo[pair, f, d * LANES + r : d * LANES + r + step, cols] = lo
         if pair == 0:
-            for copy in loads:
-                copy.wait()
+            load.wait()
         for f in range(5):
-            a = dot(matrix[...], flux_hi[f])
-            b = dot(matrix[0:LANES, :], flux_lo[f])
+            a = dot(matrix[...], flux_hi[pair, f])
+            b = dot(matrix[0:LANES, :], flux_lo[pair, f])
             total = a[0:LANES] + a[LANES : 2 * LANES] + b
             for half in range(2):
-                t = 2 * pair + half
-                out[f, t, 0:VOL, :] = section_decay * store[f, t, 0:VOL, :] + total[0:VOL, tile_cols(half)]
+                out[f, 2 * pair + half] = total[:, tile_cols(half)]
 
 
 def theta_ghost(recv, index_row):
@@ -389,155 +431,161 @@
     return dot(hi, one) + dot(lo, one)
 
 
-def theta_side(staged, ghost, acc, shift, side):
+def theta_side(staged, ghost, acc, shift, side, t):
     start = ORDER * FACE if side > 0 else 0
-    for t in range(staged.shape[1]):
-        own = [staged[value_index(f, 0), t, start : start + FACE, :] for f in range(VALS)]
-        other = [ghost[f * FACE : (f + 1) * FACE, tile_cols(t)] for f in range(VALS)]
-        for f, x in enumerate(surface(own, other, 0, side)):
-            acc[f, t, start - shift : start - shift + FACE, :] += x
+    own = [staged[value_index(f, 0), t, start : start + FACE, :] for f in range(VALS)]
+    other = [ghost[f * FACE : (f + 1) * FACE, tile_cols(t)] for f in range(VALS)]
+    for f, x in enumerate(surface(own, other, 0, side)):
+        acc[f, t, start - shift : start - shift + FACE, :] += x
 
 
 HIGH_ROW = (ORDER * FACE) // PAD * PAD
 
 
-def face_kernel(
-    per_span, sectors, slabs, pieces,
-    offset_s, turn_s, slot_v, staged, part, index, ghosts, th_a, sp_a, sp_b, turn_h, *rest,
+def side_terms(staged, ghost_ref, acc, d, side, t, keep=None, wall=None):
+    cols = tile_cols(t)
+    end = ORDER if side > 0 else 0
+    own = [face_rows(staged, value_index(f, d), t, d, end) for f in range(VALS)]
+    other = [ghost_ref[f * PAD : f * PAD + FACE, cols] for f in range(VALS)]
+    if wall is not None:
+        for f in range(VALS):
+            other[f] = jnp.where(wall, -own[f] if f == 1 + d else own[f], other[f])
+    for f, x in enumerate(surface(own, other, d, side)):
+        add_face_rows(acc, f, t, d, end, x if keep is None else jnp.where(keep, x, 0.0))
+
+
+def face_kernel(slot_v, staged, index, ghosts, th_a, sp_a, iface_a, part, acc, ghost, whole):
+    del part
+    tiles = staged.shape[1]
+    odd = axis_parity("blk")
+    slots_a = jnp.concatenate([iface_a[PAD - tiles + t : PAD - tiles + t + 1, :] for t in range(tiles)], 1)
+    ghost[...] = theta_ghost(th_a, neighbour_index([slots_a], slot_v)[0:1])
+    span_side(0, staged, index, ghosts, sp_a, acc, whole, None)
+    for t in range(tiles):
+        @pl.when(odd == 0)
+        def _():
+            theta_side(staged, ghost, acc, 0, 1, t)
+
+        @pl.when(odd == 1)
+        def _():
+            theta_side(staged, ghost, acc, 0, -1, t)
+
+
+def span_side(other_pair, staged, index, ghosts, received, acc, whole, wall, tile=None):
+    slab_odd = axis_parity("span")
+    for n, side in ((0, -1), (1, 1)):
+        @pl.when(slab_odd == (1 - n if other_pair == 0 else n))
+        def _():
+            elems = index.shape[1]
+            if tile in (None, 0):
+                hi, lo = halves(received[...])
+                one = one_hot(index[n : n + 1, :] - elems, LANES)
+                whole[...] = ghosts[n] + (dot(hi, one) + dot(lo, one))
+            for t in range(staged.shape[1]) if tile is None else (tile,):
+                at_wall = None
+                if wall is not None:
+                    at_wall = jnp.logical_and(index[n : n + 1, tile_cols(t)] >= elems, wall)
+                side_terms(staged, whole, acc, 1, side, t, wall=at_wall)
+
+
+def late_kernel(
+    per_span, sectors, slabs, pieces, far,
+    plan, slot_v, staged, index, ghosts, own_packed, sp_b, turn_t, part, *rest,
 ):
+    del part
     iface = rest[:pieces]
-    fields_out, store_out, window, index_b = rest[pieces : pieces + 4]
-    acc, fresh, turn_t, stack_hi, stack_lo, ghost, sems, small_sem = rest[pieces + 4 :]
+    fields_out, store_out, acc, index_b = rest[pieces : pieces + 4]
+    fresh, whole, stack_hi, stack_lo, sems = rest[pieces + 4 :]
     elems = slot_v.shape[1]
     tiles = elems // LANES
-    load = pltpu.make_async_copy(turn_h, turn_t, small_sem)
-    load.start()
     sector = lax.axis_index("blk")
     odd = lax.rem(sector, 2)
 
     partner = lax.rem(sector + jnp.where(odd == 1, 1, sectors - 1), sectors)
-    slots_a = iface[1][PAD - tiles : PAD, :]
     slots_b = jnp.zeros((tiles, LANES), F32)
-    small = lane_iota((1, LANES))
-    column = small % (2 * per_span)
-    want = jnp.zeros((1, LANES), jnp.int32)
-    code = jnp.zeros((1, LANES), jnp.int32)
-    for s in range(per_span):
-        shift = lax.rem(offset_s[s], sectors)
-        want = jnp.where(column == s, lax.rem(sector - shift + sectors, sectors), want)
-        want = jnp.where(column == per_span + s, lax.rem(sector + shift, sectors), want)
-        code = jnp.where(column == s, turn_s[0, s], code)
+    want, code = plan[0:1, :], plan[1:2, :]
     near = jnp.zeros((PAD, LANES), F32)
-    k = 0
-    for piece in iface:
-        for b in range(piece.shape[0] // PAD):
-            block = piece[b * PAD : (b + 1) * PAD, :]
-            near = jnp.where(want == (sector ^ k), block, near)
-            slots_b = jnp.where(partner == (sector ^ k), block[PAD - tiles :], slots_b)
-            k += 1
+    blocks = [piece[b * PAD : (b + 1) * PAD, :] for piece in iface for b in range(piece.shape[0] // PAD)]
+    for k, block in zip(far, blocks):
+        near = jnp.where(want == (sector ^ k), block, near)
+        slots_b = jnp.where(partner == (sector ^ k), block[PAD - tiles :], slots_b)
     flat = lambda x: jnp.concatenate([x[t : t + 1] for t in range(tiles)], 1)
-    theta_index = neighbour_index([flat(slots_a), flat(slots_b)], slot_v)
-    index_b[...] = theta_index
+    index_b[...] = neighbour_index([flat(slots_b)], slot_v)
+    slab = lax.axis_index("span")
+
+    near = turned(near, code, turn_t, stack_hi, stack_lo)
+    lane = lane_iota((1, LANES))
+    used = lane < 2 * per_span
+    own, other = [], []
+    for f in range(VALS):
+        at = f * 2 * per_span
+        down = pltpu.roll(own_packed[...], LANES - at - per_span, 1)
+        up = pltpu.roll(own_packed[...], (LANES - at + per_span) % LANES, 1)
+        own.append(jnp.where(used, jnp.where(lane < per_span, down, up), 0.0))
+        theirs = near if f == 0 else pltpu.roll(near, LANES - at, 1)
+        other.append(jnp.where(used, theirs, 0.0))
+    low = surface(own, other, 2, -1)
+    high = surface(own, other, 2, 1)
+    terms = jnp.concatenate([jnp.where(lane < per_span, x, y) for x, y in zip(low, high)], 0)
+    hi, lo = halves(jnp.where(used, terms, 0.0))
+
+    def placed(n):
+        one = one_hot(index[n : n + 1, :] - elems, LANES)
+        return dot(hi, one) + dot(lo, one)
+
+    fixes = (placed(2), placed(3))
+
+    def copies(t, low_row, high_row):
+        cols = pl.ds(t * LANES, LANES)
+        rows = slice(low_row, high_row)
+        return (
+            pltpu.make_async_copy(acc.at[:, t, rows, :], store_out.at[:, rows, cols], sems.at[t, 0]),
+            pltpu.make_async_copy(fresh.at[:, t, rows, :], fields_out.at[:, rows, cols], sems.at[t, 1]),
+        )
+
+    def each_way(action):
+        @pl.when(odd == 0)
+        def _():
+            action(PAD, VOL)
+
+        @pl.when(odd == 1)
+        def _():
+            action(0, HIGH_ROW)
+
+    def send(t):
+        def action(low_row, high_row):
+            for copy in copies(t, low_row, high_row):
+                copy.start()
+
+        return action
+
+    def wait(low_row, high_row):
+        for t in range(tiles):
+            for copy in copies(t, low_row, high_row):
+                copy.wait()
 
     for t in range(tiles):
+        span_side(1, staged, index, ghosts, sp_b, acc, whole, jnp.logical_or(slab == 0, slab == slabs - 1), t)
         for f in range(5):
-            acc[f, t, 0:VOL, :] = part[f, t, 0:VOL, :]
-    ghost[...] = theta_ghost(th_a, theta_index[0:1])
-
-    @pl.when(odd == 0)
-    def _():
-        theta_side(staged, ghost, acc, 0, 1)
-
-    @pl.when(odd == 1)
-    def _():
-        theta_side(staged, ghost, acc, 0, -1)
-
-    def one_side(n, d, side, extra, wall, after=None):
-        end = ORDER if side > 0 else 0
-        index_row = index[n : n + 1, :]
-        hi, lo = halves(extra)
-        one = one_hot(index_row - elems, LANES)
-        other_all = ghosts[n] + (dot(hi, one) + dot(lo, one))
-        for t in range(tiles):
-            cols = tile_cols(t)
-            own = [face_rows(staged, value_index(f, d), t, d, end) for f in range(VALS)]
-            other = [other_all[f * PAD : f * PAD + FACE, cols] for f in range(VALS)]
-            if wall is not None:
-                at_wall = jnp.logical_and(index_row[:, cols] >= elems, wall)
-                for f in range(VALS):
-                    other[f] = jnp.where(at_wall, -own[f] if f == 1 + d else own[f], other[f])
-            for f, x in enumerate(surface(own, other, d, side)):
-                add_face_rows(acc, f, t, d, end, x)
-            if after is not None:
-                after(t)
-
-    slab = lax.axis_index("span")
-    slab_odd = lax.rem(slab, 2) == 1
-    one_side(0, 1, -1, jnp.where(slab_odd, sp_a[...], sp_b[...]), slab == 0)
-    one_side(1, 1, 1, jnp.where(slab_odd, sp_b[...], sp_a[...]), slab == slabs - 1)
-
-    load.wait()
-    near = turned(near, code, turn_t, stack_hi, stack_lo)
-    used = small < 2 * per_span
-    extra = jnp.concatenate(
-        [
-            jnp.where(used, near if f == 0 else pltpu.roll(near, LANES - f * 2 * per_span, 1), 0.0)
-            for f in range(VALS)
-        ],
-        0,
-    )
-    one_side(2, 2, -1, extra, None)
-
-    def copies(t, low, high):
-        cols = pl.ds(t * LANES, LANES)
-        return (
-            pltpu.make_async_copy(acc.at[:, t, low:high, :], store_out.at[:, low:high, cols], sems.at[t, 0]),
-            pltpu.make_async_copy(fresh.at[:, t, low:high, :], fields_out.at[:, low:high, cols], sems.at[t, 1]),
-        )
-
-    def finish(t):
+            for fix, end in zip(fixes, (0, ORDER)):
+                add_face_rows(acc, f, t, 2, end, fix[f * PAD : f * PAD + FACE, tile_cols(t)])
         for f in range(5):
             fresh[f, t, 0:VOL, :] = staged[f, t, 0:VOL, :] + section_gain * acc[f, t, 0:VOL, :]
-
-        @pl.when(odd == 0)
-        def _():
-            for f in range(5):
-                window[f, t] = acc[f, t, 0:PAD, :]
-            for copy in copies(t, PAD, VOL):
-                copy.start()
-
-        @pl.when(odd == 1)
-        def _():
-            for f in range(5):
-                window[f, t, 0 : VOL - HIGH_ROW] = acc[f, t, HIGH_ROW:VOL, :]
-            for copy in copies(t, 0, HIGH_ROW):
-                copy.start()
-
-    one_side(3, 2, 1, extra, None, finish)
-
-    @pl.when(odd == 0)
-    def _():
-        for t in range(tiles):
-            for copy in copies(t, PAD, VOL):
-                copy.wait()
-
-    @pl.when(odd == 1)
-    def _():
-        for t in range(tiles):
-            for copy in copies(t, 0, HIGH_ROW):
-                copy.wait()
-
-
-def last_kernel(index_b, staged, window, th_b, fields_in, store_in, fields_out, store_out, ghost, acc, fresh, sems):
+        each_way(send(t))
+    each_way(wait)
+
+
+def last_kernel(index_b, staged, part, th_b, fields_in, store_in, fields_out, store_out, ghost, acc, fresh, sems):
     del fields_in, store_in
     tiles = staged.shape[1]
-    ghost[...] = theta_ghost(th_b, index_b[1:2])
-    acc[...] = window[...]
+    ghost[...] = theta_ghost(th_b, index_b[0:1])
 
     def finish(side, low, high):
-        theta_side(staged, ghost, acc, low, side)
         copies = []
         for t in range(tiles):
+            for f in range(5):
+                acc[f, t, 0 : high - low, :] = part[f, t, low:high, :]
+            theta_side(staged, ghost, acc, low, side, t)
             for f in range(5):
                 fresh[f, t, 0 : high - low, :] = (
                     staged[f, t, low:high, :] + section_gain * acc[f, t, 0 : high - low, :]
@@ -576,16 +624,17 @@
     return pl.BlockSpec(memory_space=pltpu.HBM)
 
 
-def smem_spec():
-    return pl.BlockSpec(memory_space=pltpu.SMEM)
-
-
 def in_hbm(x):
     return pltpu.with_memory_space_constraint(x, pltpu.HBM)
 
 
 def in_vmem(x):
     return pltpu.with_memory_space_constraint(x, pltpu.VMEM)
+
+
+def reaches(sectors):
+    steps = [1 << bit for bit in range(sectors.bit_length() - 1)]
+    return steps[:1] + steps[:0:-1]
 
 
 def on_device(fields, section_store, mean_velocity, sound_speed, element_slot, face_turn, rotor_offset):
@@ -602,41 +651,45 @@
     vmem, hbm = pltpu.VMEM, pltpu.HBM
     slot_h = in_hbm(element_slot.reshape(1, elems))
     stack = [vmem((8 * PAD, LANES), BF), vmem((8 * PAD, LANES), BF)]
-    staged, th_a, iface, slot_v = pl.pallas_call(
-        functools.partial(first_kernel, per_span, axial),
+    staged, th_a, iface, slot_v, plan, own_packed, forward_t = pl.pallas_call(
+        functools.partial(first_kernel, per_span, axial, sectors),
         out_shape=(
             vmem((9, tiles, LANES, LANES), F32),
             hbm((theta_rows, elems), F32),
             vmem((PAD, LANES), F32),
             vmem((1, elems), jnp.int32),
+            vmem((8, LANES), jnp.int32),
+            vmem((PAD, LANES), F32),
+            vmem((PAD, 8 * PAD), BF),
         ),
-        in_specs=[smem_spec(), smem_spec()] + [hbm_spec()] * 5,
-        out_specs=(vmem_spec(), hbm_spec(), vmem_spec(), vmem_spec()),
+        in_specs=[hbm_spec()] * 9,
+        out_specs=(vmem_spec(), hbm_spec()) + (vmem_spec(),) * 5,
         scratch_shapes=[
             vmem((theta_rows, elems), F32),
             vmem((PAD, 8 * PAD), BF),
             vmem((2 * rows, elems), BF),
             vmem((2 * rows, elems), BF),
             *stack,
+            pltpu.SMEM((elems,), jnp.int32),
+            pltpu.SMEM((per_theta, per_span), jnp.int32),
+            pltpu.SMEM((per_span,), jnp.int32),
             dma((tiles, 3)),
-            dma((2,)),
+            dma((6,)),
             dma(()),
         ],
         compiler_params=params(),
         name="first",
     )(
-        in_hbm(element_slot), in_hbm(face_turn), slot_h, in_hbm(fields), in_hbm(mean_velocity), in_hbm(sound_speed),
-        in_hbm(jnp.asarray(turn_matrix(True))),
+        in_hbm(element_slot), in_hbm(face_turn), in_hbm(rotor_offset), slot_h, in_hbm(fields), in_hbm(mean_velocity), in_hbm(sound_speed),
+        in_hbm(jnp.asarray(turn_matrix(True))), in_hbm(jnp.asarray(turn_matrix(False))),
     )
 
-    pieces = [iface]
-    pieces.append(lax.ppermute(iface, "blk", [(i, i ^ 1) for i in range(sectors)]))
+    pieces, far = [iface], [0]
     near_a = lax.ppermute(th_a, "blk", [(i, i ^ 1) for i in range(sectors)])
-    reach = 2
-    while reach < sectors:
+    for reach in reaches(sectors):
         block = jnp.concatenate(pieces, 0)
         pieces.append(lax.ppermute(block, "blk", [(i, i ^ reach) for i in range(sectors)]))
-        reach *= 2
+        far += [k ^ reach for k in far]
 
     th_b, sp_a, sp_b, index, rows_hi, rows_lo = pl.pallas_call(
         functools.partial(second_kernel, per_span, axial),
@@ -669,43 +722,63 @@
         name="local",
     )(in_vmem(index), in_vmem(rows_hi), in_vmem(rows_lo))
 
+    part = None
+    block = (5, tiles, LANES, LANES)
+    for place in range(2):
+        work = pl.pallas_call(
+            functools.partial(work_kernel if place else work_start, place, per_span),
+            out_shape=vmem(block, F32),
+            in_specs=[vmem_spec()] * 3 + [hbm_spec()] * 2 + [vmem_spec()] * (place > 0),
+            out_specs=vmem_spec(),
+            scratch_shapes=[
+                vmem(block, F32),
+                dma((tiles,)),
+                vmem((2 * LANES, 3 * LANES), BF),
+                vmem((tiles // 2, 5, 3 * LANES, 2 * LANES), BF),
+                vmem((tiles // 2, 5, 3 * LANES, 2 * LANES), BF),
+                dma(()),
+            ],
+            input_output_aliases={5: 0} if place else {},
+            compiler_params=params(),
+        )
+        operands = [in_vmem(staged), in_vmem(index), in_vmem(ghosts)]
+        operands += [in_hbm(jnp.asarray(volume_matrix())), in_hbm(section_store)]
+        if place:
+            operands.append(in_vmem(part))
+        part = work(*operands)
+
     part = pl.pallas_call(
-        volume_kernel,
-        out_shape=vmem((5, tiles, LANES, LANES), F32),
-        in_specs=[vmem_spec()] + [hbm_spec()] * 2,
+        face_kernel,
+        out_shape=vmem(block, F32),
+        in_specs=[vmem_spec()] * 8,
         out_specs=vmem_spec(),
-        scratch_shapes=[
-            vmem((5, tiles, LANES, LANES), F32),
-            vmem((2 * LANES, 3 * LANES), BF),
-            vmem((5, 3 * LANES, 2 * LANES), BF),
-            vmem((5, 3 * LANES, 2 * LANES), BF),
-            dma((tiles + 1,)),
-        ],
-        compiler_params=params(),
-        name="volume",
-    )(in_vmem(staged), in_hbm(section_store), in_hbm(jnp.asarray(volume_matrix())))
-
-    whole = hbm((5, VOL, elems), F32)
-    fields_part, store_part, window, index_b = pl.pallas_call(
-        functools.partial(face_kernel, per_span, sectors, slabs, len(pieces)),
-        out_shape=(whole, whole, vmem((5, tiles, PAD, LANES), F32), vmem((8, elems), jnp.int32)),
-        in_specs=[smem_spec(), smem_spec()] + [vmem_spec()] * 8 + [hbm_spec()] + [vmem_spec()] * len(pieces),
-        out_specs=(hbm_spec(),) * 2 + (vmem_spec(),) * 2,
-        scratch_shapes=[
-            vmem((5, tiles, LANES, LANES), F32),
-            vmem((5, tiles, LANES, LANES), F32),
-            vmem((PAD, 8 * PAD), BF),
-            *stack,
-            vmem((theta_rows, elems), F32),
-            dma((tiles, 2)),
-            dma(()),
-        ],
+        scratch_shapes=[vmem((theta_rows, elems), F32), vmem((rows, elems), F32)],
+        input_output_aliases={7: 0},
         compiler_params=params(),
         name="faces",
     )(
-        in_hbm(rotor_offset), in_hbm(face_turn), in_vmem(slot_v), in_vmem(staged), in_vmem(part), in_vmem(index),
-        in_vmem(ghosts), in_vmem(near_a), in_vmem(span_a), in_vmem(span_b), in_hbm(jnp.asarray(turn_matrix(False))),
-        *[in_vmem(piece) for piece in pieces],
+        in_vmem(slot_v), in_vmem(staged), in_vmem(index), in_vmem(ghosts), in_vmem(near_a), in_vmem(span_a),
+        in_vmem(pieces[1]), in_vmem(part),
+    )
+
+    whole = hbm((5, VOL, elems), F32)
+    fields_part, store_part, part, index_b = pl.pallas_call(
+        functools.partial(late_kernel, per_span, sectors, slabs, len(pieces), far),
+        out_shape=(whole, whole, vmem(block, F32), vmem((8, elems), jnp.int32)),
+        in_specs=[vmem_spec()] * (9 + len(pieces)),
+        out_specs=(hbm_spec(),) * 2 + (vmem_spec(),) * 2,
+        scratch_shapes=[
+            vmem(block, F32),
+            vmem((rows, elems), F32),
+            *stack,
+            dma((tiles, 2)),
+        ],
+        input_output_aliases={8: 2},
+        compiler_params=params(),
+        name="late",
+    )(
+        in_vmem(plan), in_vmem(slot_v), in_vmem(staged), in_vmem(index), in_vmem(ghosts), in_vmem(own_packed),
+        in_vmem(span_b), in_vmem(forward_t), in_vmem(part), *[in_vmem(piece) for piece in pieces],
     )
 
     return pl.pallas_call(
@@ -722,7 +795,7 @@
         input_output_aliases={4: 0, 5: 1},
         compiler_params=params(),
         name="last",
-    )(in_vmem(index_b), in_vmem(staged), in_vmem(window), in_vmem(near_b), fields_part, store_part)
+    )(in_vmem(index_b), in_vmem(staged), in_vmem(part), in_vmem(near_b), fields_part, store_part)
 
 
 def solution(mesh):

time: 41.3 us -> 40.9 us (level); the launches traced: 40.6 us -> 40.6 us
  starting transfers between devices: 12 us -> 14.7 us
  Pallas kernels: 14.8 us -> 13.1 us
  waiting for transfers between devices: 13.1 us -> 12 us
    ppermute x1 -> x0, waiting for transfers between devices: 11.6 us -> none  [on_device(): lax.ppermute(iface, 'blk', [(i, i ^ 1) for i in range(sectors)])]
    ppermute x2 -> x3, waiting for transfers between devices: 1.42 us -> 12 us  [on_device(): lax.ppermute(block, 'blk', [(i, i ^ reach) for i in range(sectors)])]
    ppermute x1, starting transfers between devices: 0.01 us -> 2.94 us  [on_device(): lax.ppermute(sp_a, 'span', [(i, i ^ 1) for i in range(slabs) if i ^ 1 < s...]
    pallas_call x3 -> x5, Pallas kernels: 10.5 us -> 9.62 us  [the longest x2 3.3 us: on_device(): part = work(*operands)]
    ppermute x2 -> x3, starting transfers between devices: 4.66 us -> 4.48 us  [on_device(): lax.ppermute(block, 'blk', [(i, i ^ reach) for i in range(sectors)])]
  transfers between devices with their start and end apart: 7 -> 7, of which waited for: 2 -> 1; matrix products, arithmetic and copies ran while one was open for 0% -> 0% of each run, Pallas kernels for 25% -> 22%
where the time goes in v2:
time: 40.9 us; the launch traced here: 40.6 us
  starting transfers between devices  14.7 us (36%)
  Pallas kernels  13.1 us (32%)
  waiting for transfers between devices  12 us (29%)
  between operations  0.74 us (2%)
    ppermute x3, waiting for transfers between devices, on_device(): lax.ppermute(block, 'blk', [(i, i ^ reach) for i in range(sectors)])  12 us
    ppermute x3, starting transfers between devices, on_device(): lax.ppermute(block, 'blk', [(i, i ^ reach) for i in range(sectors)])  4.48 us
    ppermute x1, starting transfers between devices, on_device(): near_b = lax.ppermute(th_b, 'blk', pairs)  3.63 us
    pallas_call x2, Pallas kernels, on_device(): part = work(*operands)  3.3 us
    ppermute x1, starting transfers between devices, on_device(): near_a = lax.ppermute(th_a, 'blk', [(i, i ^ 1) for i in range(sectors)])  3.04 us
    ppermute x1, starting transfers between devices, on_device(): lax.ppermute(sp_a, 'span', [(i, i ^ 1) for i in range(slabs) if i ^ 1 < s...  2.94 us
    pallas_call x1, Pallas kernels, on_device(): pl.pallas_call(functools.partial(first_kernel, per_span, axial, sectors),...  2.72 us
    pallas_call x1, Pallas kernels, on_device(): pl.pallas_call(functools.partial(late_kernel, per_span, sectors, slabs, l...  2.36 us
  transfers between devices with their start and end apart: 7, of which 1 were waited for; matrix products, arithmetic and copies ran while one was open for 0% of the time, Pallas kernels for 22%

profile of v2, /device:TPU:0, one launch (start us, length us, event | category | flops | bytes accessed | tf_op | source)
XLA Modules:
  0.0 40.6 jit_solution(17515113365216150624)
XLA Ops:
  0.6 2.7 %first.1 = (f32[9,4,128,128]{3,2,1,0:T(8,128)S(1)}, f32[176,512]{1,0:T(8,128)}, f32[32,128]{1,0:T(8,128)S(1)}, s32[1,512]{1,0:T(1,128)S(1)}, s32[8,128]{1,0:T(8,...) custom-call(s32[512]{0:T(512)} %slot_l.1, s32[1,4]{1,0:T(1,128)} %turn_l.1, s32[4]{0:T(128)} %offset_l.1, ...), custom_call_target="tpu_custom_call" | custom-call | tf_op jit(solution)/shard_map/first/pallas_call | solution.py:654
  3.4 3.0 %collective-permute-start.1 = (f32[176,512]{1,0:T(8,128)}, f32[176,512]{1,0:T(8,128)S(1)}, u32[]{:S(2)}, u32[]{:S(2)}) collective-permute-start(f32[176,512]{1,0:T(8,128)} %get-tuple-element.28), channel_id=1, source_target_pairs={{0,4},{4,0},{8,12},{12,8},{16,20},{20,16},{24,28},{28,24},{1,5},{5... | collective-permute-start | bytes 1081352 | tf_op jit(solution)/shard_map/ppermute | solution.py:688
  6.4 1.0 %second.1 = (f32[176,512]{1,0:T(8,128)}, f32[224,128]{1,0:T(8,128)S(1)}, f32[224,128]{1,0:T(8,128)S(1)}, s32[8,512]{1,0:T(8,128)S(1)}, bf16[896,512]{1,0:T(8,128)(2,1)S(1)}, /*index=5*/bf16[896,512]{1,0:T(8,128)(2,1)S(1)}) custom-call(s32[1,512]{1,0:T(1,128)S(1)} %get-tuple-element.20.slot_v, f32[9,4,128,128]{3,2,1,0:T(8,128)S(1)} %get-tuple-element.21.staged), custom_call_target="tpu_custom_call" | custom-call | tf_op jit(solution)/shard_map/second/pallas_call | solution.py:694
  7.5 3.6 %collective-permute-start.6 = (f32[176,512]{1,0:T(8,128)}, f32[176,512]{1,0:T(8,128)S(1)}, u32[]{:S(2)}, u32[]{:S(2)}) collective-permute-start(f32[176,512]{1,0:T(8,128)} %get-tuple-element.33), channel_id=1, source_target_pairs={{0,28},{4,8},{8,4},{12,16},{16,12},{20,24},{24,20},{28,0},{1,29},{... | collective-permute-start | bytes 1081352 | tf_op jit(solution)/shard_map/ppermute | solution.py:711
  11.1 0.0 collective-permute-start.3
  11.1 12.0 %collective-permute-done.3.iface_a.rest_1_ = f32[32,128]{1,0:T(8,128)S(1)} collective-permute-done((f32[32,128]{1,0:T(8,128)S(1)}, f32[32,128]{1,0:T(8,128)S(1)}, u32[]{:S(2)}, u32[]{:S(2)}) %collective-permute-start.3) | collective-permute-done | bytes 16416 | tf_op jit(solution)/shard_map/ppermute | solution.py:691
  23.1 2.8 %collective-permute-start.4 = (f32[64,128]{1,0:T(8,128)S(1)}, f32[64,128]{1,0:T(8,128)S(1)}, u32[]{:S(2)}, u32[]{:S(2)}) collective-permute-start(f32[64,128]{1,0:T(8,128)S(1)} %pad_maximum_fusion.1), channel_id=1, source_target_pairs={{0,16},{4,20},{8,24},{12,28},{16,0},{20,4},{24,8},{28,12},{1,17},{... | collective-permute-start | bytes 98312 | tf_op jit(solution)/shard_map/ppermute | solution.py:691
  25.9 0.7 %collective-permute-start = (f32[224,128]{1,0:T(8,128)S(1)}, f32[224,128]{1,0:T(8,128)S(1)}, u32[]{:S(2)}, u32[]{:S(2)}) collective-permute-start(f32[224,128]{1,0:T(8,128)S(1)} %get-tuple-element.26), channel_id=1, source_target_pairs={{1,2},{2,1},{5,6},{6,5},{9,10},{10,9},{13,14},{14,13},{17,18},{18,... | collective-permute-start | bytes 344072 | tf_op jit(solution)/shard_map/ppermute | solution.py:714
  26.6 2.9 %collective-permute-start.2 = (f32[224,128]{1,0:T(8,128)S(1)}, f32[224,128]{1,0:T(8,128)S(1)}, u32[]{:S(2)}, u32[]{:S(2)}) collective-permute-start(f32[224,128]{1,0:T(8,128)S(1)} %get-tuple-element.29), channel_id=1, source_target_pairs={{0,1},{1,0},{2,3},{3,2},{4,5},{5,4},{6,7},{7,6},{8,9},{9,8},{10,11... | collective-permute-start | bytes 344072 | tf_op jit(solution)/shard_map/ppermute | solution.py:712
  29.5 0.0 collective-permute-done.4.rest_2_
  29.5 1.6 %collective-permute-start.5 = (f32[128,128]{1,0:T(8,128)S(1)}, f32[128,128]{1,0:T(8,128)S(1)}, u32[]{:S(2)}, u32[]{:S(2)}) collective-permute-start(f32[128,128]{1,0:T(8,128)S(1)} %pad_maximum_fusion), channel_id=1, source_target_pairs={{0,8},{4,12},{8,0},{12,4},{16,24},{20,28},{24,16},{28,20},{1,9},{5... | collective-permute-start | bytes 196616 | tf_op jit(solution)/shard_map/ppermute | solution.py:691
  31.2 1.1 %local.1.ghosts = f32[4,224,512]{2,1,0:T(8,128)S(1)} custom-call(s32[8,512]{1,0:T(8,128)S(1)} %get-tuple-element.22.index, bf16[896,512]{1,0:T(8,128)(2,1)S(1)} %get-tuple-element.23.rows_hi, bf16[896,512]{1,0:T(8,128)(2,1)S(1)} %get-tuple-element.24.rows_lo), custom_call_target="tpu_custom_call" | custom-call | tf_op jit(solution)/shard_map/local/pallas_call | solution.py:716
  32.3 0.1 shard_map.122.earlier
  32.4 3.2 %shard_map.123.part = f32[5,4,128,128]{3,2,1,0:T(8,128)S(1)} custom-call(f32[9,4,128,128]{3,2,1,0:T(8,128)S(1)} %get-tuple-element.21.staged, s32[8,512]{1,0:T(8,128)S(1)} %get-tuple-element.22.index, f32[4,224,512]{2,1,0:T(8,128)S(1)} %local.1.ghosts, bf16[256,384]{1,0:T(8,128)(2,1)} %constant.8.clone.matrix_h, ...), custom_call_target="tpu_custom_call", output_to_operand_aliasing={{}: (5, {})} | custom-call | tf_op jit(solution)/shard_map/pallas_call | solution.py:748
  35.6 0.0 collective-permute-done.2.sp_a
  35.6 0.0 collective-permute-done.1.th_a
  35.6 1.2 %faces.1.part = f32[5,4,128,128]{3,2,1,0:T(8,128)S(1)} custom-call(s32[1,512]{1,0:T(1,128)S(1)} %get-tuple-element.20.slot_v, f32[9,4,128,128]{3,2,1,0:T(8,128)S(1)} %get-tuple-element.21.staged, s32[8,512]{1,0:T(8,128)S(1)} %get-tuple-element.22.index, f32[4,224,512]{2,1,0:T(8,128)S(1)} %local.1.ghosts, ...), custom_call_target="tpu_custom_call", output_to_operand_aliasing={{}: (7, {})} | custom-call | tf_op jit(solution)/shard_map/faces/pallas_call | solution.py:750
  36.9 0.0 collective-permute-done.5.rest_3_
  36.9 0.0 collective-permute-done.sp_b
  36.9 2.4 %late.1 = (f32[5,125,512]{2,1,0:T(8,128)}, f32[5,125,512]{2,1,0:T(8,128)}, f32[5,4,128,128]{3,2,1,0:T(8,128)S(1)}, s32[8,512]{1,0:T(8,128)S(1)}) custom-call(s32[8,128]{1,0:T(8,128)S(1)} %get-tuple-element.19.plan, s32[1,512]{1,0:T(1,128)S(1)} %get-tuple-element.20.slot_v, ...), custom_call_target="tpu_custom_call", output_to_operand_aliasing={{2}: (8, {})} | custom-call | tf_op jit(solution)/shard_map/late/pallas_call | solution.py:765
  39.3 0.0 collective-permute-done.6.th_b
  39.3 1.3 %last.1 = (f32[5,125,512]{2,1,0:T(8,128)}, f32[5,125,512]{2,1,0:T(8,128)}) custom-call(s32[8,512]{1,0:T(8,128)S(1)} %get-tuple-element.31.index_b, f32[9,4,128,128]{3,2,1,0:T(8,128)S(1)} %get-tuple-element.21.staged, f32[5,4,128,128]{3,2,1,0:T(8,128)S(1)} %get-tuple-element.32.part, ...), custom_call_target="tpu_custom_call", output_to_operand_aliasing={{0}: (4, {}), {1}: (5, {})} | custom-call | tf_op jit(solution)/shard_map/last/pallas_call | solution.py:784
  (2 shorter events, 0.0 us)
Async XLA Ops:
  3.4 32.3 %collective-permute-start.1 = (f32[176,512]{1,0:T(8,128)}, f32[176,512]{1,0:T(8,128)S(1)}, u32[]{:S(2)}, u32[]{:S(2)}) collective-permute-start(f32[176,512]{1,0:T(8,128)} %get-tuple-element.28), channel_id=1, source_target_pairs={{0,4},{4,0},{8,12},{12,8},{16,20},{20,16},{24,28},{28,24},{1,5},{5... | collective-permute-start | bytes 1081352 | tf_op jit(solution)/shard_map/ppermute | solution.py:688
  7.5 31.8 %collective-permute-start.6 = (f32[176,512]{1,0:T(8,128)}, f32[176,512]{1,0:T(8,128)S(1)}, u32[]{:S(2)}, u32[]{:S(2)}) collective-permute-start(f32[176,512]{1,0:T(8,128)} %get-tuple-element.33), channel_id=1, source_target_pairs={{0,28},{4,8},{8,4},{12,16},{16,12},{20,24},{24,20},{28,0},{1,29},{... | collective-permute-start | bytes 1081352 | tf_op jit(solution)/shard_map/ppermute | solution.py:711
  11.1 12.0 %collective-permute-start.3 = (f32[32,128]{1,0:T(8,128)S(1)}, f32[32,128]{1,0:T(8,128)S(1)}, u32[]{:S(2)}, u32[]{:S(2)}) collective-permute-start(f32[32,128]{1,0:T(8,128)S(1)} %get-tuple-element.30.rest_0_), channel_id=1, source_target_pairs={{0,4},{4,0},{8,12},{12,8},{16,20},{20,16},{24,28},{28,24},{1,5},{5... | collective-permute-start | bytes 49160 | tf_op jit(solution)/shard_map/ppermute | solution.py:691
  23.1 6.4 %collective-permute-start.4 = (f32[64,128]{1,0:T(8,128)S(1)}, f32[64,128]{1,0:T(8,128)S(1)}, u32[]{:S(2)}, u32[]{:S(2)}) collective-permute-start(f32[64,128]{1,0:T(8,128)S(1)} %pad_maximum_fusion.1), channel_id=1, source_target_pairs={{0,16},{4,20},{8,24},{12,28},{16,0},{20,4},{24,8},{28,12},{1,17},{... | collective-permute-start | bytes 98312 | tf_op jit(solution)/shard_map/ppermute | solution.py:691
  25.9 11.0 %collective-permute-start = (f32[224,128]{1,0:T(8,128)S(1)}, f32[224,128]{1,0:T(8,128)S(1)}, u32[]{:S(2)}, u32[]{:S(2)}) collective-permute-start(f32[224,128]{1,0:T(8,128)S(1)} %get-tuple-element.26), channel_id=1, source_target_pairs={{1,2},{2,1},{5,6},{6,5},{9,10},{10,9},{13,14},{14,13},{17,18},{18,... | collective-permute-start | bytes 344072 | tf_op jit(solution)/shard_map/ppermute | solution.py:714
  26.6 9.0 %collective-permute-start.2 = (f32[224,128]{1,0:T(8,128)S(1)}, f32[224,128]{1,0:T(8,128)S(1)}, u32[]{:S(2)}, u32[]{:S(2)}) collective-permute-start(f32[224,128]{1,0:T(8,128)S(1)} %get-tuple-element.29), channel_id=1, source_target_pairs={{0,1},{1,0},{2,3},{3,2},{4,5},{5,4},{6,7},{7,6},{8,9},{9,8},{10,11... | collective-permute-start | bytes 344072 | tf_op jit(solution)/shard_map/ppermute | solution.py:712
  29.5 7.4 %collective-permute-start.5 = (f32[128,128]{1,0:T(8,128)S(1)}, f32[128,128]{1,0:T(8,128)S(1)}, u32[]{:S(2)}, u32[]{:S(2)}) collective-permute-start(f32[128,128]{1,0:T(8,128)S(1)} %pad_maximum_fusion), channel_id=1, source_target_pairs={{0,8},{4,12},{8,0},{12,4},{16,24},{20,28},{24,16},{28,20},{1,9},{5... | collective-permute-start | bytes 196616 | tf_op jit(solution)/shard_map/ppermute | solution.py:691

commit v3 on v2

--- a/solution.py
+++ b/solution.py
@@ -431,15 +431,12 @@
     return dot(hi, one) + dot(lo, one)
 
 
-def theta_side(staged, ghost, acc, shift, side, t):
+def theta_side(staged, ghost, acc, side, t):
     start = ORDER * FACE if side > 0 else 0
     own = [staged[value_index(f, 0), t, start : start + FACE, :] for f in range(VALS)]
     other = [ghost[f * FACE : (f + 1) * FACE, tile_cols(t)] for f in range(VALS)]
     for f, x in enumerate(surface(own, other, 0, side)):
-        acc[f, t, start - shift : start - shift + FACE, :] += x
-
-
-HIGH_ROW = (ORDER * FACE) // PAD * PAD
+        acc[f, t, start : start + FACE, :] += x
 
 
 def side_terms(staged, ghost_ref, acc, d, side, t, keep=None, wall=None):
@@ -454,7 +451,7 @@
         add_face_rows(acc, f, t, d, end, x if keep is None else jnp.where(keep, x, 0.0))
 
 
-def face_kernel(slot_v, staged, index, ghosts, th_a, sp_a, iface_a, part, acc, ghost, whole):
+def face_kernel(slot_v, staged, index, ghosts, th_a, sp_a, iface_a, part, acc, whole, ghost):
     del part
     tiles = staged.shape[1]
     odd = axis_parity("blk")
@@ -464,11 +461,62 @@
     for t in range(tiles):
         @pl.when(odd == 0)
         def _():
-            theta_side(staged, ghost, acc, 0, 1, t)
+            theta_side(staged, ghost, acc, 1, t)
 
         @pl.when(odd == 1)
         def _():
-            theta_side(staged, ghost, acc, 0, -1, t)
+            theta_side(staged, ghost, acc, -1, t)
+
+
+def interface_kernel(
+    per_span, sectors, pieces, far,
+    plan, slot_v, index, own_packed, turn_t, part, *rest,
+):
+    del part
+    iface = rest[:pieces]
+    acc, picks, stack_hi, stack_lo = rest[pieces:]
+    elems = slot_v.shape[1]
+    tiles = elems // LANES
+    sector = lax.axis_index("blk")
+    odd = lax.rem(sector, 2)
+
+    partner = lax.rem(sector + jnp.where(odd == 1, 1, sectors - 1), sectors)
+    slots_b = jnp.zeros((tiles, LANES), F32)
+    want, code = plan[0:1, :], plan[1:2, :]
+    near = jnp.zeros((PAD, LANES), F32)
+    blocks = [piece[b * PAD : (b + 1) * PAD, :] for piece in iface for b in range(piece.shape[0] // PAD)]
+    for k, block in zip(far, blocks):
+        near = jnp.where(want == (sector ^ k), block, near)
+        slots_b = jnp.where(partner == (sector ^ k), block[PAD - tiles :], slots_b)
+    flat = lambda x: jnp.concatenate([x[t : t + 1] for t in range(tiles)], 1)
+    picks[...] = one_hot(neighbour_index([flat(slots_b)], slot_v)[0:1], elems)
+
+    near = turned(near, code, turn_t, stack_hi, stack_lo)
+    lane = lane_iota((1, LANES))
+    used = lane < 2 * per_span
+    own, other = [], []
+    for f in range(VALS):
+        at = f * 2 * per_span
+        down = pltpu.roll(own_packed[...], LANES - at - per_span, 1)
+        up = pltpu.roll(own_packed[...], (LANES - at + per_span) % LANES, 1)
+        own.append(jnp.where(used, jnp.where(lane < per_span, down, up), 0.0))
+        theirs = near if f == 0 else pltpu.roll(near, LANES - at, 1)
+        other.append(jnp.where(used, theirs, 0.0))
+    low = surface(own, other, 2, -1)
+    high = surface(own, other, 2, 1)
+    terms = jnp.concatenate([jnp.where(lane < per_span, x, y) for x, y in zip(low, high)], 0)
+    hi, lo = halves(jnp.where(used, terms, 0.0))
+
+    def placed(n):
+        one = one_hot(index[n : n + 1, :] - elems, LANES)
+        return dot(hi, one) + dot(lo, one)
+
+    fixes = (placed(2), placed(3))
+
+    for t in range(tiles):
+        for f in range(5):
+            for fix, end in zip(fixes, (0, ORDER)):
+                add_face_rows(acc, f, t, 2, end, fix[f * PAD : f * PAD + FACE, tile_cols(t)])
 
 
 def span_side(other_pair, staged, index, ghosts, received, acc, whole, wall, tile=None):
@@ -488,128 +536,40 @@
                 side_terms(staged, whole, acc, 1, side, t, wall=at_wall)
 
 
-def late_kernel(
-    per_span, sectors, slabs, pieces, far,
-    plan, slot_v, staged, index, ghosts, own_packed, sp_b, turn_t, part, *rest,
-):
+def late_kernel(slabs, staged, index, ghosts, sp_b, part, acc, whole):
     del part
-    iface = rest[:pieces]
-    fields_out, store_out, acc, index_b = rest[pieces : pieces + 4]
-    fresh, whole, stack_hi, stack_lo, sems = rest[pieces + 4 :]
-    elems = slot_v.shape[1]
-    tiles = elems // LANES
-    sector = lax.axis_index("blk")
-    odd = lax.rem(sector, 2)
-
-    partner = lax.rem(sector + jnp.where(odd == 1, 1, sectors - 1), sectors)
-    slots_b = jnp.zeros((tiles, LANES), F32)
-    want, code = plan[0:1, :], plan[1:2, :]
-    near = jnp.zeros((PAD, LANES), F32)
-    blocks = [piece[b * PAD : (b + 1) * PAD, :] for piece in iface for b in range(piece.shape[0] // PAD)]
-    for k, block in zip(far, blocks):
-        near = jnp.where(want == (sector ^ k), block, near)
-        slots_b = jnp.where(partner == (sector ^ k), block[PAD - tiles :], slots_b)
-    flat = lambda x: jnp.concatenate([x[t : t + 1] for t in range(tiles)], 1)
-    index_b[...] = neighbour_index([flat(slots_b)], slot_v)
     slab = lax.axis_index("span")
-
-    near = turned(near, code, turn_t, stack_hi, stack_lo)
-    lane = lane_iota((1, LANES))
-    used = lane < 2 * per_span
-    own, other = [], []
-    for f in range(VALS):
-        at = f * 2 * per_span
-        down = pltpu.roll(own_packed[...], LANES - at - per_span, 1)
-        up = pltpu.roll(own_packed[...], (LANES - at + per_span) % LANES, 1)
-        own.append(jnp.where(used, jnp.where(lane < per_span, down, up), 0.0))
-        theirs = near if f == 0 else pltpu.roll(near, LANES - at, 1)
-        other.append(jnp.where(used, theirs, 0.0))
-    low = surface(own, other, 2, -1)
-    high = surface(own, other, 2, 1)
-    terms = jnp.concatenate([jnp.where(lane < per_span, x, y) for x, y in zip(low, high)], 0)
-    hi, lo = halves(jnp.where(used, terms, 0.0))
-
-    def placed(n):
-        one = one_hot(index[n : n + 1, :] - elems, LANES)
-        return dot(hi, one) + dot(lo, one)
-
-    fixes = (placed(2), placed(3))
-
-    def copies(t, low_row, high_row):
-        cols = pl.ds(t * LANES, LANES)
-        rows = slice(low_row, high_row)
-        return (
-            pltpu.make_async_copy(acc.at[:, t, rows, :], store_out.at[:, rows, cols], sems.at[t, 0]),
-            pltpu.make_async_copy(fresh.at[:, t, rows, :], fields_out.at[:, rows, cols], sems.at[t, 1]),
-        )
-
-    def each_way(action):
+    span_side(1, staged, index, ghosts, sp_b, acc, whole, jnp.logical_or(slab == 0, slab == slabs - 1))
+
+
+def last_kernel(staged, picks, th_b, part, fields_out, store_out, acc, fresh, ghost, sems):
+    del part
+    tiles = staged.shape[1]
+    odd = axis_parity("blk")
+    hi, lo = halves(th_b[...])
+    ghost[...] = dot(hi, picks[...]) + dot(lo, picks[...])
+    copies = []
+    for t in range(tiles):
         @pl.when(odd == 0)
         def _():
-            action(PAD, VOL)
+            theta_side(staged, ghost, acc, -1, t)
 
         @pl.when(odd == 1)
         def _():
-            action(0, HIGH_ROW)
-
-    def send(t):
-        def action(low_row, high_row):
-            for copy in copies(t, low_row, high_row):
-                copy.start()
-
-        return action
-
-    def wait(low_row, high_row):
-        for t in range(tiles):
-            for copy in copies(t, low_row, high_row):
-                copy.wait()
-
-    for t in range(tiles):
-        span_side(1, staged, index, ghosts, sp_b, acc, whole, jnp.logical_or(slab == 0, slab == slabs - 1), t)
-        for f in range(5):
-            for fix, end in zip(fixes, (0, ORDER)):
-                add_face_rows(acc, f, t, 2, end, fix[f * PAD : f * PAD + FACE, tile_cols(t)])
+            theta_side(staged, ghost, acc, 1, t)
+
         for f in range(5):
             fresh[f, t, 0:VOL, :] = staged[f, t, 0:VOL, :] + section_gain * acc[f, t, 0:VOL, :]
-        each_way(send(t))
-    each_way(wait)
-
-
-def last_kernel(index_b, staged, part, th_b, fields_in, store_in, fields_out, store_out, ghost, acc, fresh, sems):
-    del fields_in, store_in
-    tiles = staged.shape[1]
-    ghost[...] = theta_ghost(th_b, index_b[0:1])
-
-    def finish(side, low, high):
-        copies = []
-        for t in range(tiles):
-            for f in range(5):
-                acc[f, t, 0 : high - low, :] = part[f, t, low:high, :]
-            theta_side(staged, ghost, acc, low, side, t)
-            for f in range(5):
-                fresh[f, t, 0 : high - low, :] = (
-                    staged[f, t, low:high, :] + section_gain * acc[f, t, 0 : high - low, :]
-                )
-            cols = pl.ds(t * LANES, LANES)
-            pair = (
-                pltpu.make_async_copy(acc.at[:, t, 0 : high - low, :], store_out.at[:, low:high, cols], sems.at[t, 0]),
-                pltpu.make_async_copy(fresh.at[:, t, 0 : high - low, :], fields_out.at[:, low:high, cols], sems.at[t, 1]),
-            )
-            for copy in pair:
-                copy.start()
-            copies.extend(pair)
-        for copy in copies:
-            copy.wait()
-
-    odd = axis_parity("blk")
-
-    @pl.when(odd == 0)
-    def _():
-        finish(-1, 0, PAD)
-
-    @pl.when(odd == 1)
-    def _():
-        finish(1, HIGH_ROW, VOL)
+        cols = pl.ds(t * LANES, LANES)
+        pair = [
+            pltpu.make_async_copy(acc.at[:, t, 0:VOL, :], store_out.at[:, :, cols], sems.at[t, 0]),
+            pltpu.make_async_copy(fresh.at[:, t, 0:VOL, :], fields_out.at[:, :, cols], sems.at[t, 1]),
+        ]
+        for copy in pair:
+            copy.start()
+        copies += pair
+    for copy in copies:
+        copy.wait()
 
 
 def params(limit=VMEM_LIMIT):
@@ -752,7 +712,7 @@
         out_shape=vmem(block, F32),
         in_specs=[vmem_spec()] * 8,
         out_specs=vmem_spec(),
-        scratch_shapes=[vmem((theta_rows, elems), F32), vmem((rows, elems), F32)],
+        scratch_shapes=[vmem((rows, elems), F32), vmem((theta_rows, elems), F32)],
         input_output_aliases={7: 0},
         compiler_params=params(),
         name="faces",
@@ -761,41 +721,43 @@
         in_vmem(pieces[1]), in_vmem(part),
     )
 
-    whole = hbm((5, VOL, elems), F32)
-    fields_part, store_part, part, index_b = pl.pallas_call(
-        functools.partial(late_kernel, per_span, sectors, slabs, len(pieces), far),
-        out_shape=(whole, whole, vmem(block, F32), vmem((8, elems), jnp.int32)),
-        in_specs=[vmem_spec()] * (9 + len(pieces)),
-        out_specs=(hbm_spec(),) * 2 + (vmem_spec(),) * 2,
-        scratch_shapes=[
-            vmem(block, F32),
-            vmem((rows, elems), F32),
-            *stack,
-            dma((tiles, 2)),
-        ],
-        input_output_aliases={8: 2},
+    part, picks = pl.pallas_call(
+        functools.partial(interface_kernel, per_span, sectors, len(pieces), far),
+        out_shape=(vmem(block, F32), vmem((elems, elems), BF)),
+        in_specs=[vmem_spec()] * (6 + len(pieces)),
+        out_specs=(vmem_spec(),) * 2,
+        scratch_shapes=stack,
+        input_output_aliases={5: 0},
+        compiler_params=params(),
+        name="interface",
+    )(
+        in_vmem(plan), in_vmem(slot_v), in_vmem(index), in_vmem(own_packed), in_vmem(forward_t), in_vmem(part),
+        *[in_vmem(piece) for piece in pieces],
+    )
+
+    part = pl.pallas_call(
+        functools.partial(late_kernel, slabs),
+        out_shape=vmem(block, F32),
+        in_specs=[vmem_spec()] * 5,
+        out_specs=vmem_spec(),
+        scratch_shapes=[vmem((rows, elems), F32)],
+        input_output_aliases={4: 0},
         compiler_params=params(),
         name="late",
-    )(
-        in_vmem(plan), in_vmem(slot_v), in_vmem(staged), in_vmem(index), in_vmem(ghosts), in_vmem(own_packed),
-        in_vmem(span_b), in_vmem(forward_t), in_vmem(part), *[in_vmem(piece) for piece in pieces],
-    )
-
-    return pl.pallas_call(
+    )(in_vmem(staged), in_vmem(index), in_vmem(ghosts), in_vmem(span_b), in_vmem(part))
+
+    whole = hbm((5, VOL, elems), F32)
+    fields_next, store_next, _ = pl.pallas_call(
         last_kernel,
-        out_shape=(whole, whole),
-        in_specs=[vmem_spec()] * 4 + [hbm_spec()] * 2,
-        out_specs=(hbm_spec(),) * 2,
-        scratch_shapes=[
-            vmem((theta_rows, elems), F32),
-            vmem((5, tiles, PAD, LANES), F32),
-            vmem((5, tiles, PAD, LANES), F32),
-            dma((tiles, 2)),
-        ],
-        input_output_aliases={4: 0, 5: 1},
+        out_shape=(whole, whole, vmem(block, F32)),
+        in_specs=[vmem_spec()] * 4,
+        out_specs=(hbm_spec(),) * 2 + (vmem_spec(),),
+        scratch_shapes=[vmem(block, F32), vmem((theta_rows, elems), F32), dma((tiles, 2))],
+        input_output_aliases={3: 2},
         compiler_params=params(),
         name="last",
-    )(in_vmem(index_b), in_vmem(staged), in_vmem(part), in_vmem(near_b), fields_part, store_part)
+    )(in_vmem(staged), in_vmem(picks), in_vmem(near_b), in_vmem(part))
+    return fields_next, store_next
 
 
 def solution(mesh):

time: 40.9 us -> 39.6 us (0.968)
  the two profiles are of different devices: /device:TPU:0 before, /device:TPU:1 now
where the time goes in v3:
time: 39.6 us; the launch traced here: 39.3 us
  starting transfers between devices  13.9 us (35%)
  Pallas kernels  12.6 us (32%)
  waiting for transfers between devices  12 us (30%)
  between operations  0.76 us (2%)
    ppermute x3, waiting for transfers between devices, on_device(): lax.ppermute(block, 'blk', [(i, i ^ reach) for i in range(sectors)])  12 us
    ppermute x3, starting transfers between devices, on_device(): lax.ppermute(block, 'blk', [(i, i ^ reach) for i in range(sectors)])  3.64 us
    ppermute x1, starting transfers between devices, on_device(): near_b = lax.ppermute(th_b, 'blk', pairs)  3.35 us
    pallas_call x2, Pallas kernels, on_device(): part = work(*operands)  3.32 us
    ppermute x1, starting transfers between devices, on_device(): lax.ppermute(sp_b, 'span', [(i, j) for i, j in pairs if 0 <= j < slabs])  3.02 us
    pallas_call x1, Pallas kernels, on_device(): pl.pallas_call(functools.partial(first_kernel, per_span, axial, sectors),...  2.72 us
    ppermute x1, starting transfers between devices, on_device(): near_a = lax.ppermute(th_a, 'blk', [(i, i ^ 1) for i in range(sectors)])  2.1 us
    pallas_call x1, Pallas kernels, on_device(): pl.pallas_call(last_kernel, out_shape=(whole, whole, vmem(block, F32)), i...  1.99 us
  transfers between devices with their start and end apart: 7, of which 1 were waited for; matrix products, arithmetic and copies ran while one was open for 0% of the time, Pallas kernels for 20%

profile of v3, /device:TPU:1, one launch (start us, length us, event | category | flops | bytes accessed | tf_op | source)
XLA Modules:
  0.0 39.3 jit_solution(13357896714092811396)
XLA Ops:
  0.6 2.7 %first.1 = (f32[9,4,128,128]{3,2,1,0:T(8,128)S(1)}, f32[176,512]{1,0:T(8,128)}, f32[32,128]{1,0:T(8,128)S(1)}, s32[1,512]{1,0:T(1,128)S(1)}, s32[8,128]{1,0:T(8,...) custom-call(s32[512]{0:T(512)} %slot_l.1, s32[1,4]{1,0:T(1,128)} %turn_l.1, s32[4]{0:T(128)} %offset_l.1, ...), custom_call_target="tpu_custom_call" | custom-call | tf_op jit(solution)/shard_map/first/pallas_call | solution.py:614
  3.4 2.1 %collective-permute-start = (f32[176,512]{1,0:T(8,128)}, f32[176,512]{1,0:T(8,128)S(1)}, u32[]{:S(2)}, u32[]{:S(2)}) collective-permute-start(f32[176,512]{1,0:T(8,128)} %get-tuple-element.27), channel_id=1, source_target_pairs={{0,4},{4,0},{8,12},{12,8},{16,20},{20,16},{24,28},{28,24},{1,5},{5... | collective-permute-start | bytes 1081352 | tf_op jit(solution)/shard_map/ppermute | solution.py:648
  5.5 1.0 %second.1 = (f32[176,512]{1,0:T(8,128)}, f32[224,128]{1,0:T(8,128)S(1)}, f32[224,128]{1,0:T(8,128)S(1)}, s32[8,512]{1,0:T(8,128)S(1)}, bf16[896,512]{1,0:T(8,128)(2,1)S(1)}, /*index=5*/bf16[896,512]{1,0:T(8,128)(2,1)S(1)}) custom-call(s32[1,512]{1,0:T(1,128)S(1)} %get-tuple-element.21.slot_v, f32[9,4,128,128]{3,2,1,0:T(8,128)S(1)} %get-tuple-element.19.staged), custom_call_target="tpu_custom_call" | custom-call | tf_op jit(solution)/shard_map/second/pallas_call | solution.py:654
  6.5 3.4 %collective-permute-start.5 = (f32[176,512]{1,0:T(8,128)}, f32[176,512]{1,0:T(8,128)S(1)}, u32[]{:S(2)}, u32[]{:S(2)}) collective-permute-start(f32[176,512]{1,0:T(8,128)} %get-tuple-element.31), channel_id=1, source_target_pairs={{0,28},{4,8},{8,4},{12,16},{16,12},{20,24},{24,20},{28,0},{1,29},{... | collective-permute-start | bytes 1081352 | tf_op jit(solution)/shard_map/ppermute | solution.py:671
  9.9 0.0 collective-permute-start.2
  9.9 12.0 %collective-permute-done.2.iface_a.rest_1_ = f32[32,128]{1,0:T(8,128)S(1)} collective-permute-done((f32[32,128]{1,0:T(8,128)S(1)}, f32[32,128]{1,0:T(8,128)S(1)}, u32[]{:S(2)}, u32[]{:S(2)}) %collective-permute-start.2) | collective-permute-done | bytes 16416 | tf_op jit(solution)/shard_map/ppermute | solution.py:651
  21.9 2.3 %collective-permute-start.3 = (f32[64,128]{1,0:T(8,128)S(1)}, f32[64,128]{1,0:T(8,128)S(1)}, u32[]{:S(2)}, u32[]{:S(2)}) collective-permute-start(f32[64,128]{1,0:T(8,128)S(1)} %pad_maximum_fusion.1), channel_id=1, source_target_pairs={{0,16},{4,20},{8,24},{12,28},{16,0},{20,4},{24,8},{28,12},{1,17},{... | collective-permute-start | bytes 98312 | tf_op jit(solution)/shard_map/ppermute | solution.py:651
  24.1 1.8 %collective-permute-start.1 = (f32[224,128]{1,0:T(8,128)S(1)}, f32[224,128]{1,0:T(8,128)S(1)}, u32[]{:S(2)}, u32[]{:S(2)}) collective-permute-start(f32[224,128]{1,0:T(8,128)S(1)} %get-tuple-element.28), channel_id=1, source_target_pairs={{0,1},{1,0},{2,3},{3,2},{4,5},{5,4},{6,7},{7,6},{8,9},{9,8},{10,11... | collective-permute-start | bytes 344072 | tf_op jit(solution)/shard_map/ppermute | solution.py:672
  25.9 3.0 %collective-permute-start.6 = (f32[224,128]{1,0:T(8,128)S(1)}, f32[224,128]{1,0:T(8,128)S(1)}, u32[]{:S(2)}, u32[]{:S(2)}) collective-permute-start(f32[224,128]{1,0:T(8,128)S(1)} %get-tuple-element.32), channel_id=1, source_target_pairs={{1,2},{2,1},{5,6},{6,5},{9,10},{10,9},{13,14},{14,13},{17,18},{18,... | collective-permute-start | bytes 344072 | tf_op jit(solution)/shard_map/ppermute | solution.py:674
  29.0 0.0 collective-permute-done.3.rest_2_
  29.0 1.4 %collective-permute-start.4 = (f32[128,128]{1,0:T(8,128)S(1)}, f32[128,128]{1,0:T(8,128)S(1)}, u32[]{:S(2)}, u32[]{:S(2)}) collective-permute-start(f32[128,128]{1,0:T(8,128)S(1)} %pad_maximum_fusion), channel_id=1, source_target_pairs={{0,8},{4,12},{8,0},{12,4},{16,24},{20,28},{24,16},{28,20},{1,9},{5... | collective-permute-start | bytes 196616 | tf_op jit(solution)/shard_map/ppermute | solution.py:651
  30.4 1.1 %local.1.ghosts = f32[4,224,512]{2,1,0:T(8,128)S(1)} custom-call(s32[8,512]{1,0:T(8,128)S(1)} %get-tuple-element.22.index, bf16[896,512]{1,0:T(8,128)(2,1)S(1)} %get-tuple-element.25.rows_hi, bf16[896,512]{1,0:T(8,128)(2,1)S(1)} %get-tuple-element.26.rows_lo), custom_call_target="tpu_custom_call" | custom-call | tf_op jit(solution)/shard_map/local/pallas_call | solution.py:676
  31.5 3.3 %shard_map.122.earlier = f32[5,4,128,128]{3,2,1,0:T(8,128)S(1)} custom-call(f32[9,4,128,128]{3,2,1,0:T(8,128)S(1)} %get-tuple-element.19.staged, s32[8,512]{1,0:T(8,128)S(1)} %get-tuple-element.22.index, f32[4,224,512]{2,1,0:T(8,128)S(1)} %local.1.ghosts, bf16[256,384]{1,0:T(8,128)(2,1)} %constant.8.clone.matrix_h, f32[5,125,512]{2,1,0:T(8,128)} %store_h.3), custom_call_target="tpu_custom_call" | custom-call | tf_op jit(solution)/shard_map/pallas_call | solution.py:708
  34.8 0.1 shard_map.123.part
  34.8 0.0 collective-permute-done.1.sp_a
  34.8 0.0 collective-permute-done.th_a
  34.8 1.2 %faces.1.part = f32[5,4,128,128]{3,2,1,0:T(8,128)S(1)} custom-call(s32[1,512]{1,0:T(1,128)S(1)} %get-tuple-element.21.slot_v, f32[9,4,128,128]{3,2,1,0:T(8,128)S(1)} %get-tuple-element.19.staged, s32[8,512]{1,0:T(8,128)S(1)} %get-tuple-element.22.index, f32[4,224,512]{2,1,0:T(8,128)S(1)} %local.1.ghosts, ...), custom_call_target="tpu_custom_call", output_to_operand_aliasing={{}: (7, {})} | custom-call | tf_op jit(solution)/shard_map/faces/pallas_call | solution.py:710
  36.1 0.0 collective-permute-done.4.rest_3_
  36.1 0.7 %interface.1 = (f32[5,4,128,128]{3,2,1,0:T(8,128)S(1)}, bf16[512,512]{1,0:T(8,128)(2,1)S(1)}) custom-call(s32[8,128]{1,0:T(8,128)S(1)} %get-tuple-element.20.plan, s32[1,512]{1,0:T(1,128)S(1)} %get-tuple-element.21.slot_v, s32[8,512]{1,0:T(8,128)S(1)} %get-tuple-element.22.index, ...), custom_call_target="tpu_custom_call", output_to_operand_aliasing={{0}: (5, {})} | custom-call | tf_op jit(solution)/shard_map/interface/pallas_call | solution.py:724
  36.9 0.0 collective-permute-done.6.sp_b
  36.9 0.5 %late.1.part = f32[5,4,128,128]{3,2,1,0:T(8,128)S(1)} custom-call(f32[9,4,128,128]{3,2,1,0:T(8,128)S(1)} %get-tuple-element.19.staged, s32[8,512]{1,0:T(8,128)S(1)} %get-tuple-element.22.index, f32[4,224,512]{2,1,0:T(8,128)S(1)} %local.1.ghosts, f32[224,128]{1,0:T(8,128)S(1)} %collective-permute-done.6.sp_b, ...), custom_call_target="tpu_custom_call", output_to_operand_aliasing={{}: (4, {})} | custom-call | tf_op jit(solution)/shard_map/late/pallas_call | solution.py:738
  37.3 0.0 collective-permute-done.5.th_b
  37.4 2.0 %last.1 = (f32[5,125,512]{2,1,0:T(8,128)}, f32[5,125,512]{2,1,0:T(8,128)}, f32[5,4,128,128]{3,2,1,0:T(8,128)S(1)}) custom-call(f32[9,4,128,128]{3,2,1,0:T(8,128)S(1)} %get-tuple-element.19.staged, bf16[512,512]{1,0:T(8,128)(2,1)S(1)} %get-tuple-element.30.picks, f32[176,512]{1,0:T(8,128)S(1)} %collective-permute-done.5.th_b, ...), custom_call_target="tpu_custom_call", output_to_operand_aliasing={{2}: (3, {})} | custom-call | tf_op jit(solution)/shard_map/last/pallas_call | solution.py:750
  (2 shorter events, 0.0 us)
Async XLA Ops:
  3.4 31.5 %collective-permute-start = (f32[176,512]{1,0:T(8,128)}, f32[176,512]{1,0:T(8,128)S(1)}, u32[]{:S(2)}, u32[]{:S(2)}) collective-permute-start(f32[176,512]{1,0:T(8,128)} %get-tuple-element.27), channel_id=1, source_target_pairs={{0,4},{4,0},{8,12},{12,8},{16,20},{20,16},{24,28},{28,24},{1,5},{5... | collective-permute-start | bytes 1081352 | tf_op jit(solution)/shard_map/ppermute | solution.py:648
  6.5 30.8 %collective-permute-start.5 = (f32[176,512]{1,0:T(8,128)}, f32[176,512]{1,0:T(8,128)S(1)}, u32[]{:S(2)}, u32[]{:S(2)}) collective-permute-start(f32[176,512]{1,0:T(8,128)} %get-tuple-element.31), channel_id=1, source_target_pairs={{0,28},{4,8},{8,4},{12,16},{16,12},{20,24},{24,20},{28,0},{1,29},{... | collective-permute-start | bytes 1081352 | tf_op jit(solution)/shard_map/ppermute | solution.py:671
  9.9 12.0 %collective-permute-start.2 = (f32[32,128]{1,0:T(8,128)S(1)}, f32[32,128]{1,0:T(8,128)S(1)}, u32[]{:S(2)}, u32[]{:S(2)}) collective-permute-start(f32[32,128]{1,0:T(8,128)S(1)} %get-tuple-element.29.rest_0_), channel_id=1, source_target_pairs={{0,4},{4,0},{8,12},{12,8},{16,20},{20,16},{24,28},{28,24},{1,5},{5... | collective-permute-start | bytes 49160 | tf_op jit(solution)/shard_map/ppermute | solution.py:651
  21.9 7.1 %collective-permute-start.3 = (f32[64,128]{1,0:T(8,128)S(1)}, f32[64,128]{1,0:T(8,128)S(1)}, u32[]{:S(2)}, u32[]{:S(2)}) collective-permute-start(f32[64,128]{1,0:T(8,128)S(1)} %pad_maximum_fusion.1), channel_id=1, source_target_pairs={{0,16},{4,20},{8,24},{12,28},{16,0},{20,4},{24,8},{28,12},{1,17},{... | collective-permute-start | bytes 98312 | tf_op jit(solution)/shard_map/ppermute | solution.py:651
  24.1 10.7 %collective-permute-start.1 = (f32[224,128]{1,0:T(8,128)S(1)}, f32[224,128]{1,0:T(8,128)S(1)}, u32[]{:S(2)}, u32[]{:S(2)}) collective-permute-start(f32[224,128]{1,0:T(8,128)S(1)} %get-tuple-element.28), channel_id=1, source_target_pairs={{0,1},{1,0},{2,3},{3,2},{4,5},{5,4},{6,7},{7,6},{8,9},{9,8},{10,11... | collective-permute-start | bytes 344072 | tf_op jit(solution)/shard_map/ppermute | solution.py:672
  25.9 10.9 %collective-permute-start.6 = (f32[224,128]{1,0:T(8,128)S(1)}, f32[224,128]{1,0:T(8,128)S(1)}, u32[]{:S(2)}, u32[]{:S(2)}) collective-permute-start(f32[224,128]{1,0:T(8,128)S(1)} %get-tuple-element.32), channel_id=1, source_target_pairs={{1,2},{2,1},{5,6},{6,5},{9,10},{10,9},{13,14},{14,13},{17,18},{18,... | collective-permute-start | bytes 344072 | tf_op jit(solution)/shard_map/ppermute | solution.py:674
  29.0 7.1 %collective-permute-start.4 = (f32[128,128]{1,0:T(8,128)S(1)}, f32[128,128]{1,0:T(8,128)S(1)}, u32[]{:S(2)}, u32[]{:S(2)}) collective-permute-start(f32[128,128]{1,0:T(8,128)S(1)} %pad_maximum_fusion), channel_id=1, source_target_pairs={{0,8},{4,12},{8,0},{12,4},{16,24},{20,28},{24,16},{28,20},{1,9},{5... | collective-permute-start | bytes 196616 | tf_op jit(solution)/shard_map/ppermute | solution.py:651

commit v4 on v3

--- a/solution.py
+++ b/solution.py
@@ -194,8 +194,8 @@
 
 def first_kernel(
     per_span, axial, sectors, slot_l, turn_l, offset_l, slot_h, fields, velocity, sound, turn_h, forward_h,
-    staged, th_a, iface, slot_v, plan, own_packed, forward_t, theta, turn_t, rows_hi, rows_lo, stack_hi, stack_lo, slot_s, turn_s, offset_s,
-    sems, small_sems, out_sem,
+    staged, theta, iface, slot_v, plan, own_packed, forward_t, turn_t, rows_hi, rows_lo, stack_hi, stack_lo, slot_s, turn_s, offset_s,
+    sems, small_sems,
 ):
     elems = slot_v.shape[1]
     tiles = elems // LANES
@@ -263,8 +263,6 @@
             for f in range(VALS):
                 at = n * rows + f * PAD
                 store_halves(rows_hi, rows_lo, at, cols, face_rows(staged, value_index(f, 2), t, 2, end))
-    out = pltpu.make_async_copy(theta, th_a, out_sem)
-    out.start()
     both = dot(rows_hi[...], one) + dot(rows_lo[...], one)
     both = jnp.where(lane < per_span, both[0:rows], jnp.where(lane < 2 * per_span, both[rows:], 0.0))
     packed = both[0:PAD]
@@ -274,15 +272,16 @@
     iface[...] = turned(packed, code, turn_t, stack_hi, stack_lo)
     for t in range(tiles):
         iface[PAD - tiles + t : PAD - tiles + t + 1, :] = slot_v[:, tile_cols(t)].astype(F32)
-    out.wait()
 
 
 LOCAL_FACES = ((1, 1), (1, 0), (2, 1), (2, 0))
 
 
 def second_kernel(
-    per_span, axial, slot_v, staged, th_b, sp_a, sp_b, index, rows_hi, rows_lo, theta, out_sem,
+    per_span, axial, slot_v, staged, matrix_h, theta, sp_a, sp_b, index, rows_hi, rows_lo, matrix, sem,
 ):
+    load = pltpu.make_async_copy(matrix_h, matrix, sem)
+    load.start()
     elems = slot_v.shape[1]
     tiles = elems // LANES
     half = axial // 2
@@ -302,8 +301,6 @@
             for f in range(VALS):
                 theta[f * FACE : (f + 1) * FACE, tile_cols(t)] = face_rows(staged, value_index(f, 0), t, 0, ORDER)
 
-    out = pltpu.make_async_copy(theta, th_b, out_sem)
-    out.start()
     for n, (d, end) in enumerate(LOCAL_FACES):
         for t in range(tiles):
             for f in range(VALS):
@@ -341,7 +338,7 @@
     ax_high = jnp.where(position == half - 1, elems + per_span + row, pltpu.roll(slots, elems - 1, 1))
     ax_high = jnp.where(position == axial - 1, none, ax_high)
     index[...] = neighbour_index([span_low, span_high, ax_low, ax_high], slot_v)
-    out.wait()
+    load.wait()
 
 
 def local_kernel(index, rows_hi, rows_lo, ghosts):
@@ -353,7 +350,7 @@
         ghosts[n] = dot(rows_hi[at, :], one) + dot(rows_lo[at, :], one)
 
 
-def work_kernel(place, per_span, staged, index, ghosts, matrix_h, store_h, earlier, out, store, sems, *scratch):
+def work_kernel(place, per_span, staged, index, ghosts, matrix, store_h, earlier, out, store, sems, *scratch):
     del earlier
 
     @pl.when(work_place() == place)
@@ -366,7 +363,7 @@
         ]
         for copy in stores:
             copy.start()
-        volume_terms(staged, matrix_h, out, *scratch)
+        volume_terms(staged, matrix, out, *scratch)
         for copy in stores:
             copy.wait()
         for t in range(tiles):
@@ -378,18 +375,16 @@
                 side_terms(staged, ghosts.at[n], out, 2, side, t, keep=keep)
 
 
-def work_start(place, per_span, staged, index, ghosts, matrix_h, store_h, out, *scratch):
-    work_kernel(place, per_span, staged, index, ghosts, matrix_h, store_h, None, out, *scratch)
+def work_start(place, per_span, staged, index, ghosts, matrix, store_h, out, *scratch):
+    work_kernel(place, per_span, staged, index, ghosts, matrix, store_h, None, out, *scratch)
 
 
 def work_place():
     return jnp.where(axis_parity("span") == 1, 0, 1)
 
 
-def volume_terms(staged, matrix_h, out, matrix, flux_hi, flux_lo, sem):
+def volume_terms(staged, matrix, out, flux_hi, flux_lo):
     tiles = staged.shape[1]
-    load = pltpu.make_async_copy(matrix_h, matrix, sem)
-    load.start()
     step = 16
     for pair in range(tiles // 2):
         for half in range(2):
@@ -415,8 +410,6 @@
                         hi, lo = halves(x)
                         flux_hi[pair, f, d * LANES + r : d * LANES + r + step, cols] = hi
                         flux_lo[pair, f, d * LANES + r : d * LANES + r + step, cols] = lo
-        if pair == 0:
-            load.wait()
         for f in range(5):
             a = dot(matrix[...], flux_hi[pair, f])
             b = dot(matrix[0:LANES, :], flux_lo[pair, f])
@@ -615,7 +608,7 @@
         functools.partial(first_kernel, per_span, axial, sectors),
         out_shape=(
             vmem((9, tiles, LANES, LANES), F32),
-            hbm((theta_rows, elems), F32),
+            vmem((theta_rows, elems), F32),
             vmem((PAD, LANES), F32),
             vmem((1, elems), jnp.int32),
             vmem((8, LANES), jnp.int32),
@@ -623,9 +616,8 @@
             vmem((PAD, 8 * PAD), BF),
         ),
         in_specs=[hbm_spec()] * 9,
-        out_specs=(vmem_spec(), hbm_spec()) + (vmem_spec(),) * 5,
+        out_specs=(vmem_spec(),) * 7,
         scratch_shapes=[
-            vmem((theta_rows, elems), F32),
             vmem((PAD, 8 * PAD), BF),
             vmem((2 * rows, elems), BF),
             vmem((2 * rows, elems), BF),
@@ -635,7 +627,6 @@
             pltpu.SMEM((per_span,), jnp.int32),
             dma((tiles, 3)),
             dma((6,)),
-            dma(()),
         ],
         compiler_params=params(),
         name="first",
@@ -651,22 +642,23 @@
         pieces.append(lax.ppermute(block, "blk", [(i, i ^ reach) for i in range(sectors)]))
         far += [k ^ reach for k in far]
 
-    th_b, sp_a, sp_b, index, rows_hi, rows_lo = pl.pallas_call(
+    th_b, sp_a, sp_b, index, rows_hi, rows_lo, matrix = pl.pallas_call(
         functools.partial(second_kernel, per_span, axial),
         out_shape=(
-            hbm((theta_rows, elems), F32),
+            vmem((theta_rows, elems), F32),
             vmem((rows, LANES), F32),
             vmem((rows, LANES), F32),
             vmem((8, elems), jnp.int32),
             vmem((len(LOCAL_FACES) * rows, elems), BF),
             vmem((len(LOCAL_FACES) * rows, elems), BF),
+            vmem((2 * LANES, 3 * LANES), BF),
         ),
-        in_specs=[vmem_spec()] * 2,
-        out_specs=(hbm_spec(),) + (vmem_spec(),) * 5,
-        scratch_shapes=[vmem((theta_rows, elems), F32), dma(())],
+        in_specs=[vmem_spec()] * 2 + [hbm_spec()],
+        out_specs=(vmem_spec(),) * 7,
+        scratch_shapes=[dma(())],
         compiler_params=params(),
         name="second",
-    )(in_vmem(slot_v), in_vmem(staged))
+    )(in_vmem(slot_v), in_vmem(staged), in_hbm(jnp.asarray(volume_matrix())))
     pairs = [(i, (i + 1 if i % 2 else i - 1) % sectors) for i in range(sectors)]
     near_b = lax.ppermute(th_b, "blk", pairs)
     span_a = lax.ppermute(sp_a, "span", [(i, i ^ 1) for i in range(slabs) if i ^ 1 < slabs])
@@ -688,21 +680,19 @@
         work = pl.pallas_call(
             functools.partial(work_kernel if place else work_start, place, per_span),
             out_shape=vmem(block, F32),
-            in_specs=[vmem_spec()] * 3 + [hbm_spec()] * 2 + [vmem_spec()] * (place > 0),
+            in_specs=[vmem_spec()] * 4 + [hbm_spec()] + [vmem_spec()] * (place > 0),
             out_specs=vmem_spec(),
             scratch_shapes=[
                 vmem(block, F32),
                 dma((tiles,)),
-                vmem((2 * LANES, 3 * LANES), BF),
                 vmem((tiles // 2, 5, 3 * LANES, 2 * LANES), BF),
                 vmem((tiles // 2, 5, 3 * LANES, 2 * LANES), BF),
-                dma(()),
             ],
             input_output_aliases={5: 0} if place else {},
             compiler_params=params(),
         )
         operands = [in_vmem(staged), in_vmem(index), in_vmem(ghosts)]
-        operands += [in_hbm(jnp.asarray(volume_matrix())), in_hbm(section_store)]
+        operands += [in_vmem(matrix), in_hbm(section_store)]
         if place:
             operands.append(in_vmem(part))
         part = work(*operands)

time: 39.6 us -> 38.2 us (0.965)
  Pallas kernels: 12.6 us -> 11.4 us
    pallas_call x2, Pallas kernels: 3.32 us -> 2.2 us  [on_device(): part = work(*operands)]
  transfers between devices with their start and end apart: 7 -> 7, of which waited for: 1 -> 1; matrix products, arithmetic and copies ran while one was open for 0% -> 0% of each run, Pallas kernels for 20% -> 18%
where the time goes in v4:
time: 38.2 us; the launch traced here: 37.9 us
  starting transfers between devices  13.9 us (36%)
  waiting for transfers between devices  11.8 us (31%)
  Pallas kernels  11.4 us (30%)
  between operations  0.76 us (2%)
    ppermute x3, waiting for transfers between devices, on_device(): lax.ppermute(block, 'blk', [(i, i ^ reach) for i in range(sectors)])  11.8 us
    ppermute x3, starting transfers between devices, on_device(): lax.ppermute(block, 'blk', [(i, i ^ reach) for i in range(sectors)])  3.64 us
    ppermute x1, starting transfers between devices, on_device(): near_b = lax.ppermute(th_b, 'blk', pairs)  3.35 us
    ppermute x1, starting transfers between devices, on_device(): lax.ppermute(sp_b, 'span', [(i, j) for i, j in pairs if 0 <= j < slabs])  3.02 us
    pallas_call x1, Pallas kernels, on_device(): pl.pallas_call(functools.partial(first_kernel, per_span, axial, sectors),...  2.65 us
    pallas_call x2, Pallas kernels, on_device(): part = work(*operands)  2.2 us
    ppermute x1, starting transfers between devices, on_device(): near_a = lax.ppermute(th_a, 'blk', [(i, i ^ 1) for i in range(sectors)])  2.1 us
    pallas_call x1, Pallas kernels, on_device(): pl.pallas_call(last_kernel, out_shape=(whole, whole, vmem(block, F32)), i...  1.99 us
  transfers between devices with their start and end apart: 7, of which 1 were waited for; matrix products, arithmetic and copies ran while one was open for 0% of the time, Pallas kernels for 18%

profile of v4, /device:TPU:1, one launch (start us, length us, event | category | flops | bytes accessed | tf_op | source)
XLA Modules:
  0.0 37.9 jit_solution(12816278194927375597)
XLA Ops:
  0.6 2.6 %first.1 = (f32[9,4,128,128]{3,2,1,0:T(8,128)S(1)}, f32[176,512]{1,0:T(8,128)S(1)}, f32[32,128]{1,0:T(8,128)S(1)}, s32[1,512]{1,0:T(1,128)S(1)}, s32[8,128]{1,0:...) custom-call(s32[512]{0:T(512)} %slot_l.1, s32[1,4]{1,0:T(1,128)} %turn_l.1, s32[4]{0:T(128)} %offset_l.1, ...), custom_call_target="tpu_custom_call" | custom-call | tf_op jit(solution)/shard_map/first/pallas_call | solution.py:607
  3.3 2.1 %collective-permute-start = (f32[176,512]{1,0:T(8,128)S(1)}, f32[176,512]{1,0:T(8,128)S(1)}, u32[]{:S(2)}, u32[]{:S(2)}) collective-permute-start(f32[176,512]{1,0:T(8,128)S(1)} %get-tuple-element.28), channel_id=1, source_target_pairs={{0,4},{4,0},{8,12},{12,8},{16,20},{20,16},{24,28},{28,24},{1,5},{5... | collective-permute-start | bytes 1081352 | tf_op jit(solution)/shard_map/ppermute | solution.py:639
  5.4 1.0 %second.1 = (f32[176,512]{1,0:T(8,128)S(1)}, f32[224,128]{1,0:T(8,128)S(1)}, f32[224,128]{1,0:T(8,128)S(1)}, s32[8,512]{1,0:T(8,128)S(1)}, bf16[896,512]{1,0:T(8...) custom-call(s32[1,512]{1,0:T(1,128)S(1)} %get-tuple-element.22.slot_v, ...), custom_call_target="tpu_custom_call" | custom-call | tf_op jit(solution)/shard_map/second/pallas_call | solution.py:645
  6.4 3.4 %collective-permute-start.5 = (f32[176,512]{1,0:T(8,128)S(1)}, f32[176,512]{1,0:T(8,128)S(1)}, u32[]{:S(2)}, u32[]{:S(2)}) collective-permute-start(f32[176,512]{1,0:T(8,128)S(1)} %get-tuple-element.33), channel_id=1, source_target_pairs={{0,28},{4,8},{8,4},{12,16},{16,12},{20,24},{24,20},{28,0},{1,29},{... | collective-permute-start | bytes 1081352 | tf_op jit(solution)/shard_map/ppermute | solution.py:663
  9.8 0.0 collective-permute-start.2
  9.8 11.8 %collective-permute-done.2.iface_a.rest_1_ = f32[32,128]{1,0:T(8,128)S(1)} collective-permute-done((f32[32,128]{1,0:T(8,128)S(1)}, f32[32,128]{1,0:T(8,128)S(1)}, u32[]{:S(2)}, u32[]{:S(2)}) %collective-permute-start.2) | collective-permute-done | bytes 16416 | tf_op jit(solution)/shard_map/ppermute | solution.py:642
  21.6 2.3 %collective-permute-start.3 = (f32[64,128]{1,0:T(8,128)S(1)}, f32[64,128]{1,0:T(8,128)S(1)}, u32[]{:S(2)}, u32[]{:S(2)}) collective-permute-start(f32[64,128]{1,0:T(8,128)S(1)} %pad_maximum_fusion.1), channel_id=1, source_target_pairs={{0,16},{4,20},{8,24},{12,28},{16,0},{20,4},{24,8},{28,12},{1,17},{... | collective-permute-start | bytes 98312 | tf_op jit(solution)/shard_map/ppermute | solution.py:642
  23.9 1.8 %collective-permute-start.1 = (f32[224,128]{1,0:T(8,128)S(1)}, f32[224,128]{1,0:T(8,128)S(1)}, u32[]{:S(2)}, u32[]{:S(2)}) collective-permute-start(f32[224,128]{1,0:T(8,128)S(1)} %get-tuple-element.29), channel_id=1, source_target_pairs={{0,1},{1,0},{2,3},{3,2},{4,5},{5,4},{6,7},{7,6},{8,9},{9,8},{10,11... | collective-permute-start | bytes 344072 | tf_op jit(solution)/shard_map/ppermute | solution.py:664
  25.7 3.0 %collective-permute-start.6 = (f32[224,128]{1,0:T(8,128)S(1)}, f32[224,128]{1,0:T(8,128)S(1)}, u32[]{:S(2)}, u32[]{:S(2)}) collective-permute-start(f32[224,128]{1,0:T(8,128)S(1)} %get-tuple-element.34), channel_id=1, source_target_pairs={{1,2},{2,1},{5,6},{6,5},{9,10},{10,9},{13,14},{14,13},{17,18},{18,... | collective-permute-start | bytes 344072 | tf_op jit(solution)/shard_map/ppermute | solution.py:666
  28.7 0.0 collective-permute-done.3.rest_2_
  28.7 1.4 %collective-permute-start.4 = (f32[128,128]{1,0:T(8,128)S(1)}, f32[128,128]{1,0:T(8,128)S(1)}, u32[]{:S(2)}, u32[]{:S(2)}) collective-permute-start(f32[128,128]{1,0:T(8,128)S(1)} %pad_maximum_fusion), channel_id=1, source_target_pairs={{0,8},{4,12},{8,0},{12,4},{16,24},{20,28},{24,16},{28,20},{1,9},{5... | collective-permute-start | bytes 196616 | tf_op jit(solution)/shard_map/ppermute | solution.py:642
  30.1 1.1 %local.1.ghosts = f32[4,224,512]{2,1,0:T(8,128)S(1)} custom-call(s32[8,512]{1,0:T(8,128)S(1)} %get-tuple-element.23.index, bf16[896,512]{1,0:T(8,128)(2,1)S(1)} %get-tuple-element.26.rows_hi, bf16[896,512]{1,0:T(8,128)(2,1)S(1)} %get-tuple-element.27.rows_lo), custom_call_target="tpu_custom_call" | custom-call | tf_op jit(solution)/shard_map/local/pallas_call | solution.py:668
  31.2 2.1 %shard_map.113.earlier = f32[5,4,128,128]{3,2,1,0:T(8,128)S(1)} custom-call(f32[9,4,128,128]{3,2,1,0:T(8,128)S(1)} %get-tuple-element.20.staged, s32[8,512]{1,0:T(8,128)S(1)} %get-tuple-element.23.index, f32[4,224,512]{2,1,0:T(8,128)S(1)} %local.1.ghosts, bf16[256,384]{1,0:T(8,128)(2,1)S(1)} %get-tuple-element.31.matrix, f32[5,125,512]{2,1,0:T(8,128)} %store_h.3), custom_call_target="tpu_custom_call" | custom-call | tf_op jit(solution)/shard_map/pallas_call | solution.py:698
  33.4 0.1 shard_map.114.part
  33.4 0.0 collective-permute-done.1.sp_a
  33.4 0.0 collective-permute-done.th_a
  33.4 1.2 %faces.1.part = f32[5,4,128,128]{3,2,1,0:T(8,128)S(1)} custom-call(s32[1,512]{1,0:T(1,128)S(1)} %get-tuple-element.22.slot_v, f32[9,4,128,128]{3,2,1,0:T(8,128)S(1)} %get-tuple-element.20.staged, s32[8,512]{1,0:T(8,128)S(1)} %get-tuple-element.23.index, f32[4,224,512]{2,1,0:T(8,128)S(1)} %local.1.ghosts, ...), custom_call_target="tpu_custom_call", output_to_operand_aliasing={{}: (7, {})} | custom-call | tf_op jit(solution)/shard_map/faces/pallas_call | solution.py:700
  34.7 0.0 collective-permute-done.4.rest_3_
  34.7 0.7 %interface.1 = (f32[5,4,128,128]{3,2,1,0:T(8,128)S(1)}, bf16[512,512]{1,0:T(8,128)(2,1)S(1)}) custom-call(s32[8,128]{1,0:T(8,128)S(1)} %get-tuple-element.21.plan, s32[1,512]{1,0:T(1,128)S(1)} %get-tuple-element.22.slot_v, s32[8,512]{1,0:T(8,128)S(1)} %get-tuple-element.23.index, ...), custom_call_target="tpu_custom_call", output_to_operand_aliasing={{0}: (5, {})} | custom-call | tf_op jit(solution)/shard_map/interface/pallas_call | solution.py:714
  35.5 0.0 collective-permute-done.6.sp_b
  35.5 0.5 %late.1.part = f32[5,4,128,128]{3,2,1,0:T(8,128)S(1)} custom-call(f32[9,4,128,128]{3,2,1,0:T(8,128)S(1)} %get-tuple-element.20.staged, s32[8,512]{1,0:T(8,128)S(1)} %get-tuple-element.23.index, f32[4,224,512]{2,1,0:T(8,128)S(1)} %local.1.ghosts, f32[224,128]{1,0:T(8,128)S(1)} %collective-permute-done.6.sp_b, ...), custom_call_target="tpu_custom_call", output_to_operand_aliasing={{}: (4, {})} | custom-call | tf_op jit(solution)/shard_map/late/pallas_call | solution.py:728
  36.0 0.0 collective-permute-done.5.th_b
  36.0 2.0 %last.1 = (f32[5,125,512]{2,1,0:T(8,128)}, f32[5,125,512]{2,1,0:T(8,128)}, f32[5,4,128,128]{3,2,1,0:T(8,128)S(1)}) custom-call(f32[9,4,128,128]{3,2,1,0:T(8,128)S(1)} %get-tuple-element.20.staged, bf16[512,512]{1,0:T(8,128)(2,1)S(1)} %get-tuple-element.32.picks, f32[176,512]{1,0:T(8,128)S(1)} %collective-permute-done.5.th_b, ...), custom_call_target="tpu_custom_call", output_to_operand_aliasing={{2}: (3, {})} | custom-call | tf_op jit(solution)/shard_map/last/pallas_call | solution.py:740
  (2 shorter events, 0.0 us)
Async XLA Ops:
  3.3 30.2 %collective-permute-start = (f32[176,512]{1,0:T(8,128)S(1)}, f32[176,512]{1,0:T(8,128)S(1)}, u32[]{:S(2)}, u32[]{:S(2)}) collective-permute-start(f32[176,512]{1,0:T(8,128)S(1)} %get-tuple-element.28), channel_id=1, source_target_pairs={{0,4},{4,0},{8,12},{12,8},{16,20},{20,16},{24,28},{28,24},{1,5},{5... | collective-permute-start | bytes 1081352 | tf_op jit(solution)/shard_map/ppermute | solution.py:639
  6.4 29.5 %collective-permute-start.5 = (f32[176,512]{1,0:T(8,128)S(1)}, f32[176,512]{1,0:T(8,128)S(1)}, u32[]{:S(2)}, u32[]{:S(2)}) collective-permute-start(f32[176,512]{1,0:T(8,128)S(1)} %get-tuple-element.33), channel_id=1, source_target_pairs={{0,28},{4,8},{8,4},{12,16},{16,12},{20,24},{24,20},{28,0},{1,29},{... | collective-permute-start | bytes 1081352 | tf_op jit(solution)/shard_map/ppermute | solution.py:663
  9.8 11.8 %collective-permute-start.2 = (f32[32,128]{1,0:T(8,128)S(1)}, f32[32,128]{1,0:T(8,128)S(1)}, u32[]{:S(2)}, u32[]{:S(2)}) collective-permute-start(f32[32,128]{1,0:T(8,128)S(1)} %get-tuple-element.30.rest_0_), channel_id=1, source_target_pairs={{0,4},{4,0},{8,12},{12,8},{16,20},{20,16},{24,28},{28,24},{1,5},{5... | collective-permute-start | bytes 49160 | tf_op jit(solution)/shard_map/ppermute | solution.py:642
  21.6 7.1 %collective-permute-start.3 = (f32[64,128]{1,0:T(8,128)S(1)}, f32[64,128]{1,0:T(8,128)S(1)}, u32[]{:S(2)}, u32[]{:S(2)}) collective-permute-start(f32[64,128]{1,0:T(8,128)S(1)} %pad_maximum_fusion.1), channel_id=1, source_target_pairs={{0,16},{4,20},{8,24},{12,28},{16,0},{20,4},{24,8},{28,12},{1,17},{... | collective-permute-start | bytes 98312 | tf_op jit(solution)/shard_map/ppermute | solution.py:642
  23.9 9.6 %collective-permute-start.1 = (f32[224,128]{1,0:T(8,128)S(1)}, f32[224,128]{1,0:T(8,128)S(1)}, u32[]{:S(2)}, u32[]{:S(2)}) collective-permute-start(f32[224,128]{1,0:T(8,128)S(1)} %get-tuple-element.29), channel_id=1, source_target_pairs={{0,1},{1,0},{2,3},{3,2},{4,5},{5,4},{6,7},{7,6},{8,9},{9,8},{10,11... | collective-permute-start | bytes 344072 | tf_op jit(solution)/shard_map/ppermute | solution.py:664
  25.7 9.8 %collective-permute-start.6 = (f32[224,128]{1,0:T(8,128)S(1)}, f32[224,128]{1,0:T(8,128)S(1)}, u32[]{:S(2)}, u32[]{:S(2)}) collective-permute-start(f32[224,128]{1,0:T(8,128)S(1)} %get-tuple-element.34), channel_id=1, source_target_pairs={{1,2},{2,1},{5,6},{6,5},{9,10},{10,9},{13,14},{14,13},{17,18},{18,... | collective-permute-start | bytes 344072 | tf_op jit(solution)/shard_map/ppermute | solution.py:666
  28.7 6.0 %collective-permute-start.4 = (f32[128,128]{1,0:T(8,128)S(1)}, f32[128,128]{1,0:T(8,128)S(1)}, u32[]{:S(2)}, u32[]{:S(2)}) collective-permute-start(f32[128,128]{1,0:T(8,128)S(1)} %pad_maximum_fusion), channel_id=1, source_target_pairs={{0,8},{4,12},{8,0},{12,4},{16,24},{20,28},{24,16},{28,20},{1,9},{5... | collective-permute-start | bytes 196616 | tf_op jit(solution)/shard_map/ppermute | solution.py:642

commit v5 on v4

--- a/solution.py
+++ b/solution.py
@@ -535,13 +535,32 @@
     span_side(1, staged, index, ghosts, sp_b, acc, whole, jnp.logical_or(slab == 0, slab == slabs - 1))
 
 
+HIGH_ROW = (ORDER * FACE) // PAD * PAD
+LOWER, MIDDLE, UPPER = slice(0, PAD), slice(PAD, HIGH_ROW), slice(HIGH_ROW, VOL)
+
+
 def last_kernel(staged, picks, th_b, part, fields_out, store_out, acc, fresh, ghost, sems):
     del part
     tiles = staged.shape[1]
     odd = axis_parity("blk")
+    copies = []
+
+    def send(n, t, rows):
+        for f in range(5):
+            fresh[f, t, rows, :] = staged[f, t, rows, :] + section_gain * acc[f, t, rows, :]
+        cols = pl.ds(t * LANES, LANES)
+        pair = [
+            pltpu.make_async_copy(acc.at[:, t, rows, :], store_out.at[:, rows, cols], sems.at[n, t, 0]),
+            pltpu.make_async_copy(fresh.at[:, t, rows, :], fields_out.at[:, rows, cols], sems.at[n, t, 1]),
+        ]
+        for copy in pair:
+            copy.start()
+        copies.extend(pair)
+
+    for t in range(tiles):
+        send(0, t, MIDDLE)
     hi, lo = halves(th_b[...])
     ghost[...] = dot(hi, picks[...]) + dot(lo, picks[...])
-    copies = []
     for t in range(tiles):
         @pl.when(odd == 0)
         def _():
@@ -551,16 +570,8 @@
         def _():
             theta_side(staged, ghost, acc, 1, t)
 
-        for f in range(5):
-            fresh[f, t, 0:VOL, :] = staged[f, t, 0:VOL, :] + section_gain * acc[f, t, 0:VOL, :]
-        cols = pl.ds(t * LANES, LANES)
-        pair = [
-            pltpu.make_async_copy(acc.at[:, t, 0:VOL, :], store_out.at[:, :, cols], sems.at[t, 0]),
-            pltpu.make_async_copy(fresh.at[:, t, 0:VOL, :], fields_out.at[:, :, cols], sems.at[t, 1]),
-        ]
-        for copy in pair:
-            copy.start()
-        copies += pair
+        send(1, t, LOWER)
+        send(2, t, UPPER)
     for copy in copies:
         copy.wait()
 
@@ -742,7 +753,7 @@
         out_shape=(whole, whole, vmem(block, F32)),
         in_specs=[vmem_spec()] * 4,
         out_specs=(hbm_spec(),) * 2 + (vmem_spec(),),
-        scratch_shapes=[vmem(block, F32), vmem((theta_rows, elems), F32), dma((tiles, 2))],
+        scratch_shapes=[vmem(block, F32), vmem((theta_rows, elems), F32), dma((3, tiles, 2))],
         input_output_aliases={3: 2},
         compiler_params=params(),
         name="last",

time: 38.2 us -> 38 us (level)
  no operation moved by 1% of the time
where the time goes in v5:
time: 38 us; the launch traced here: 37.7 us
  starting transfers between devices  13.9 us (37%)
  waiting for transfers between devices  11.8 us (31%)
  Pallas kernels  11.2 us (29%)
  between operations  0.76 us (2%)
    ppermute x3, waiting for transfers between devices, on_device(): lax.ppermute(block, 'blk', [(i, i ^ reach) for i in range(sectors)])  11.8 us
    ppermute x3, starting transfers between devices, on_device(): lax.ppermute(block, 'blk', [(i, i ^ reach) for i in range(sectors)])  3.64 us
    ppermute x1, starting transfers between devices, on_device(): near_b = lax.ppermute(th_b, 'blk', pairs)  3.35 us
    ppermute x1, starting transfers between devices, on_device(): lax.ppermute(sp_b, 'span', [(i, j) for i, j in pairs if 0 <= j < slabs])  3.02 us
    pallas_call x1, Pallas kernels, on_device(): pl.pallas_call(functools.partial(first_kernel, per_span, axial, sectors),...  2.65 us
    pallas_call x2, Pallas kernels, on_device(): part = work(*operands)  2.2 us
    ppermute x1, starting transfers between devices, on_device(): near_a = lax.ppermute(th_a, 'blk', [(i, i ^ 1) for i in range(sectors)])  2.1 us
    ppermute x1, starting transfers between devices, on_device(): lax.ppermute(sp_a, 'span', [(i, i ^ 1) for i in range(slabs) if i ^ 1 < s...  1.81 us
  transfers between devices with their start and end apart: 7, of which 1 were waited for; matrix products, arithmetic and copies ran while one was open for 0% of the time, Pallas kernels for 18%

profile of v5, /device:TPU:1, one launch (start us, length us, event | category | flops | bytes accessed | tf_op | source)
XLA Modules:
  0.0 37.7 jit_solution(11093156180893165948)
XLA Ops:
  0.6 2.6 %first.1 = (f32[9,4,128,128]{3,2,1,0:T(8,128)S(1)}, f32[176,512]{1,0:T(8,128)S(1)}, f32[32,128]{1,0:T(8,128)S(1)}, s32[1,512]{1,0:T(1,128)S(1)}, s32[8,128]{1,0:...) custom-call(s32[512]{0:T(512)} %slot_l.1, s32[1,4]{1,0:T(1,128)} %turn_l.1, s32[4]{0:T(128)} %offset_l.1, ...), custom_call_target="tpu_custom_call" | custom-call | tf_op jit(solution)/shard_map/first/pallas_call | solution.py:618
  3.3 2.1 %collective-permute-start = (f32[176,512]{1,0:T(8,128)S(1)}, f32[176,512]{1,0:T(8,128)S(1)}, u32[]{:S(2)}, u32[]{:S(2)}) collective-permute-start(f32[176,512]{1,0:T(8,128)S(1)} %get-tuple-element.28), channel_id=1, source_target_pairs={{0,4},{4,0},{8,12},{12,8},{16,20},{20,16},{24,28},{28,24},{1,5},{5... | collective-permute-start | bytes 1081352 | tf_op jit(solution)/shard_map/ppermute | solution.py:650
  5.4 1.0 %second.1 = (f32[176,512]{1,0:T(8,128)S(1)}, f32[224,128]{1,0:T(8,128)S(1)}, f32[224,128]{1,0:T(8,128)S(1)}, s32[8,512]{1,0:T(8,128)S(1)}, bf16[896,512]{1,0:T(8...) custom-call(s32[1,512]{1,0:T(1,128)S(1)} %get-tuple-element.22.slot_v, ...), custom_call_target="tpu_custom_call" | custom-call | tf_op jit(solution)/shard_map/second/pallas_call | solution.py:656
  6.4 3.4 %collective-permute-start.5 = (f32[176,512]{1,0:T(8,128)S(1)}, f32[176,512]{1,0:T(8,128)S(1)}, u32[]{:S(2)}, u32[]{:S(2)}) collective-permute-start(f32[176,512]{1,0:T(8,128)S(1)} %get-tuple-element.33), channel_id=1, source_target_pairs={{0,28},{4,8},{8,4},{12,16},{16,12},{20,24},{24,20},{28,0},{1,29},{... | collective-permute-start | bytes 1081352 | tf_op jit(solution)/shard_map/ppermute | solution.py:674
  9.8 0.0 collective-permute-start.2
  9.8 11.8 %collective-permute-done.2.iface_a.rest_1_ = f32[32,128]{1,0:T(8,128)S(1)} collective-permute-done((f32[32,128]{1,0:T(8,128)S(1)}, f32[32,128]{1,0:T(8,128)S(1)}, u32[]{:S(2)}, u32[]{:S(2)}) %collective-permute-start.2) | collective-permute-done | bytes 16416 | tf_op jit(solution)/shard_map/ppermute | solution.py:653
  21.6 2.3 %collective-permute-start.3 = (f32[64,128]{1,0:T(8,128)S(1)}, f32[64,128]{1,0:T(8,128)S(1)}, u32[]{:S(2)}, u32[]{:S(2)}) collective-permute-start(f32[64,128]{1,0:T(8,128)S(1)} %pad_maximum_fusion.1), channel_id=1, source_target_pairs={{0,16},{4,20},{8,24},{12,28},{16,0},{20,4},{24,8},{28,12},{1,17},{... | collective-permute-start | bytes 98312 | tf_op jit(solution)/shard_map/ppermute | solution.py:653
  23.9 1.8 %collective-permute-start.1 = (f32[224,128]{1,0:T(8,128)S(1)}, f32[224,128]{1,0:T(8,128)S(1)}, u32[]{:S(2)}, u32[]{:S(2)}) collective-permute-start(f32[224,128]{1,0:T(8,128)S(1)} %get-tuple-element.29), channel_id=1, source_target_pairs={{0,1},{1,0},{2,3},{3,2},{4,5},{5,4},{6,7},{7,6},{8,9},{9,8},{10,11... | collective-permute-start | bytes 344072 | tf_op jit(solution)/shard_map/ppermute | solution.py:675
  25.7 3.0 %collective-permute-start.6 = (f32[224,128]{1,0:T(8,128)S(1)}, f32[224,128]{1,0:T(8,128)S(1)}, u32[]{:S(2)}, u32[]{:S(2)}) collective-permute-start(f32[224,128]{1,0:T(8,128)S(1)} %get-tuple-element.34), channel_id=1, source_target_pairs={{1,2},{2,1},{5,6},{6,5},{9,10},{10,9},{13,14},{14,13},{17,18},{18,... | collective-permute-start | bytes 344072 | tf_op jit(solution)/shard_map/ppermute | solution.py:677
  28.7 0.0 collective-permute-done.3.rest_2_
  28.7 1.4 %collective-permute-start.4 = (f32[128,128]{1,0:T(8,128)S(1)}, f32[128,128]{1,0:T(8,128)S(1)}, u32[]{:S(2)}, u32[]{:S(2)}) collective-permute-start(f32[128,128]{1,0:T(8,128)S(1)} %pad_maximum_fusion), channel_id=1, source_target_pairs={{0,8},{4,12},{8,0},{12,4},{16,24},{20,28},{24,16},{28,20},{1,9},{5... | collective-permute-start | bytes 196616 | tf_op jit(solution)/shard_map/ppermute | solution.py:653
  30.1 1.1 %local.1.ghosts = f32[4,224,512]{2,1,0:T(8,128)S(1)} custom-call(s32[8,512]{1,0:T(8,128)S(1)} %get-tuple-element.23.index, bf16[896,512]{1,0:T(8,128)(2,1)S(1)} %get-tuple-element.26.rows_hi, bf16[896,512]{1,0:T(8,128)(2,1)S(1)} %get-tuple-element.27.rows_lo), custom_call_target="tpu_custom_call" | custom-call | tf_op jit(solution)/shard_map/local/pallas_call | solution.py:679
  31.2 2.1 %shard_map.113.earlier = f32[5,4,128,128]{3,2,1,0:T(8,128)S(1)} custom-call(f32[9,4,128,128]{3,2,1,0:T(8,128)S(1)} %get-tuple-element.20.staged, s32[8,512]{1,0:T(8,128)S(1)} %get-tuple-element.23.index, f32[4,224,512]{2,1,0:T(8,128)S(1)} %local.1.ghosts, bf16[256,384]{1,0:T(8,128)(2,1)S(1)} %get-tuple-element.31.matrix, f32[5,125,512]{2,1,0:T(8,128)} %store_h.3), custom_call_target="tpu_custom_call" | custom-call | tf_op jit(solution)/shard_map/pallas_call | solution.py:709
  33.4 0.1 shard_map.114.part
  33.4 0.0 collective-permute-done.1.sp_a
  33.4 0.0 collective-permute-done.th_a
  33.4 1.2 %faces.1.part = f32[5,4,128,128]{3,2,1,0:T(8,128)S(1)} custom-call(s32[1,512]{1,0:T(1,128)S(1)} %get-tuple-element.22.slot_v, f32[9,4,128,128]{3,2,1,0:T(8,128)S(1)} %get-tuple-element.20.staged, s32[8,512]{1,0:T(8,128)S(1)} %get-tuple-element.23.index, f32[4,224,512]{2,1,0:T(8,128)S(1)} %local.1.ghosts, ...), custom_call_target="tpu_custom_call", output_to_operand_aliasing={{}: (7, {})} | custom-call | tf_op jit(solution)/shard_map/faces/pallas_call | solution.py:711
  34.7 0.0 collective-permute-done.4.rest_3_
  34.7 0.7 %interface.1 = (f32[5,4,128,128]{3,2,1,0:T(8,128)S(1)}, bf16[512,512]{1,0:T(8,128)(2,1)S(1)}) custom-call(s32[8,128]{1,0:T(8,128)S(1)} %get-tuple-element.21.plan, s32[1,512]{1,0:T(1,128)S(1)} %get-tuple-element.22.slot_v, s32[8,512]{1,0:T(8,128)S(1)} %get-tuple-element.23.index, ...), custom_call_target="tpu_custom_call", output_to_operand_aliasing={{0}: (5, {})} | custom-call | tf_op jit(solution)/shard_map/interface/pallas_call | solution.py:725
  35.5 0.0 collective-permute-done.6.sp_b
  35.5 0.5 %late.1.part = f32[5,4,128,128]{3,2,1,0:T(8,128)S(1)} custom-call(f32[9,4,128,128]{3,2,1,0:T(8,128)S(1)} %get-tuple-element.20.staged, s32[8,512]{1,0:T(8,128)S(1)} %get-tuple-element.23.index, f32[4,224,512]{2,1,0:T(8,128)S(1)} %local.1.ghosts, f32[224,128]{1,0:T(8,128)S(1)} %collective-permute-done.6.sp_b, ...), custom_call_target="tpu_custom_call", output_to_operand_aliasing={{}: (4, {})} | custom-call | tf_op jit(solution)/shard_map/late/pallas_call | solution.py:739
  36.0 0.0 collective-permute-done.5.th_b
  36.0 1.8 %last.1 = (f32[5,125,512]{2,1,0:T(8,128)}, f32[5,125,512]{2,1,0:T(8,128)}, f32[5,4,128,128]{3,2,1,0:T(8,128)S(1)}) custom-call(f32[9,4,128,128]{3,2,1,0:T(8,128)S(1)} %get-tuple-element.20.staged, bf16[512,512]{1,0:T(8,128)(2,1)S(1)} %get-tuple-element.32.picks, f32[176,512]{1,0:T(8,128)S(1)} %collective-permute-done.5.th_b, ...), custom_call_target="tpu_custom_call", output_to_operand_aliasing={{2}: (3, {})} | custom-call | tf_op jit(solution)/shard_map/last/pallas_call | solution.py:751
  (2 shorter events, 0.0 us)
Async XLA Ops:
  3.3 30.2 %collective-permute-start = (f32[176,512]{1,0:T(8,128)S(1)}, f32[176,512]{1,0:T(8,128)S(1)}, u32[]{:S(2)}, u32[]{:S(2)}) collective-permute-start(f32[176,512]{1,0:T(8,128)S(1)} %get-tuple-element.28), channel_id=1, source_target_pairs={{0,4},{4,0},{8,12},{12,8},{16,20},{20,16},{24,28},{28,24},{1,5},{5... | collective-permute-start | bytes 1081352 | tf_op jit(solution)/shard_map/ppermute | solution.py:650
  6.4 29.5 %collective-permute-start.5 = (f32[176,512]{1,0:T(8,128)S(1)}, f32[176,512]{1,0:T(8,128)S(1)}, u32[]{:S(2)}, u32[]{:S(2)}) collective-permute-start(f32[176,512]{1,0:T(8,128)S(1)} %get-tuple-element.33), channel_id=1, source_target_pairs={{0,28},{4,8},{8,4},{12,16},{16,12},{20,24},{24,20},{28,0},{1,29},{... | collective-permute-start | bytes 1081352 | tf_op jit(solution)/shard_map/ppermute | solution.py:674
  9.8 11.8 %collective-permute-start.2 = (f32[32,128]{1,0:T(8,128)S(1)}, f32[32,128]{1,0:T(8,128)S(1)}, u32[]{:S(2)}, u32[]{:S(2)}) collective-permute-start(f32[32,128]{1,0:T(8,128)S(1)} %get-tuple-element.30.rest_0_), channel_id=1, source_target_pairs={{0,4},{4,0},{8,12},{12,8},{16,20},{20,16},{24,28},{28,24},{1,5},{5... | collective-permute-start | bytes 49160 | tf_op jit(solution)/shard_map/ppermute | solution.py:653
  21.6 7.1 %collective-permute-start.3 = (f32[64,128]{1,0:T(8,128)S(1)}, f32[64,128]{1,0:T(8,128)S(1)}, u32[]{:S(2)}, u32[]{:S(2)}) collective-permute-start(f32[64,128]{1,0:T(8,128)S(1)} %pad_maximum_fusion.1), channel_id=1, source_target_pairs={{0,16},{4,20},{8,24},{12,28},{16,0},{20,4},{24,8},{28,12},{1,17},{... | collective-permute-start | bytes 98312 | tf_op jit(solution)/shard_map/ppermute | solution.py:653
  23.9 9.6 %collective-permute-start.1 = (f32[224,128]{1,0:T(8,128)S(1)}, f32[224,128]{1,0:T(8,128)S(1)}, u32[]{:S(2)}, u32[]{:S(2)}) collective-permute-start(f32[224,128]{1,0:T(8,128)S(1)} %get-tuple-element.29), channel_id=1, source_target_pairs={{0,1},{1,0},{2,3},{3,2},{4,5},{5,4},{6,7},{7,6},{8,9},{9,8},{10,11... | collective-permute-start | bytes 344072 | tf_op jit(solution)/shard_map/ppermute | solution.py:675
  25.7 9.8 %collective-permute-start.6 = (f32[224,128]{1,0:T(8,128)S(1)}, f32[224,128]{1,0:T(8,128)S(1)}, u32[]{:S(2)}, u32[]{:S(2)}) collective-permute-start(f32[224,128]{1,0:T(8,128)S(1)} %get-tuple-element.34), channel_id=1, source_target_pairs={{1,2},{2,1},{5,6},{6,5},{9,10},{10,9},{13,14},{14,13},{17,18},{18,... | collective-permute-start | bytes 344072 | tf_op jit(solution)/shard_map/ppermute | solution.py:677
  28.7 6.0 %collective-permute-start.4 = (f32[128,128]{1,0:T(8,128)S(1)}, f32[128,128]{1,0:T(8,128)S(1)}, u32[]{:S(2)}, u32[]{:S(2)}) collective-permute-start(f32[128,128]{1,0:T(8,128)S(1)} %pad_maximum_fusion), channel_id=1, source_target_pairs={{0,8},{4,12},{8,0},{12,4},{16,24},{20,28},{24,16},{28,20},{1,9},{5... | collective-permute-start | bytes 196616 | tf_op jit(solution)/shard_map/ppermute | solution.py:653
